TPU v7x, 32 devices: a whole 2x2x4 slice. The times are simulated.
32 devices in a mesh: dp: 8 (over z, y), tp: 4 (over x, core).
Axes of the slice: x: 2, y: 2, z: 4, core: 2. Of those that a mesh axis runs over, the one named last changes fastest.
Arguments:
- hidden: bfloat16 [64, 256, 1024], P('dp')
- table: bfloat16 [50688, 1024], P('tp')
- labels: int32 [64, 256], P('dp')
- loss_mask: int32 [64, 256], P('dp')
- ln_gain: bfloat16 [1024], replicated
- ln_bias: bfloat16 [1024], replicated
Outputs:
- output 1: float32 [], replicated
- output 2: bfloat16 [64, 256, 1024], P('dp')
- output 3: float32 [50688, 1024], P('tp')
- output 4: float32 [1024], replicated
- output 5: float32 [1024], replicated
All inputs are finite; a program needn't handle non-finite values.
Results may differ from a plain program's by a relative error of at most 0.001.
Values sent between devices are 32-bit elements.
A program may use at most 1 GiB of HBM per device.

v0:
```python
import jax
import jax.numpy as jnp
from jax import lax
from jax.sharding import PartitionSpec as P

LN_EPS = 1e-5


def layer_norm(hidden, ln_gain, ln_bias):
    h32 = hidden.astype(jnp.float32)
    mean = jnp.mean(h32, axis=-1, keepdims=True)
    centred = h32 - mean
    variance = jnp.mean(centred * centred, axis=-1, keepdims=True)
    inv_std = lax.rsqrt(variance + LN_EPS)
    x_hat = centred * inv_std
    x_norm = (x_hat * ln_gain.astype(jnp.float32) + ln_bias.astype(jnp.float32)).astype(jnp.bfloat16)
    return x_norm, x_hat, inv_std


def norm_backward(grad_x, x_hat, inv_std, ln_gain):
    grad_hat = grad_x * ln_gain.astype(jnp.float32)
    mean_grad = jnp.mean(grad_hat, axis=-1, keepdims=True)
    mean_proj = jnp.mean(grad_hat * x_hat, axis=-1, keepdims=True)
    return (inv_std * (grad_hat - mean_grad - x_hat * mean_proj)).astype(jnp.bfloat16)


def solution(mesh):
    def device_step(hidden, table, labels, loss_mask, ln_gain, ln_bias):
        shard_rows = table.shape[0]
        first_row = lax.axis_index('tp') * shard_rows
        x_norm, x_hat, inv_std = layer_norm(hidden, ln_gain, ln_bias)
        logits = jnp.einsum('btd,vd->btv', x_norm, table, preferred_element_type=jnp.float32)
        live_rows = jnp.any(table != 0, axis=1)
        logits = jnp.where(live_rows, logits, -jnp.inf)
        top = lax.pmax(jnp.max(logits, axis=-1), 'tp')
        shifted = jnp.exp(logits - top[..., None])
        local_ids = labels - first_row
        one_hot = lax.broadcasted_iota(jnp.int32, (1, 1, shard_rows), 2) == local_ids[..., None]
        target_part = jnp.sum(jnp.where(one_hot, logits, 0.0), axis=-1)
        stats = lax.psum(jnp.stack([jnp.sum(shifted, axis=-1), target_part]), 'tp')
        exp_sum = stats[0]
        target = stats[1]
        weight = loss_mask.astype(jnp.float32)
        count = lax.psum(jnp.sum(weight), 'dp')
        log_norm = top + jnp.log(exp_sum)
        loss = lax.psum(jnp.sum(weight * (log_norm - target)), 'dp') / count
        prob_vals = shifted * (1.0 / exp_sum)[..., None]
        grad_logits = ((prob_vals - one_hot.astype(jnp.float32)) * (weight / count)[..., None]).astype(jnp.bfloat16)
        grad_x = lax.psum(jnp.einsum('btv,vd->btd', grad_logits, table, preferred_element_type=jnp.float32), 'tp')
        grad_table = lax.psum(jnp.einsum('btv,btd->vd', grad_logits, x_norm, preferred_element_type=jnp.float32), 'dp')
        grad_hidden = norm_backward(grad_x, x_hat, inv_std, ln_gain)
        grad_gain = lax.psum(jnp.sum(grad_x * x_hat, axis=(0, 1)), 'dp')
        grad_bias = lax.psum(jnp.sum(grad_x, axis=(0, 1)), 'dp')
        return loss, grad_hidden, grad_table, grad_gain, grad_bias

    specs_in = (P('dp', None, None), P('tp', None), P('dp', None), P('dp', None), P(None), P(None))
    specs_out = (P(), P('dp', None, None), P('tp', None), P(None), P(None))
    return jax.shard_map(device_step, mesh=mesh, in_specs=specs_in, out_specs=specs_out, check_vma=False)
```

profile of v0, /device:TPU:0, one launch (start us, length us, event | category | flops | bytes accessed | tf_op | source)
XLA Modules:
  0.0 1975.0 jit_solution(10665865320233122524)
XLA Ops:
  7.2 0.0 all-reduce.4.cloned.1.call-start
  7.2 0.0 copy-start.11
  7.2 0.0 copy-start.12
  7.2 0.0 copy-start
  7.2 11.4 compare_reduce_fusion
  18.6 0.0 copy-done.11
  18.7 0.0 copy-done.12
  18.7 0.0 copy-start.7
  18.7 0.0 copy-done
  18.7 0.0 copy-start.5
  18.7 0.6 convert_reduce_fusion
  19.3 0.0 copy-start.1
  19.3 1.4 fusion.18
  20.8 0.0 copy-done.5
  20.8 0.0 copy-done.1
  20.8 0.0 copy-start.3
  20.8 0.6 copy-done.3
  21.4 1.7 fusion.20.clone.4
  23.1 0.0 copy-start.10
  23.1 63.2 %select_reduce_fusion.1 = (f32[8,256]{1,0:T(8,128)S(1)}, f32[8,256,12672]{2,1,0:T(8,128)}) fusion(pred[12672]{0:T(1024)(128)(4,1)S(1)} %compare_reduce_fusion, bf16[12672,1024]{1,0:T(8,128)(2,1)} %param.7, bf16[8,256,1024]{2,1,0:T(8,128)(2,1)S(1)} %fusion.20.clone.4), kind=kOutput, calls=%fused_computation.5 | convolution fusion | flops 53202124800 | bytes 133976448 | tf_op jit(solution)/shard_map/btd,vd->btv/dot_general | solution.py:32
  86.3 0.0 copy-done.7
  86.4 8.5 pmax.7
  94.9 0.0 copy-done.10
  94.9 0.0 copy-start.9
  94.9 38.7 %fusion = (f32[8,256]{1,0:T(8,128)S(1)}, f32[8,256]{1,0:T(8,128)S(1)}) fusion(f32[8,256,12672]{2,1,0:T(8,128)} %get-tuple-element.17, f32[8,256]{1,0:T(8,128)S(1)} %pmax.7, pred[12672]{0:T(1024)(128)(4,1)S(1)} %compare_reduce_fusion, s32[8,256]{1,0:T(8,128)S(1)} %broadcast_subtract_fusion), kind=kLoop, calls=%fused_computation.4 | loop fusion | flops 155709440 | bytes 103854464 | tf_op jit(solution)/shard_map/reduce_sum | solution.py:40
  133.6 10.1 psum.49
  143.8 0.0 copy-done.9
  143.8 0.6 convert_reduce_fusion.1
  144.4 22.5 %psum.51 = f32[]{:T(128)} all-reduce(f32[]{:T(128)} %get-tuple-element.11), channel_id=1, replica_groups=mesh['dp'=8,'tp'=4] {'dp'}, use_global_device_ids=true, to_apply=%region_11.12 | all-reduce | flops 1 | bytes 8 | tf_op jit(solution)/shard_map/psum | solution.py:44
  166.9 0.6 convert_divide_fusion
  167.6 0.0 copy-start.2
  167.6 0.0 copy-start.4
  167.6 0.0 copy-start.6
  167.6 0.0 copy-start.8
  167.6 93.1 %fusion.1 = f32[8,256,1024]{2,1,0:T(8,128)} fusion(bf16[12672,1024]{1,0:T(8,128)(2,1)} %param.7, f32[8,256,12672]{2,1,0:T(8,128)} %get-tuple-element.17, f32[8,256]{1,0:T(8,128)S(1)} %convert_divide_fusion, f32[8,256]{1,0:T(8,128)S(1)} %divide_bitcast_fusion, s32[8,256]{1,0:T(8,128)S(1)} %broadcast_subtract_fusion, f32[8,256]{1,0:T(8,128)S(1)} %pmax.7, ...), kind=kOutput, calls=%fused_computation.8 | convolution fusion | flops 53357838336 | bytes 138195328 | tf_op jit(solution)/shard_map/btv,vd->btd/dot_general | solution.py:49
  260.7 0.0 all-reduce.4.cloned.1.call-update
  260.7 0.0 all-reduce.6.cloned.1.call-start
  260.7 0.0 copy-done.2
  260.8 0.0 copy-done.4
  260.8 0.0 copy-done.6
  260.8 0.0 copy-done.8
  260.8 5.0 fusion.29
  265.8 90.2 %convolution_bitcast_fusion = f32[12672,1024]{1,0:T(8,128)} fusion(f32[8,256,12672]{2,1,0:T(8,128)} %get-tuple-element.17, f32[8,256]{1,0:T(8,128)S(1)} %convert_divide_fusion, f32[8,256]{1,0:T(8,128)S(1)} %divide_bitcast_fusion, s32[8,256]{1,0:T(8,128)S(1)} %broadcast_subtract_fusion, f32[8,256]{1,0:T(8,128)S(1)} %pmax.7, ...), kind=kOutput, calls=%fused_computation.7 | convolution fusion | flops 53357838336 | bytes 159953280 | tf_op jit(solution)/shard_map/btv,btd->vd/dot_general | solution.py:50
  356.0 0.0 all-reduce.6.cloned.1.call-update
  356.0 53.9 %all-reduce.4.cloned.1.call-done = f32[8,256,1024]{2,1,0:T(8,128)} async-done(((f32[8,256,1024]{2,1,0:T(8,128)}), f32[8,256,1024]{2,1,0:T(8,128)}) %all-reduce.4.cloned.1.call-update) | async-done | bytes 8388624 | tf_op jit(solution)/shard_map/psum | solution.py:49
  409.9 6.8 fusion.17
  416.7 24.4 %all-reduce = (f32[]{:T(128)}, f32[1024]{0:T(1024)}, f32[1024]{0:T(1024)}) all-reduce(f32[]{:T(128)} %get-tuple-element.12, f32[1024]{0:T(1024)S(1)} %get-tuple-element.7, f32[1024]{0:T(1024)S(1)} %get-tuple-element.10), channel_id=1, replica_groups=mesh['dp'=8,'tp'=4] {'dp'}, use_global_device_ids=true, to_apply=%region_9.10 | all-reduce | flops 2049 | bytes 16392 | tf_op jit(solution)/shard_map/psum | solution.py:46
  442.5 7.3 fusion.16
  449.8 1482.2 %all-reduce.6.cloned.1.call-done = f32[12672,1024]{1,0:T(8,128)} async-done(((f32[12672,1024]{1,0:T(8,128)}), f32[12672,1024]{1,0:T(8,128)}) %all-reduce.6.cloned.1.call-update) | async-done | bytes 51904528 | tf_op jit(solution)/shard_map/psum | solution.py:50
  1932.0 35.1 %copy.15 = f32[12672,1024]{1,0:T(8,128)} copy(f32[12672,1024]{1,0:T(8,128)} %all-reduce.6.cloned.1.call-done) | data formatting | bytes 103809024
  (8 shorter events, 0.0 us)
Async XLA Ops:
  7.2 402.7 %all-reduce.4.cloned.1.call-start = ((), (), s32[]{:S(2)}) async-start(), calls=%async_computation | async-start | bytes 16777216 | tf_op jit(solution)/shard_map/psum | solution.py:49
  7.2 11.4 copy-start.11
  7.2 11.4 copy-start.12
  7.2 11.5 copy-start
  18.7 67.7 %copy-start.7 = (f32[1024]{0:T(1024)}, f32[1024]{0:T(1024)S(1)}, u32[]{:S(2)}) copy-start(f32[1024]{0:T(1024)S(1)} %convert_element_type.28) | copy-start | bytes 12292
  18.7 2.1 copy-start.5
  19.3 1.5 copy-start.1
  20.8 0.6 copy-start.3
  23.1 71.8 %copy-start.10 = (s32[8,256]{1,0:T(8,128)S(1)}, s32[8,256]{1,0:T(8,128)}, u32[]{:S(2)}) copy-start(s32[8,256]{1,0:T(8,128)} %param.8) | copy-start | bytes 24580
  94.9 48.9 %copy-start.9 = (s32[8,256]{1,0:T(8,128)S(1)}, s32[8,256]{1,0:T(8,128)}, u32[]{:S(2)}) copy-start(s32[8,256]{1,0:T(8,128)} %param.9) | copy-start | bytes 24580
  167.6 93.2 %copy-start.2 = (f32[8,256]{1,0:T(8,128)S(1)}, f32[8,256]{1,0:T(8,128)}, u32[]{:S(2)}) copy-start(f32[8,256]{1,0:T(8,128)} %copy-done.1) | copy-start | bytes 24580
  167.6 93.2 %copy-start.4 = (f32[8,256]{1,0:T(8,128)S(1)}, f32[8,256]{1,0:T(8,128)}, u32[]{:S(2)}) copy-start(f32[8,256]{1,0:T(8,128)} %copy-done.3) | copy-start | bytes 24580
  167.6 93.2 %copy-start.6 = (f32[1024]{0:T(1024)S(1)}, f32[1024]{0:T(1024)}, u32[]{:S(2)}) copy-start(f32[1024]{0:T(1024)} %copy-done.5) | copy-start | bytes 12292
  167.6 93.2 %copy-start.8 = (f32[1024]{0:T(1024)S(1)}, f32[1024]{0:T(1024)}, u32[]{:S(2)}) copy-start(f32[1024]{0:T(1024)} %copy-done.7) | copy-start | bytes 12292
  260.7 1671.3 %all-reduce.6.cloned.1.call-start = ((), (), s32[]{:S(2)}) async-start(), calls=%async_computation.1 | async-start | bytes 103809024 | tf_op jit(solution)/shard_map/psum | solution.py:50
Sparse Core Ops, SparseCore 0:
  260.8 149.0 all-reduce.3
  414.7 1517.2 all-reduce.5
where the time goes:
time: 1980 us
  waiting for transfers between devices  1540 us (78%)
  matrix products  246 us (12%)
  other arithmetic  74.2 us (4%)
  blocking collectives  65.6 us (3%)
  local copies, waits for them, and re-layouts  35.7 us (2%)
    psum x1, waiting for transfers between devices, device_step(): lax.psum(jnp.einsum('btv,btd->vd', grad_logits, x_norm, preferred_element...  1480 us
    dot_general x1, matrix products, device_step(): jnp.einsum('btv,vd->btd', grad_logits, table, preferred_element_type=jnp....  93.1 us
    dot_general x1, matrix products, device_step(): jnp.einsum('btv,btd->vd', grad_logits, x_norm, preferred_element_type=jnp...  90.2 us
    dot_general x1, matrix products, device_step(): jnp.einsum('btd,vd->btv', x_norm, table, preferred_element_type=jnp.float32)  63.2 us
    psum x1, waiting for transfers between devices, device_step(): lax.psum(jnp.einsum('btv,vd->btd', grad_logits, table, preferred_element_...  53.9 us
  transfers between devices with their start and end apart: 2, of which 2 were waited for; matrix products, arithmetic and copies ran while one was open for 6% of the time, Pallas kernels for 0%

commit v1 on v0

v1 whole, which is shorter than its diff:
```python
import functools

import jax
import jax.numpy as jnp
from jax import lax
from jax.experimental import pallas as pl
from jax.experimental.pallas import tpu as pltpu
from jax.sharding import PartitionSpec as P

LN_EPS = 1e-5
VOCAB = 50257
Z = 4
Y = 2
CHUNKS = 33
MESH = pl.DeviceIdType.MESH


def chain_kernel(chunks, part, out, red, loc, red_send, red_recv, bc_send, bc_recv, y_send, y_recv, loc_sem, own_sem):
    rows = red.shape[2]
    half = part.shape[0]
    dp = lax.axis_index('dp')
    y = dp % Y
    z = dp // Y
    mate = dp + 1 - 2 * y
    place = (Z - 1 - z, z)
    onward = (dp - Y, dp + Y)
    back = (dp + Y, dp - Y)

    barrier = pltpu.get_barrier_semaphore()
    pl.semaphore_signal(barrier, inc=1, device_id={'dp': mate}, device_id_type=MESH)

    @pl.when(z > 0)
    def _():
        pl.semaphore_signal(barrier, inc=1, device_id={'dp': dp - Y}, device_id_type=MESH)

    @pl.when(z < Z - 1)
    def _():
        pl.semaphore_signal(barrier, inc=1, device_id={'dp': dp + Y}, device_id_type=MESH)

    inner = jnp.where((z > 0) & (z < Z - 1), 1, 0)
    pl.semaphore_wait(barrier, 2 + inner)

    def part_rows(x, c):
        return part.at[pl.ds(x * (half // 2) + c * rows, rows)]

    def out_rows(side, x, c):
        return out.at[pl.ds(side * half + x * (half // 2) + c * rows, rows)]

    def fetch(x, c):
        return pltpu.make_async_copy(part_rows(x, c), loc.at[x, c], loc_sem.at[x, c])

    def reduce_copy(x, c, src):
        return pltpu.make_async_remote_copy(
            src_ref=src, dst_ref=red.at[x, c], send_sem=red_send.at[x, c], recv_sem=red_recv.at[x, c],
            device_id={'dp': onward[x]}, device_id_type=MESH)

    def spread_copy(x, c, src):
        return pltpu.make_async_remote_copy(
            src_ref=src, dst_ref=out_rows(y, x, c), send_sem=bc_send.at[x], recv_sem=bc_recv.at[x, c],
            device_id={'dp': back[x]}, device_id_type=MESH)

    def mate_copy(x, c, src):
        return pltpu.make_async_remote_copy(
            src_ref=src, dst_ref=out_rows(y, x, c), send_sem=y_send.at[x], recv_sem=y_recv.at[x],
            device_id={'dp': mate}, device_id_type=MESH)

    def own_copy(x, c):
        return pltpu.make_async_copy(red.at[x, c], out_rows(y, x, c), own_sem.at[x])

    def begin(c, carry):
        for x in range(2):
            @pl.when(place[x] > 0)
            def _():
                fetch(x, c).start()
        return carry

    lax.fori_loop(0, chunks, begin, 0)

    def add(x, c):
        reduce_copy(x, c, red.at[x, c]).wait_recv()
        fetch(x, c).wait()
        red[x, c] = red[x, c] + loc[x, c]

    def step(s, carry):
        for x in range(2):
            p = place[x]
            c = s - p
            here = (c >= 0) & (c < chunks)

            @pl.when(here & (p == 0))
            def _():
                reduce_copy(x, c, part_rows(x, c)).start()

            @pl.when(here & (p > 0) & (p < Z - 1))
            def _():
                add(x, c)
                reduce_copy(x, c, red.at[x, c]).start()

            @pl.when(here & (p < Z - 1) & (c >= 2))
            def _():
                reduce_copy(x, c - 2, red.at[x, c - 2]).wait_send()

            @pl.when(here & (p == Z - 1))
            def _():
                add(x, c)
                spread_copy(x, c, red.at[x, c]).start()
                mate_copy(x, c, red.at[x, c]).start()
                own_copy(x, c).start()

        for x in range(2):
            p = place[x]
            c = s - 2 * (Z - 1) + p

            @pl.when((c >= 0) & (c < chunks) & (p < Z - 1))
            def _():
                spread_copy(x, c, out_rows(y, x, c)).wait_recv()

                @pl.when(p > 0)
                def _():
                    spread_copy(x, c, out_rows(y, x, c)).start()

                mate_copy(x, c, out_rows(y, x, c)).start()
        return carry

    lax.fori_loop(0, chunks + 2 * (Z - 1), step, 0)

    for x in range(2):
        p = place[x]
        mine = out.at[pl.ds(y * half + x * (half // 2), half // 2)]
        theirs = out.at[pl.ds((1 - y) * half + x * (half // 2), half // 2)]

        @pl.when(p < Z - 1)
        def _():
            reduce_copy(x, chunks - 2, red.at[x, chunks - 2]).wait_send()
            reduce_copy(x, chunks - 1, red.at[x, chunks - 1]).wait_send()

        @pl.when(p > 0)
        def _():
            pltpu.make_async_copy(mine, mine, bc_send.at[x]).wait()

        @pl.when(p == Z - 1)
        def _():
            pltpu.make_async_copy(mine, mine, own_sem.at[x]).wait()

        pltpu.make_async_copy(mine, mine, y_send.at[x]).wait()
        pltpu.make_async_copy(theirs, theirs, y_recv.at[x]).wait()


def chain_all_reduce(part, chunks=CHUNKS):
    half, width = part.shape
    rows = half // (2 * chunks)
    assert rows * 2 * chunks == half and rows % 8 == 0
    dma = pltpu.SemaphoreType.DMA
    return pl.pallas_call(
        functools.partial(chain_kernel, chunks),
        out_shape=jax.ShapeDtypeStruct((Y * half, width), jnp.float32),
        in_specs=[pl.BlockSpec(memory_space=pl.ANY)],
        out_specs=pl.BlockSpec(memory_space=pl.ANY),
        scratch_shapes=[
            pltpu.VMEM((2, chunks, rows, width), jnp.float32),
            pltpu.VMEM((2, chunks, rows, width), jnp.float32),
            dma((2, chunks)), dma((2, chunks)),
            dma((2,)), dma((2, chunks)),
            dma((2,)), dma((2,)),
            dma((2, chunks)), dma((2,)),
        ],
        compiler_params=pltpu.CompilerParams(
            collective_id=0, has_side_effects=True, vmem_limit_bytes=60 * 1024 * 1024),
        cost_estimate=pl.CostEstimate(flops=4 * half * width, bytes_accessed=12 * half * width, transcendentals=0),
    )(part)


def norm_stats(hidden):
    h32 = hidden.astype(jnp.float32)
    mean = jnp.mean(h32, axis=-1, keepdims=True)
    centred = h32 - mean
    variance = jnp.mean(centred * centred, axis=-1, keepdims=True)
    inv_std = lax.rsqrt(variance + LN_EPS)
    return centred * inv_std, inv_std


def norm_backward(grad_x, x_hat, inv_std, ln_gain):
    grad_hat = grad_x * ln_gain.astype(jnp.float32)
    mean_grad = jnp.mean(grad_hat, axis=-1, keepdims=True)
    mean_proj = jnp.mean(grad_hat * x_hat, axis=-1, keepdims=True)
    return (inv_std * (grad_hat - mean_grad - x_hat * mean_proj)).astype(jnp.bfloat16)


def solution(mesh):
    n_dp = mesh.shape['dp']
    n_tp = mesh.shape['tp']
    to_mate = [(i, i ^ 1) for i in range(n_dp)]
    to_core = [(i, i ^ 1) for i in range(n_tp)]

    def device_step(hidden, table, labels, loss_mask, ln_gain, ln_bias):
        batch, seq, width = hidden.shape
        tokens = batch * seq
        shard = table.shape[0]
        half = shard // Y
        dp = lax.axis_index('dp')
        tp = lax.axis_index('tp')
        y = dp % Y
        core = tp % 2
        gain = ln_gain.astype(jnp.float32)
        bias = ln_bias.astype(jnp.float32)

        x_hat, inv_std = norm_stats(hidden.reshape(tokens, width))
        ids = jnp.stack([labels.reshape(tokens), loss_mask.reshape(tokens)])
        ids_mate = lax.ppermute(ids, 'dp', to_mate)

        piece = lax.dynamic_slice(x_hat, (core * (tokens // 2), 0), (tokens // 2, width))
        got = lax.ppermute(piece, 'dp', to_mate)
        got2 = lax.ppermute(got, 'tp', to_core)
        first = jnp.where(core == 0, got, got2)
        second = jnp.where(core == 0, got2, got)
        hat_mate = jnp.concatenate([first, second])

        def pair(own, mate):
            return jnp.where(y == 0, jnp.stack([own, mate]), jnp.stack([mate, own]))

        hat_all = pair(x_hat, hat_mate).reshape(Y * tokens, width)
        x_all = (hat_all * gain + bias).astype(jnp.bfloat16)
        ids_all = pair(ids, ids_mate)
        labels_all = ids_all[:, 0].reshape(Y * tokens)
        mask_all = ids_all[:, 1].reshape(Y * tokens)

        rows = lax.dynamic_slice(table, (y * half, 0), (half, width))
        first_row = tp * shard + y * half
        logits = lax.dot_general(x_all, rows, (((1,), (1,)), ((), ())), preferred_element_type=jnp.float32)
        row_ids = first_row + lax.broadcasted_iota(jnp.int32, (1, half), 1)
        logits = jnp.where(row_ids < VOCAB, logits, -jnp.inf)
        one_hot = row_ids == labels_all[:, None]
        top = jnp.maximum(jnp.max(logits, axis=-1), jnp.finfo(jnp.float32).min)
        exp_sum = jnp.sum(jnp.exp(logits - top[:, None]), axis=-1)
        target = jnp.sum(jnp.where(one_hot, logits, 0.0), axis=-1)

        def merge(stats):
            best = jnp.max(stats[:, 0], axis=0)
            total = jnp.sum(stats[:, 1] * jnp.exp(stats[:, 0] - best), axis=0)
            return jnp.stack([best, total, jnp.sum(stats[:, 2], axis=0)])

        stats = merge(lax.all_gather(jnp.stack([top, exp_sum, target]), 'tp'))
        stats = merge(jnp.stack([stats, lax.ppermute(stats, 'dp', to_mate)]))
        log_norm = stats[0] + jnp.log(stats[1])

        weight = mask_all.astype(jnp.float32)
        own_weight = loss_mask.reshape(tokens).astype(jnp.float32)
        count = lax.psum(jnp.sum(own_weight), 'dp')
        scale = weight / count
        grad_logits = ((jnp.exp(logits - log_norm[:, None]) - one_hot.astype(jnp.float32)) * scale[:, None]).astype(jnp.bfloat16)
        part_table = lax.dot_general(grad_logits, x_all, (((0,), (0,)), ((), ())), preferred_element_type=jnp.float32)
        part_x = lax.dot_general(grad_logits, rows, (((1,), (0,)), ((), ())), preferred_element_type=jnp.float32)

        quarter = tokens // n_tp
        part_x = part_x.reshape(Y, n_tp, quarter, width)
        mixed = lax.psum_scatter(part_x, 'tp', scatter_dimension=1, tiled=False)
        mine = lax.dynamic_index_in_dim(mixed, y, 0, keepdims=False)
        other = lax.dynamic_index_in_dim(mixed, 1 - y, 0, keepdims=False)
        grad_quarter = mine + lax.ppermute(other, 'dp', to_mate)
        grad_x = lax.all_gather(grad_quarter, 'tp', tiled=True)

        grad_table = chain_all_reduce(part_table)

        grad_hidden = norm_backward(grad_x, x_hat, inv_std, ln_gain).reshape(batch, seq, width)
        own_norm = lax.dynamic_slice(log_norm - stats[2], (y * tokens,), (tokens,))
        sums = jnp.stack([jnp.sum(grad_x * x_hat, axis=0), jnp.sum(grad_x, axis=0)])
        lost = jnp.sum(own_weight * own_norm)
        sums, lost = lax.psum((sums, lost), 'dp')
        return lost / count, grad_hidden, grad_table, sums[0], sums[1]

    specs_in = (P('dp', None, None), P('tp', None), P('dp', None), P('dp', None), P(None), P(None))
    specs_out = (P(), P('dp', None, None), P('tp', None), P(None), P(None))
    return jax.shard_map(device_step, mesh=mesh, in_specs=specs_in, out_specs=specs_out, check_vma=False)
```

time: 1980 us -> 1500 us (0.76)
  waiting for transfers between devices: 1540 us -> 424 us
  Pallas kernels: 0 us -> 599 us
  other arithmetic: 74.2 us -> 163 us
  matrix products: 246 us -> 190 us
    psum x2 -> x0, waiting for transfers between devices: 1540 us -> none  [the longest x1 1480 us: device_step(): lax.psum(jnp.einsum('btv,btd->vd', grad_logits, x_norm, preferred_element...]
    pallas_call x0 -> x1, Pallas kernels: none -> 599 us  [chain_all_reduce(): pl.pallas_call(functools.partial(chain_kernel, chunks), out_shape=jax.Sha...]
    unnamed x2 -> x3, waiting for transfers between devices: 0.03 us -> 284 us
    ppermute x0 -> x5, waiting for transfers between devices: none -> 140 us  [the longest x1 90.7 us: device_step(): got = lax.ppermute(piece, 'dp', to_mate)]
    convert_element_type x2 -> x5, other arithmetic: 0.01 us -> 61.8 us  [the longest x1 50.7 us: device_step(): ((jnp.exp(logits - log_norm[:, None]) - one_hot.astype(jnp.float32)) * sc...]
    dot_general x3, matrix products: 246 us -> 190 us  [the longest x1 63.5 us: device_step(): lax.dot_general(x_all, rows, (((1,), (1,)), ((), ())), preferred_element_...]
    psum x3 -> x2, blocking collectives: 57.1 us -> 50.5 us  [the longest x1 29 us: device_step(): sums, lost = lax.psum((sums, lost), 'dp')]
    reduce_sum x5 -> x8, other arithmetic: 48.1 us -> 53.6 us  [the longest x1 40 us: device_step(): exp_sum = jnp.sum(jnp.exp(logits - top[:, None]), axis=-1)]
  transfers between devices with their start and end apart: 2 -> 7, of which waited for: 2 -> 4; matrix products, arithmetic and copies ran while one was open for 6% -> 5% of each run, Pallas kernels for 0% -> 40%
where the time goes in v1:
time: 1500 us
  Pallas kernels  599 us (40%)
  waiting for transfers between devices  424 us (28%)
  matrix products  190 us (13%)
  other arithmetic  163 us (11%)
  blocking collectives  56.5 us (4%)
  local copies, waits for them, and re-layouts  41.6 us (3%)
  between operations  17.6 us (1%)
    pallas_call x1, Pallas kernels, chain_all_reduce(): pl.pallas_call(functools.partial(chain_kernel, chunks), out_shape=jax.Sha...  599 us
    unnamed x3, waiting for transfers between devices  284 us
    ppermute x1, waiting for transfers between devices, device_step(): got = lax.ppermute(piece, 'dp', to_mate)  90.7 us
    dot_general x1, matrix products, device_step(): lax.dot_general(x_all, rows, (((1,), (1,)), ((), ())), preferred_element_...  63.5 us
    dot_general x1, matrix products, device_step(): lax.dot_general(grad_logits, rows, (((1,), (0,)), ((), ())), preferred_el...  63.4 us
    dot_general x1, matrix products, device_step(): lax.dot_general(grad_logits, x_all, (((0,), (0,)), ((), ())), preferred_e...  62.8 us
    convert_element_type x1, other arithmetic, device_step(): ((jnp.exp(logits - log_norm[:, None]) - one_hot.astype(jnp.float32)) * sc...  50.7 us
    ppermute x1, waiting for transfers between devices, device_step(): grad_quarter = mine + lax.ppermute(other, 'dp', to_mate)  45.8 us
  transfers between devices with their start and end apart: 7, of which 4 were waited for; matrix products, arithmetic and copies ran while one was open for 5% of the time, Pallas kernels for 40%

profile of v1, /device:TPU:0, one launch (start us, length us, event | category | flops | bytes accessed | tf_op | source)
XLA Modules:
  0.0 1498.6 jit_solution(1137902155823813725)
XLA Ops:
  7.2 0.0 all-reduce.4.cloned.1.call-start
  7.2 2.8 convert_reduce_fusion
  10.0 3.0 multiply_reduce_fusion.2
  13.1 0.0 copy-start.4
  13.1 0.0 copy-start.11
  13.1 0.0 copy-start.16
  13.2 5.5 fusion.10
  18.6 2.5 constant_dynamic-slice_fusion
  21.1 3.1 collective-permute-start
  24.2 90.7 %collective-permute-done = f32[1024,1024]{1,0:T(8,128)} collective-permute-done((f32[1024,1024]{1,0:T(8,128)S(1)}, f32[1024,1024]{1,0:T(8,128)}, u32[]{:S(2)}, u32[]{:S(2)}) %collective-permute-start) | collective-permute-done | bytes 4194336 | tf_op jit(solution)/shard_map/ppermute | solution.py:212
  114.9 0.0 collective-permute-start.1
  114.9 1.8 collective-permute-start.2
  116.8 6.6 convert_element_type.70
  123.4 0.6 convert_reduce_fusion.1
  124.0 0.6 iota_add_fusion
  124.6 0.0 copy-done.2
  124.6 5.9 fusion.11
  130.5 21.5 %psum.22 = f32[]{:T(128)} all-reduce(f32[]{:T(128)} %convert_reduce_fusion.1), channel_id=1, replica_groups=mesh['dp'=8,'tp'=4] {'dp'}, use_global_device_ids=true, to_apply=%region_14.15 | all-reduce | flops 1 | bytes 8 | tf_op jit(solution)/shard_map/psum | solution.py:248
  152.0 0.0 copy-start.13
  152.0 0.0 collective-permute-done.2
  152.1 0.0 copy-start.7
  152.1 0.6 slice.42
  152.7 0.0 collective-permute-done.1
  152.7 7.1 broadcast_select_fusion.1
  159.8 7.1 maximum_bitcast_fusion
  166.9 8.8 maximum_select_fusion
  175.7 4.5 fusion.5
  180.2 63.5 %select_reduce_fusion = (f32[4096]{0:T(1024)S(1)}, f32[4096,6336]{0,1:T(8,128)}) fusion(pred[6336]{0:T(1024)(128)(4,1)S(1)} %broadcast_compare_fusion, bf16[4096,1024]{1,0:T(8,128)(2,1)S(1)} %fusion.5, bf16[12672,1024]{1,0:T(8,128)(2,1)} %param.7, s32[]{:T(128)S(6)} %select_n.76), kind=kOutput, calls=%fused_computation.7 | convolution fusion | flops 53202120704 | bytes 125196480 | tf_op jit(solution)/shard_map/dot_general | solution.py:229
  243.7 0.0 copy-done.1
  243.7 0.0 copy-done.6
  243.7 0.0 copy-start.8
  243.7 40.0 %exponential_reduce_fusion = (f32[4096]{0:T(1024)S(1)}, f32[4096]{0:T(1024)S(1)}) fusion(f32[4096,6336]{0,1:T(8,128)} %get-tuple-element.33, f32[4096]{0:T(1024)S(1)} %broadcast_maximum_fusion, pred[6336]{0:T(1024)(128)(4,1)S(1)} %broadcast_compare_fusion, s32[4096]{0:T(1024)S(1)} %bitcast.113, s32[6336]{0:T(1024)S(1)} %copy-done.1), kind=kLoop, calls=%fused_computation.6 | loop fusion | flops 155705344 | bytes 103906240 | tf_op jit(solution)/shard_map/reduce_sum | solution.py:234
  283.7 6.0 all-gather.1
  289.7 0.2 fusion.33
  290.0 0.1 fusion.16
  290.1 0.1 fusion.30
  290.1 0.1 collective-permute-start.3
  290.2 0.7 fusion.23
  290.9 0.1 copy.16
  291.0 3.6 collective-permute-done.3
  294.6 0.7 fusion.31
  295.3 0.1 fusion.22
  295.4 50.7 %fusion.3 = bf16[4096,6336]{0,1:T(8,128)(2,1)} fusion(f32[4096,6336]{0,1:T(8,128)} %get-tuple-element.33, f32[4096]{0:T(1024)S(1)} %bitcast.120, f32[4096]{0:T(1024)S(1)} %log_add_fusion, s32[4096]{0:T(1024)S(1)} %bitcast.114, s32[6336]{0:T(1024)S(1)} %copy-done.1, pred[6336]{0:T(1024)(128)(4,1)S(1)} %broadcast_compare_fusion), kind=kLoop, calls=%fused_computation.5 | loop fusion | flops 181665792 | bytes 155794368 | tf_op jit(solution)/shard_map/convert_element_type | solution.py:250
  346.1 63.4 %fusion.6 = f32[4096,1024]{1,0:T(8,128)} fusion(bf16[4096,6336]{0,1:T(8,128)(2,1)} %fusion.3, bf16[12672,1024]{1,0:T(8,128)(2,1)} %param.7, s32[]{:T(128)S(6)} %select_n.76), kind=kOutput, calls=%fused_computation.12 | convolution fusion | flops 53150220288 | bytes 81657856 | tf_op jit(solution)/shard_map/dot_general | solution.py:252
  409.5 0.0 all-reduce.4.cloned.1.call-update
  409.6 0.0 copy-start.12
  409.6 0.3 all-gather.4.cloned.1.call-start
  409.9 0.3 copy-done.19
  410.2 0.6 dynamic-slice.2
  411.4 283.9 %all-reduce.4.cloned.1.call-done = f32[2,4,512,1024]{3,2,1,0:T(8,128)} async-done(((f32[2,4,512,1024]{3,2,1,0:T(8,128)}), f32[2,4,512,1024]{3,2,1,0:T(8,128)}) %all-reduce.4.cloned.1.call-update) | async-done | bytes 16777232
  695.3 1.7 dynamic-slice_bitcast_fusion
  697.0 1.5 collective-permute-start.4
  698.5 45.8 %collective-permute-done.4 = f32[512,1024]{1,0:T(8,128)} collective-permute-done((f32[512,1024]{1,0:T(8,128)S(1)}, f32[512,1024]{1,0:T(8,128)}, u32[]{:S(2)}, u32[]{:S(2)}) %collective-permute-start.4) | collective-permute-done | bytes 2097184 | tf_op jit(solution)/shard_map/ppermute | solution.py:259
  744.4 4.1 fusion.12
  748.5 0.0 all-gather.4.cloned.1.call-update
  748.5 62.8 %fusion.35.part = f32[6336,1024]{1,0:T(8,128)} fusion(bf16[4096,6336]{0,1:T(8,128)(2,1)} %fusion.3, bf16[4096,1024]{1,0:T(8,128)(2,1)} %copy-done), kind=kOutput, calls=%fused_computation.80 | convolution fusion | flops 53150220288 | bytes 86245376 | tf_op jit(solution)/shard_map/dot_general | solution.py:251
  811.4 0.0 copy-start.14
  811.4 598.9 %shard_map.101 = f32[12672,1024]{1,0:T(8,128)} custom-call(f32[6336,1024]{1,0:T(8,128)} %fusion.35.part), custom_call_target="tpu_custom_call" | custom-call | flops 25952256 | bytes 77856768 | tf_op jit(solution)/shard_map/pallas_call | solution.py:154
  1410.3 0.6 fusion.25
  1410.9 6.4 multiply_reduce_fusion
  1417.4 29.0 %all-reduce.1 = (f32[]{:T(128)}, f32[2,1024]{1,0:T(2,128)S(1)}) all-reduce(f32[]{:T(128)} %fusion.25, f32[2,1024]{1,0:T(2,128)S(1)} %pad_maximum_fusion.2), channel_id=1, replica_groups=mesh['dp'=8,'tp'=4] {'dp'}, use_global_device_ids=true, to_apply=%region_12.13 | all-reduce | flops 2049 | bytes 16392 | tf_op jit(solution)/shard_map/psum | solution.py:268
  1447.7 0.6 fusion.34
  1448.3 7.3 multiply_convert_fusion
  1455.5 35.1 %copy.39 = f32[12672,1024]{1,0:T(8,128)} copy(f32[12672,1024]{1,0:T(8,128)} %shard_map.101) | data formatting | bytes 103809024
  (53 shorter events, 0.3 us)
Async XLA Ops:
  7.2 688.1 %all-reduce.4.cloned.1.call-start = ((), (), s32[]{:S(2)}) async-start(), calls=%async_computation.1 | async-start | bytes 33554432
  13.1 111.5 %copy-start.2 = (f32[1,2,8,128]{3,1,2,0:T(2,128)}, f32[1,2,8,128]{3,1,2,0:T(2,128)S(1)}, u32[]{:S(2)}) copy-start(f32[1,2,8,128]{3,1,2,0:T(2,128)S(1)} %copy.24) | copy-start | bytes 24580
  13.1 111.5 %copy-start.4 = (f32[1,2,8,128]{3,1,2,0:T(2,128)}, f32[1,2,8,128]{3,1,2,0:T(2,128)S(1)}, u32[]{:S(2)}) copy-start(f32[1,2,8,128]{3,1,2,0:T(2,128)S(1)} %copy.23) | copy-start | bytes 24580
  13.1 101.8 %copy-start.11 = (s32[8,256]{1,0:T(8,128)S(1)}, s32[8,256]{1,0:T(8,128)}, u32[]{:S(2)}) copy-start(s32[8,256]{1,0:T(8,128)} %param.9) | copy-start | bytes 24580
  13.1 101.8 %copy-start.16 = (s32[8,256]{1,0:T(8,128)S(1)}, s32[8,256]{1,0:T(8,128)}, u32[]{:S(2)}) copy-start(s32[8,256]{1,0:T(8,128)} %param.8) | copy-start | bytes 24580
  21.1 93.7 %collective-permute-start = (f32[1024,1024]{1,0:T(8,128)S(1)}, f32[1024,1024]{1,0:T(8,128)}, u32[]{:S(2)}, u32[]{:S(2)}) collective-permute-start(f32[1024,1024]{1,0:T(8,128)S(1)} %constant_dynamic-slice_fusion), channel_id=1, source_target_pairs={{0,4},{4,0},{8,12},{12,8},{16,20},{20,16},{24,28},{28,24},{1,5},{5... | collective-permute-start | bytes 12582920 | tf_op jit(solution)/shard_map/ppermute | solution.py:212
  114.9 37.8 %collective-permute-start.1 = (f32[1024,1024]{1,0:T(8,128)}, f32[1024,1024]{1,0:T(8,128)}, u32[]{:S(2)}, u32[]{:S(2)}) collective-permute-start(f32[1024,1024]{1,0:T(8,128)} %collective-permute-done), channel_id=1, source_target_pairs={{0,1},{1,0},{2,3},{3,2},{4,5},{5,4},{6,7},{7,6},{8,9},{9,8},{10,11... | collective-permute-start | bytes 12582920 | tf_op jit(solution)/shard_map/ppermute | solution.py:213
  114.9 37.1 %collective-permute-start.2 = (s32[2,2048]{1,0:T(2,128)S(1)}, s32[2,2048]{1,0:T(2,128)S(1)}, u32[]{:S(2)}, u32[]{:S(2)}) collective-permute-start(s32[2,2048]{1,0:T(2,128)S(1)} %get-tuple-element.27), channel_id=1, source_target_pairs={{0,4},{4,0},{8,12},{12,8},{16,20},{20,16},{24,28},{28,24},{1,5},{5... | collective-permute-start | bytes 49160 | tf_op jit(solution)/shard_map/ppermute | solution.py:209
  124.6 27.4 %copy-start.17 = (bf16[1024]{0:T(1024)(128)(2,1)S(1)}, bf16[1024]{0:T(1024)(128)(2,1)}, u32[]{:S(2)}) copy-start(bf16[1024]{0:T(1024)(128)(2,1)} %param.11) | copy-start | bytes 6148
  124.6 27.4 %copy-start.18 = (bf16[1024]{0:T(1024)(128)(2,1)S(1)}, bf16[1024]{0:T(1024)(128)(2,1)}, u32[]{:S(2)}) copy-start(bf16[1024]{0:T(1024)(128)(2,1)} %param.10) | copy-start | bytes 6148
  152.0 23.6 %copy-start.13 = (f32[1024]{0:T(1024)}, f32[1024]{0:T(1024)S(1)}, u32[]{:S(2)}) copy-start(f32[1024]{0:T(1024)S(1)} %convert_element_type.63) | copy-start | bytes 12292
  152.1 0.6 copy-start.7
  152.7 14.2 slice-start
  159.8 7.1 slice-start.1
  180.1 63.5 %copy-start = (bf16[4096,1024]{1,0:T(8,128)(2,1)}, bf16[4096,1024]{1,0:T(8,128)(2,1)S(1)}, u32[]{:S(2)}) copy-start(bf16[4096,1024]{1,0:T(8,128)(2,1)S(1)} %fusion.5) | copy-start | bytes 25165828
  180.1 63.5 %copy-start.1 = (s32[6336]{0:T(1024)S(1)}, s32[6336]{0:T(1024)}, u32[]{:S(2)}) copy-start(s32[6336]{0:T(1024)} %iota_add_fusion) | copy-start | bytes 76036
  180.2 63.5 %copy-start.6 = (s32[2,1,2048]{2,1,0:T(1,128)S(1)}, s32[2,1,2048]{2,1,0:T(1,128)}, u32[]{:S(2)}) copy-start(s32[2,1,2048]{2,1,0:T(1,128)} %slice.42) | copy-start | bytes 49156
  243.7 46.5 %copy-start.8 = (s32[2,2,2048]{2,1,0:T(2,128)S(1)}, s32[2,2,2048]{2,1,0:T(2,128)}, u32[]{:S(2)}) copy-start(s32[2,2,2048]{2,1,0:T(2,128)} %copy-done.7) | copy-start | bytes 98308
  290.1 4.4 collective-permute-start.3
  295.4 50.7 %copy-start.9 = (f32[4096]{0:T(1024)}, f32[4096]{0:T(1024)S(1)}, u32[]{:S(2)}) copy-start(f32[4096]{0:T(1024)S(1)} %log_add_fusion) | copy-start | bytes 49156
  409.5 0.7 copy-start.19
  409.6 338.9 %copy-start.12 = (s32[8,256]{1,0:T(8,128)S(1)}, s32[8,256]{1,0:T(8,128)}, u32[]{:S(2)}) copy-start(s32[8,256]{1,0:T(8,128)} %param.9) | copy-start | bytes 24580
  409.6 1001.3 %all-gather.4.cloned.1.call-start = ((), (), s32[]{:S(2)}) async-start(), calls=%async_computation | async-start | bytes 10485760 | tf_op jit(solution)/shard_map/all_gather | solution.py:260
  697.0 47.4 %collective-permute-start.4 = (f32[512,1024]{1,0:T(8,128)S(1)}, f32[512,1024]{1,0:T(8,128)}, u32[]{:S(2)}, u32[]{:S(2)}) collective-permute-start(f32[512,1024]{1,0:T(8,128)S(1)} %dynamic-slice_bitcast_fusion), channel_id=1, source_target_pairs={{0,4},{4,0},{8,12},{12,8},{16,20},{20,16},{24,28},{28,24},{1,5},{5... | collective-permute-start | bytes 6291464 | tf_op jit(solution)/shard_map/ppermute | solution.py:259
  811.4 598.9 %copy-start.10 = (f32[4096]{0:T(1024)S(1)}, f32[4096]{0:T(1024)}, u32[]{:S(2)}) copy-start(f32[4096]{0:T(1024)} %copy-done.9) | copy-start | bytes 49156
  811.4 598.9 %copy-start.15 = (f32[4096]{0:T(1024)S(1)}, f32[4096]{0:T(1024)}, u32[]{:S(2)}) copy-start(f32[4096]{0:T(1024)} %get-tuple-element.23) | copy-start | bytes 49156
  811.4 599.6 %copy-start.3 = (f32[1,2,8,128]{3,1,2,0:T(2,128)S(1)}, f32[1,2,8,128]{3,1,2,0:T(2,128)}, u32[]{:S(2)}) copy-start(f32[1,2,8,128]{3,1,2,0:T(2,128)} %copy-done.2) | copy-start | bytes 24580
  811.4 599.6 %copy-start.5 = (f32[1,2,8,128]{3,1,2,0:T(2,128)S(1)}, f32[1,2,8,128]{3,1,2,0:T(2,128)}, u32[]{:S(2)}) copy-start(f32[1,2,8,128]{3,1,2,0:T(2,128)} %copy-done.4) | copy-start | bytes 24580
  811.4 599.5 %copy-start.14 = (f32[1024]{0:T(1024)S(1)}, f32[1024]{0:T(1024)}, u32[]{:S(2)}) copy-start(f32[1024]{0:T(1024)} %copy-done.13) | copy-start | bytes 12292
Sparse Core Ops, SparseCore 0:
  409.7 285.5 all-reduce.3
  748.6 58.4 all-gather.3

commit v2 on v0

v2 whole, which is shorter than its diff:
```python
import functools

import jax
import jax.numpy as jnp
from jax import lax
from jax.experimental import pallas as pl
from jax.experimental.pallas import tpu as pltpu
from jax.sharding import PartitionSpec as P

LN_EPS = 1e-5
VOCAB = 50257
Z = 4
Y = 2
CHUNKS = 33
SLOTS = 8
TILE = 512
MESH = pl.DeviceIdType.MESH


def unit_at(i):
    return 1 + i // 2 + (i // 2 + i % 2) // 2


def has_unit(i, units):
    return ((i % 2 == 1) | (i // 2 % 2 == 1)) & (unit_at(i) < units)


def last_tick(units):
    return max(i for i in range(1, 4 * units) if has_unit(i, units))


def backward_kernel(
        chunks, table, x, x_t, lse, scale, label,
        out, part, dx, target,
        red, loc, q_t, rows_buf, more_buf, stage, dx_t, from_core, from_x, dx_q,
        red_send, red_recv, credit, bc_send, bc_recv, y_send, y_recv, loc_sem, own_sem, part_sem, rows_sem, more_sem,
        core_sem, x_sem, share_send, share_recv):
    size = red.shape[2]
    half = part.shape[0]
    unit = 2 * size
    tokens = x.shape[0]
    own = tokens // Y
    width = x.shape[1]
    quarter = dx.shape[1]
    dp = lax.axis_index('dp')
    tp = lax.axis_index('tp')
    y = dp % Y
    z = dp // Y
    core = tp % 2
    mate = dp + 1 - 2 * y
    partner = tp + 1 - 2 * core
    beside = tp + 2 - 4 * (tp // 2)
    across = beside + 1 - 2 * core
    place = (Z - 1 - z, z)
    onward = (dp - Y, dp + Y)
    back = (dp + Y, dp - Y)

    barrier = pltpu.get_barrier_semaphore()
    pl.semaphore_signal(barrier, inc=1, device_id={'dp': mate}, device_id_type=MESH)
    for other in (partner, beside, across):
        pl.semaphore_signal(barrier, inc=1, device_id={'tp': other}, device_id_type=MESH)

    @pl.when(z > 0)
    def _():
        pl.semaphore_signal(barrier, inc=1, device_id={'dp': dp - Y}, device_id_type=MESH)

    @pl.when(z < Z - 1)
    def _():
        pl.semaphore_signal(barrier, inc=1, device_id={'dp': dp + Y}, device_id_type=MESH)

    inner = jnp.where((z > 0) & (z < Z - 1), 1, 0)

    def part_rows(h, c):
        return part.at[pl.ds(h * (half // 2) + c * size, size)]

    def out_rows(side, h, c):
        return out.at[pl.ds(side * half + h * (half // 2) + c * size, size)]

    def fetch(h, c):
        return pltpu.make_async_copy(part_rows(h, c), loc.at[h, c % 2], loc_sem.at[h, c % 2])

    def reduce_copy(h, c, src):
        slot = c % SLOTS
        return pltpu.make_async_remote_copy(
            src_ref=src, dst_ref=red.at[h, slot], send_sem=red_send.at[h, slot], recv_sem=red_recv.at[h, slot],
            device_id={'dp': onward[h]}, device_id_type=MESH)

    def spread_copy(h, c):
        return pltpu.make_async_remote_copy(
            src_ref=out_rows(y, h, c), dst_ref=out_rows(y, h, c), send_sem=bc_send.at[h], recv_sem=bc_recv.at[h, c],
            device_id={'dp': back[h]}, device_id_type=MESH)

    def mate_copy(h, c):
        return pltpu.make_async_remote_copy(
            src_ref=out_rows(y, h, c), dst_ref=out_rows(y, h, c), send_sem=y_send.at[h], recv_sem=y_recv.at[h],
            device_id={'dp': mate}, device_id_type=MESH)

    def own_copy(h, c):
        return pltpu.make_async_copy(red.at[h, c % SLOTS], out_rows(y, h, c), own_sem.at[h])

    def rows_copy(h, u):
        return pltpu.make_async_copy(
            table.at[pl.ds(y * half + h * (half // 2) + u * size, size)],
            rows_buf.at[u % 2, pl.ds(h * size, size)], rows_sem.at[u % 2, h])

    def more_copy(u):
        return pltpu.make_async_copy(
            table.at[pl.ds((1 - y) * half + u * unit, unit)], more_buf.at[u % 2], more_sem.at[u % 2])

    def part_copy(h, u):
        return pltpu.make_async_copy(stage.at[pl.ds(h * size, size)], part_rows(h, u), part_sem.at[h])

    shard_first = tp * Y * half
    steps_in_unit = lax.broadcasted_iota(jnp.int32, (unit, 1), 0)

    def grads(table_rows, row_ids, t):
        at = pl.ds(pl.multiple_of(t * TILE, TILE), TILE)
        logits = jnp.dot(table_rows, x_t[:, at], preferred_element_type=jnp.float32)
        hit = row_ids == label[:, at]
        probs = jnp.where(row_ids + shard_first < VOCAB, jnp.exp(logits - lse[:, at]), 0.0)
        q = ((probs - jnp.where(hit, 1.0, 0.0)) * scale[:, at]).astype(jnp.bfloat16)
        return q, jnp.where(hit, logits, 0.0)

    def add_dx(table_rows, q, t):
        dx_t[t] = dx_t[t] + lax.dot_general(
            table_rows, q, (((0,), (0,)), ((), ())), preferred_element_type=jnp.float32)

    def settle(u):
        for h in range(2):
            part_copy(h, u).wait()

    def compute(u):
        for h in range(2):
            rows_copy(h, u).wait()
        more_copy(u).wait()

        @pl.when(u + 1 < chunks)
        def _():
            for h in range(2):
                rows_copy(h, u + 1).start()
            more_copy(u + 1).start()

        slot = u % 2
        mine = y * half + u * size + steps_in_unit
        row_ids = jnp.where(steps_in_unit < size, mine, mine + (half // 2 - size))

        def main_tile(t, carry):
            q, hits = grads(rows_buf[slot], row_ids, t)
            at = pl.ds(pl.multiple_of(t * TILE, TILE), TILE)
            q_t[:, at] = q
            target[:, at] = target[:, at] + jnp.sum(hits, axis=0, keepdims=True)

            @pl.when(t < own // TILE)
            def _():
                add_dx(rows_buf[slot], q_t[:, at], t)
            return carry

        lax.fori_loop(0, tokens // TILE, main_tile, 0)

        def table_tile(n, carry):
            at = pl.ds(pl.multiple_of(n * 256, 256), 256)
            stage[:, at] = jnp.dot(q_t[...], x[:, at], preferred_element_type=jnp.float32)
            return carry

        lax.fori_loop(0, width // 256, table_tile, 0)
        for h in range(2):
            part_copy(h, u).start()

        theirs = (1 - y) * half + u * unit + steps_in_unit

        def more_tile(t, carry):
            q, _ = grads(more_buf[slot], theirs, t)
            add_dx(more_buf[slot], q, t)
            return carry

        lax.fori_loop(0, own // TILE, more_tile, 0)

    def send_reduced(h, c, src):
        @pl.when(c >= SLOTS)
        def _():
            pl.semaphore_wait(credit.at[h], 1)
        reduce_copy(h, c, src).start()

    def free_slot(h, c):
        @pl.when(c + SLOTS < chunks)
        def _():
            pl.semaphore_signal(credit.at[h], inc=1, device_id={'dp': back[h]}, device_id_type=MESH)

    def reduce_phase(s):
        for h in range(2):
            p = place[h]
            c = s - p
            here = (c >= 0) & (c < chunks)

            @pl.when(here & (p == 0))
            def _():
                @pl.when(c >= 2)
                def _():
                    reduce_copy(h, c - 2, part_rows(h, c - 2)).wait_send()
                send_reduced(h, c, part_rows(h, c))

            @pl.when(here & (p > 0))
            def _():
                slot = c % SLOTS
                reduce_copy(h, c, red.at[h, slot]).wait_recv()
                fetch(h, c).wait()
                red[h, slot] = red[h, slot] + loc[h, c % 2]

                @pl.when(p < Z - 1)
                def _():
                    @pl.when(c >= 2)
                    def _():
                        reduce_copy(h, c - 2, red.at[h, (c - 2) % SLOTS]).wait_send()
                        free_slot(h, c - 2)
                    send_reduced(h, c, red.at[h, slot])

                @pl.when(p == Z - 1)
                def _():
                    own_copy(h, c).start()

            @pl.when((p > 0) & (c >= -1) & (c + 1 < chunks))
            def _():
                fetch(h, c + 1).start()

    def spread_phase(s):
        for h in range(2):
            p = place[h]
            c = s - 2 * (Z - 1) + p

            @pl.when((c >= 0) & (c < chunks))
            def _():
                @pl.when(p == Z - 1)
                def _():
                    own_copy(h, c).wait()
                    free_slot(h, c)

                @pl.when(p < Z - 1)
                def _():
                    spread_copy(h, c).wait_recv()

                @pl.when(p > 0)
                def _():
                    spread_copy(h, c).start()

                mate_copy(h, c).start()

    def core_copy(i):
        return pltpu.make_async_remote_copy(
            src_ref=dx_t.at[2 * i + 1 - core], dst_ref=from_core.at[i], send_sem=core_sem.at[0, i],
            recv_sem=core_sem.at[1, i], device_id={'tp': partner}, device_id_type=MESH)

    def beside_copy():
        return pltpu.make_async_remote_copy(
            src_ref=dx_t.at[beside], dst_ref=from_x, send_sem=x_sem.at[0], recv_sem=x_sem.at[1],
            device_id={'tp': beside}, device_id_type=MESH)

    def share_copy(i, other):
        return pltpu.make_async_remote_copy(
            src_ref=dx_q, dst_ref=dx.at[tp], send_sem=share_send.at[i], recv_sem=share_recv.at[i],
            device_id={'tp': other}, device_id_type=MESH)

    def keep_copy():
        return pltpu.make_async_copy(dx_q, dx.at[tp], share_send.at[3])

    others = (partner, beside, across)
    block = 128

    def add_into(j, ref):
        def body(i, carry):
            at = pl.ds(pl.multiple_of(i * block, block), block)
            dx_t[j, at] = dx_t[j, at] + ref[at]
            return carry
        lax.fori_loop(0, width // block, body, 0)

    def dx_start():
        for i in range(2):
            core_copy(i).start()

    def dx_middle():
        for i in range(2):
            core_copy(i).wait_recv()
            add_into(2 * i + core, from_core.at[i])
        beside_copy().start()

    def dx_finish():
        beside_copy().wait_recv()
        add_into(tp, from_x)
        for i in range(width // block):
            at = pl.ds(i * block, block)
            dx_q[:, at] = dx_t[tp, at].T
        for i, other in enumerate(others):
            share_copy(i, other).start()
        keep_copy().start()

    def dx_end():
        for i in range(2):
            core_copy(i).wait_send()
        beside_copy().wait_send()
        for i, other in enumerate(others):
            share_copy(i, other).wait()
        keep_copy().wait()

    for h in range(2):
        rows_copy(h, 0).start()
    more_copy(0).start()
    target[...] = jnp.zeros_like(target)

    def clear(t, carry):
        dx_t[t] = jnp.zeros(dx_t.shape[1:], jnp.float32)
        return carry

    lax.fori_loop(0, own // TILE, clear, 0)
    pl.semaphore_wait(barrier, 5 + inner)

    done = last_tick(chunks)
    ticks = 1 + 2 * (chunks + 2 * (Z - 1))
    assert done + 9 < ticks

    def tick(i, carry):
        k = i // 2
        odd = i % 2 == 1
        earlier = jnp.maximum(i - 1, 1)

        @pl.when(i == 1)
        def _():
            settle(0)

        @pl.when(odd)
        def _():
            reduce_phase(k)

        @pl.when((i > 0) & (i % 2 == 0))
        def _():
            spread_phase(k - 1)

        @pl.when((i > 1) & has_unit(earlier, chunks))
        def _():
            settle(unit_at(earlier))

        @pl.when((i == 0) | has_unit(i, chunks))
        def _():
            compute(jnp.where(i == 0, 0, unit_at(i)))

        @pl.when(i == done + 1)
        def _():
            dx_start()

        @pl.when(i == done + 2)
        def _():
            dx_middle()

        @pl.when(i == done + 9)
        def _():
            dx_finish()
        return carry

    lax.fori_loop(0, ticks, tick, 0)

    for h in range(2):
        p = place[h]
        mine = out.at[pl.ds(y * half + h * (half // 2), half // 2)]
        theirs = out.at[pl.ds((1 - y) * half + h * (half // 2), half // 2)]

        @pl.when(p < Z - 1)
        def _():
            for c in (chunks - 2, chunks - 1):
                reduce_copy(h, c, red.at[h, c % SLOTS]).wait_send()

        @pl.when(p > 0)
        def _():
            pltpu.make_async_copy(mine, mine, bc_send.at[h]).wait()

        pltpu.make_async_copy(mine, mine, y_send.at[h]).wait()
        pltpu.make_async_copy(theirs, theirs, y_recv.at[h]).wait()
    dx_end()


def backward(table, x, x_t, lse, scale, label, n_tp, chunks):
    shard, width = table.shape
    half = shard // Y
    size = half // (2 * chunks)
    tokens = x.shape[0]
    quarter = tokens // Y // n_tp
    assert size * 2 * chunks == half and size % 16 == 0 and quarter == TILE
    f32 = jnp.float32
    dma = pltpu.SemaphoreType.DMA
    vmem = pl.BlockSpec(memory_space=pltpu.VMEM)
    hbm = pl.BlockSpec(memory_space=pl.ANY)
    flops = 2 * width * half * (2 * tokens + 3 * tokens // Y)
    return pl.pallas_call(
        functools.partial(backward_kernel, chunks),
        out_shape=(
            jax.ShapeDtypeStruct((shard, width), f32),
            jax.ShapeDtypeStruct((half, width), f32),
            jax.ShapeDtypeStruct((n_tp, quarter, width), f32),
            jax.ShapeDtypeStruct((1, tokens), f32)),
        in_specs=[hbm, vmem, vmem, vmem, vmem, vmem],
        out_specs=(hbm, hbm, hbm, vmem),
        scratch_shapes=[
            pltpu.VMEM((2, SLOTS, size, width), f32),
            pltpu.VMEM((2, 2, size, width), f32),
            pltpu.VMEM((2 * size, tokens), jnp.bfloat16),
            pltpu.VMEM((2, 2 * size, width), jnp.bfloat16),
            pltpu.VMEM((2, 2 * size, width), jnp.bfloat16),
            pltpu.VMEM((2 * size, width), f32),
            pltpu.VMEM((n_tp, width, quarter), f32),
            pltpu.VMEM((2, width, quarter), f32),
            pltpu.VMEM((width, quarter), f32),
            pltpu.VMEM((quarter, width), f32),
            dma((2, SLOTS)), dma((2, SLOTS)), pltpu.SemaphoreType.REGULAR((2,)),
            dma((2,)), dma((2, chunks)),
            dma((2,)), dma((2,)),
            dma((2, 2)), dma((2,)), dma((2,)), dma((2, 2)), dma((2,)),
            dma((2, 2)), dma((2,)), dma((4,)), dma((3,)),
        ],
        compiler_params=pltpu.CompilerParams(
            collective_id=0, has_side_effects=True, vmem_limit_bytes=62 * 1024 * 1024),
        cost_estimate=pl.CostEstimate(flops=flops, bytes_accessed=12 * half * width, transcendentals=half * tokens),
    )(table, x, x_t, lse, scale, label)


def norm_stats(hidden):
    h32 = hidden.astype(jnp.float32)
    mean = jnp.mean(h32, axis=-1, keepdims=True)
    centred = h32 - mean
    variance = jnp.mean(centred * centred, axis=-1, keepdims=True)
    inv_std = lax.rsqrt(variance + LN_EPS)
    return centred * inv_std, inv_std


def norm_backward(grad_x, x_hat, inv_std, ln_gain):
    grad_hat = grad_x * ln_gain.astype(jnp.float32)
    mean_grad = jnp.mean(grad_hat, axis=-1, keepdims=True)
    mean_proj = jnp.mean(grad_hat * x_hat, axis=-1, keepdims=True)
    return (inv_std * (grad_hat - mean_grad - x_hat * mean_proj)).astype(jnp.bfloat16)


def solution(mesh):
    n_dp = mesh.shape['dp']
    n_tp = mesh.shape['tp']
    to_mate = [(i, i ^ 1) for i in range(n_dp)]
    to_core = [(i, i ^ 1) for i in range(n_tp)]

    def device_step(hidden, table, labels, loss_mask, ln_gain, ln_bias):
        batch, seq, width = hidden.shape
        tokens = batch * seq
        shard = table.shape[0]
        tp = lax.axis_index('tp')
        core = tp % 2
        gain = ln_gain.astype(jnp.float32)
        bias = ln_bias.astype(jnp.float32)

        x_hat, inv_std = norm_stats(hidden.reshape(tokens, width))
        piece = lax.dynamic_slice(x_hat, (core * (tokens // 2), 0), (tokens // 2, width))
        got = lax.ppermute(piece, 'dp', to_mate)
        got2 = lax.ppermute(got, 'tp', to_core)
        ids = jnp.stack([labels.reshape(tokens), loss_mask.reshape(tokens)])
        ids_mate = lax.ppermute(ids, 'dp', to_mate)

        x = (x_hat * gain + bias).astype(jnp.bfloat16)
        logits = lax.dot_general(x, table, (((1,), (1,)), ((), ())), preferred_element_type=jnp.float32)
        row_ids = tp * shard + lax.broadcasted_iota(jnp.int32, (1, shard), 1)
        logits = jnp.where(row_ids < VOCAB, logits, -jnp.inf)
        top = jnp.maximum(jnp.max(logits, axis=-1), jnp.finfo(jnp.float32).min)
        exp_sum = jnp.sum(jnp.exp(logits - top[:, None]), axis=-1)
        stats = lax.all_gather(jnp.stack([top, exp_sum]), 'tp')
        best = jnp.max(stats[:, 0], axis=0)
        log_norm = best + jnp.log(jnp.sum(stats[:, 1] * jnp.exp(stats[:, 0] - best), axis=0))
        norm_mate = lax.ppermute(log_norm, 'dp', to_mate)

        mask = loss_mask.reshape(tokens).astype(jnp.float32)
        count = lax.psum(jnp.sum(mask), 'dp')

        first = jnp.where(core == 0, got, got2)
        second = jnp.where(core == 0, got2, got)
        x_mate = (jnp.concatenate([first, second]) * gain + bias).astype(jnp.bfloat16)
        x_all = jnp.concatenate([x, x_mate])
        lse = jnp.concatenate([log_norm, norm_mate])[None]
        label = jnp.concatenate([ids[0], ids_mate[0]])[None] - tp * shard
        weight = jnp.concatenate([mask, ids_mate[1].astype(jnp.float32)])[None]

        grad_table, _, grad_x, target = backward(table, x_all, x_all.T, lse, weight / count, label, n_tp, CHUNKS)

        grad_x = grad_x.reshape(tokens, width)
        grad_hidden = norm_backward(grad_x, x_hat, inv_std, ln_gain).reshape(batch, seq, width)
        sums = jnp.stack([jnp.sum(grad_x * x_hat, axis=0), jnp.sum(grad_x, axis=0)])
        lost = jnp.sum(mask * log_norm) / n_tp - jnp.sum(weight * target)
        sums, lost = lax.psum((sums / n_tp, lost), ('dp', 'tp'))
        return lost / count, grad_hidden, grad_table, sums[0], sums[1]

    specs_in = (P('dp', None, None), P('tp', None), P('dp', None), P('dp', None), P(None), P(None))
    specs_out = (P(), P('dp', None, None), P('tp', None), P(None), P(None))
    return jax.shard_map(device_step, mesh=mesh, in_specs=specs_in, out_specs=specs_out, check_vma=False)
```

time: 1980 us -> 1000 us (0.51)
  waiting for transfers between devices: 1540 us -> 26.7 us
  Pallas kernels: 0 us -> 687 us
  matrix products: 246 us -> 65.6 us
  local copies, waits for them, and re-layouts: 35.7 us -> 63.1 us
    psum x2 -> x0, waiting for transfers between devices: 1540 us -> none  [the longest x1 1480 us: device_step(): lax.psum(jnp.einsum('btv,btd->vd', grad_logits, x_norm, preferred_element...]
    pallas_call x0 -> x1, Pallas kernels: none -> 687 us  [backward(): pl.pallas_call(functools.partial(backward_kernel, chunks), out_shape=(jax...]
    dot_general x3 -> x1, matrix products: 246 us -> 65.6 us  [device_step(): lax.dot_general(x, table, (((1,), (1,)), ((), ())), preferred_element_typ...]
    ppermute x0 -> x4, waiting for transfers between devices: none -> 26.7 us  [the longest x1 26.7 us: device_step(): got = lax.ppermute(piece, 'dp', to_mate)]
    psum x3 -> x2, blocking collectives: 57.1 us -> 62.7 us  [the longest x1 40.2 us: device_step(): sums, lost = lax.psum((sums / n_tp, lost), ('dp', 'tp'))]
    reduce_sum x5 -> x7, other arithmetic: 48.1 us -> 47.9 us  [the longest x1 32.3 us: device_step(): exp_sum = jnp.sum(jnp.exp(logits - top[:, None]), axis=-1)]
  transfers between devices with their start and end apart: 2 -> 4, of which waited for: 2 -> 1; matrix products, arithmetic and copies ran while one was open for 6% -> 13% of each run, Pallas kernels for 0% -> 0%
where the time goes in v2:
time: 1000 us
  Pallas kernels  687 us (69%)
  other arithmetic  82.7 us (8%)
  blocking collectives  67.9 us (7%)
  matrix products  65.6 us (7%)
  local copies, waits for them, and re-layouts  63.1 us (6%)
  waiting for transfers between devices  26.7 us (3%)
    pallas_call x1, Pallas kernels, backward(): pl.pallas_call(functools.partial(backward_kernel, chunks), out_shape=(jax...  687 us
    dot_general x1, matrix products, device_step(): lax.dot_general(x, table, (((1,), (1,)), ((), ())), preferred_element_typ...  65.6 us
    psum x1, blocking collectives, device_step(): sums, lost = lax.psum((sums / n_tp, lost), ('dp', 'tp'))  40.2 us
    unnamed x33, local copies, waits for them, and re-layouts  37.6 us
    reduce_sum x1, other arithmetic, device_step(): exp_sum = jnp.sum(jnp.exp(logits - top[:, None]), axis=-1)  32.3 us
    ppermute x1, waiting for transfers between devices, device_step(): got = lax.ppermute(piece, 'dp', to_mate)  26.7 us
    psum x1, blocking collectives, device_step(): count = lax.psum(jnp.sum(mask), 'dp')  22.5 us
  transfers between devices with their start and end apart: 4, of which 1 were waited for; matrix products, arithmetic and copies ran while one was open for 13% of the time, Pallas kernels for 0%

profile of v2, /device:TPU:0, one launch (start us, length us, event | category | flops | bytes accessed | tf_op | source)
XLA Modules:
  0.0 1001.0 jit_solution(2547480366611190896)
XLA Ops:
  0.6 0.7 copy.24
  1.3 0.7 copy.23
  2.1 3.1 collective-permute-start
  5.1 0.0 copy-start.11
  5.1 0.0 copy-start.12
  5.1 2.8 convert_reduce_fusion
  8.0 6.6 convert_element_type.70
  14.6 0.0 copy-done.11
  14.6 0.0 copy-done.12
  14.6 0.0 copy-start.3
  14.7 0.0 copy-start.1
  14.7 3.0 multiply_reduce_fusion.2
  17.7 0.0 copy-start.5
  17.7 9.2 copy.17
  26.9 5.6 add_convert_fusion
  32.5 2.5 constant_dynamic-slice_fusion
  35.0 0.0 collective-permute-start.1
  35.0 65.6 %select_reduce_fusion = (f32[2048]{0:T(1024)S(1)}, f32[2048,12672]{1,0:T(8,128)}) fusion(pred[12672]{0:T(1024)(128)(4,1)S(1)} %add_compare_fusion, bf16[2048,1024]{0,1:T(8,128)(2,1)} %get-tuple-element.19, bf16[12672,1024]{1,0:T(8,128)(2,1)} %table.1), kind=kOutput, calls=%fused_computation.1 | convolution fusion | flops 53202124800 | bytes 133976448 | tf_op jit(solution)/shard_map/dot_general | solution.py:461
  100.6 26.7 %collective-permute-done.1 = f32[1024,1024]{0,1:T(8,128)} collective-permute-done((f32[1024,1024]{0,1:T(8,128)}, f32[1024,1024]{0,1:T(8,128)}, u32[]{:S(2)}, u32[]{:S(2)}) %collective-permute-start.1) | collective-permute-done | bytes 4194336 | tf_op jit(solution)/shard_map/ppermute | solution.py:455
  127.4 0.0 collective-permute-start.2
  127.4 0.0 copy-start.7
  127.4 32.3 %exponential_reduce_fusion = f32[2048]{0:T(1024)S(1)} fusion(f32[2048,12672]{1,0:T(8,128)} %get-tuple-element.39, f32[2048]{0:T(1024)S(1)} %broadcast_maximum_fusion, pred[12672]{0:T(1024)(128)(4,1)S(1)} %add_compare_fusion), kind=kLoop, calls=%fused_computation | loop fusion | flops 77854720 | bytes 103838080 | tf_op jit(solution)/shard_map/reduce_sum | solution.py:465
  159.7 5.2 all-gather.1
  164.9 0.1 fusion.9
  165.0 0.5 collective-permute-start.3
  165.5 0.0 copy-done.7
  165.6 0.6 convert_reduce_fusion.1
  166.2 22.5 %psum.21 = f32[]{:T(128)} all-reduce(f32[]{:T(128)} %get-tuple-element.15), channel_id=1, replica_groups=mesh['dp'=8,'tp'=4] {'dp'}, use_global_device_ids=true, to_apply=%region_8.9 | all-reduce | flops 1 | bytes 8 | tf_op jit(solution)/shard_map/psum | solution.py:472
  188.7 0.0 copy-done.1
  188.7 0.6 div.47
  189.3 0.0 copy-done.5
  189.3 0.6 rsqrt.18
  190.6 0.0 collective-permute-done.3
  190.6 0.6 pad_maximum_fusion.2
  191.2 0.0 collective-permute-done
  191.2 0.6 pad_maximum_fusion.1
  191.8 0.6 add_subtract_fusion.label
  192.4 1.3 maximum_divide_fusion.scale
  193.7 0.0 collective-permute-done.2
  193.7 4.4 broadcast_select_fusion.1
  198.1 0.0 copy-start
  198.2 0.0 copy-done.3
  198.2 1.1 fusion.1
  199.3 1.1 copy-done
  200.3 6.4 fusion.8
  206.7 11.9 %copy.16.x = bf16[4096,1024]{1,0:T(8,128)(2,1)} copy(bf16[4096,1024]{0,1:T(8,128)(2,1)} %get-tuple-element.22) | data formatting | bytes 16777216 | tf_op jit(solution)/shard_map/concatenate | solution.py:477
  218.7 0.0 copy-start.8
  218.7 0.0 copy-start.4
  218.7 0.0 copy-start.9
  218.7 0.0 copy-start.10
  218.7 686.7 %shard_map.101 = (f32[12672,1024]{1,0:T(8,128)}, f32[6336,1024]{1,0:T(8,128)}, f32[4,512,1024]{2,1,0:T(8,128)}, f32[1,4096]{1,0:T(1,128)}) custom-call(bf16[12672,1024]{1,0:T(8,128)(2,1)} %table.1, bf16[4096,1024]{1,0:T(8,128)(2,1)} %copy.16.x, bf16[1024,4096]{1,0:T(8,128)(2,1)} %get-tuple-element.21.x_t, f32[1,4096]{1,0:T(1,128)} %bitcast.74, ...), custom_call_target="tpu_custom_call" | custom-call | flops 186025771008 | bytes 77856768 | tf_op jit(solution)/shard_map/pallas_call | solution.py:390
  905.4 0.0 copy-done.8
  905.5 1.4 multiply_reduce_fusion.4
  906.8 0.0 copy-done.4
  906.8 0.0 copy-done.9
  906.8 0.0 copy-done.10
  906.8 0.0 copy-start.6
  906.8 7.8 multiply_reduce_fusion
  915.3 40.2 %all-reduce = (f32[]{:T(128)}, f32[2,1024]{1,0:T(2,128)S(1)}) all-reduce(f32[]{:T(128)S(6)} %sub.68, f32[2,1024]{1,0:T(2,128)S(1)} %maximum_multiply_fusion.1), channel_id=1, replica_groups=mesh['dp'=8,'tp'=4] {'dp','tp'}, use_global_device_ids=true, to_apply=%region_10.11 | all-reduce | flops 2049 | bytes 16392 | tf_op jit(solution)/shard_map/psum | solution.py:488
  956.9 0.6 fusion.11
  957.5 0.0 copy-done.2
  957.5 0.0 copy-done.6
  957.5 7.3 multiply_convert_fusion
  964.8 35.1 %copy.33 = f32[12672,1024]{1,0:T(8,128)} copy(f32[12672,1024]{1,0:T(8,128)} %get-tuple-element.49) | data formatting | bytes 103809024
  (22 shorter events, 0.2 us)
Async XLA Ops:
  2.1 189.1 %collective-permute-start = (s32[2,2048]{1,0:T(2,128)S(1)}, s32[2,2048]{1,0:T(2,128)S(1)}, u32[]{:S(2)}, u32[]{:S(2)}) collective-permute-start(s32[2,2048]{1,0:T(2,128)S(1)} %pad_add_fusion), channel_id=1, source_target_pairs={{0,4},{4,0},{8,12},{12,8},{16,20},{20,16},{24,28},{28,24},{1,5},{5... | collective-permute-start | bytes 49160 | tf_op jit(solution)/shard_map/ppermute | solution.py:458
  5.1 9.5 copy-start.11
  5.1 9.5 copy-start.12
  14.6 183.5 %copy-start.3 = (f32[1024]{0:T(1024)}, f32[1024]{0:T(1024)S(1)}, u32[]{:S(2)}) copy-start(f32[1024]{0:T(1024)S(1)} %convert_element_type.60) | copy-start | bytes 12292
  14.7 174.0 %copy-start.1 = (f32[8,256]{1,0:T(8,128)}, f32[8,256]{1,0:T(8,128)S(1)}, u32[]{:S(2)}) copy-start(f32[8,256]{1,0:T(8,128)S(1)} %get-tuple-element.37) | copy-start | bytes 24580
  17.7 171.6 %copy-start.5 = (f32[8,256]{1,0:T(8,128)}, f32[8,256]{1,0:T(8,128)S(1)}, u32[]{:S(2)}) copy-start(f32[8,256]{1,0:T(8,128)S(1)} %get-tuple-element.32) | copy-start | bytes 24580
  35.0 92.3 %collective-permute-start.1 = (f32[1024,1024]{0,1:T(8,128)}, f32[1024,1024]{0,1:T(8,128)}, u32[]{:S(2)}, u32[]{:S(2)}) collective-permute-start(f32[1024,1024]{0,1:T(8,128)} %constant_dynamic-slice_fusion), channel_id=1, source_target_pairs={{0,4},{4,0},{8,12},{12,8},{16,20},{20,16},{24,28},{28,24},{1,5},{5... | collective-permute-start | bytes 12582920 | tf_op jit(solution)/shard_map/ppermute | solution.py:455
  127.4 66.3 %collective-permute-start.2 = (f32[1024,1024]{0,1:T(8,128)}, f32[1024,1024]{0,1:T(8,128)}, u32[]{:S(2)}, u32[]{:S(2)}) collective-permute-start(f32[1024,1024]{0,1:T(8,128)} %collective-permute-done.1), channel_id=1, source_target_pairs={{0,1},{1,0},{2,3},{3,2},{4,5},{5,4},{6,7},{7,6},{8,9},{9,8},{10,11... | collective-permute-start | bytes 12582920 | tf_op jit(solution)/shard_map/ppermute | solution.py:456
  127.4 38.2 %copy-start.7 = (s32[8,256]{1,0:T(8,128)S(1)}, s32[8,256]{1,0:T(8,128)}, u32[]{:S(2)}) copy-start(s32[8,256]{1,0:T(8,128)} %param.9) | copy-start | bytes 24580
  165.0 25.6 %collective-permute-start.3 = (f32[2048]{0:T(1024)S(1)}, f32[2048]{0:T(1024)S(1)}, u32[]{:S(2)}, u32[]{:S(2)}) collective-permute-start(f32[2048]{0:T(1024)S(1)} %log_add_fusion), channel_id=1, source_target_pairs={{0,4},{4,0},{8,12},{12,8},{16,20},{20,16},{24,28},{28,24},{1,5},{5... | collective-permute-start | bytes 24584 | tf_op jit(solution)/shard_map/ppermute | solution.py:469
  198.1 2.2 copy-start
  218.7 686.8 %copy-start.8 = (f32[4096]{0:T(1024)S(1)}, f32[4096]{0:T(1024)}, u32[]{:S(2)}) copy-start(f32[4096]{0:T(1024)} %pad_maximum_fusion.1) | copy-start | bytes 49156
  218.7 688.1 %copy-start.4 = (f32[1024]{0:T(1024)S(1)}, f32[1024]{0:T(1024)}, u32[]{:S(2)}) copy-start(f32[1024]{0:T(1024)} %copy-done.3) | copy-start | bytes 12292
  218.7 688.1 %copy-start.9 = (f32[4,512]{1,0:T(4,128)S(1)}, f32[4,512]{1,0:T(4,128)}, u32[]{:S(2)}) copy-start(f32[4,512]{1,0:T(4,128)} %div.47) | copy-start | bytes 24580
  218.7 688.1 %copy-start.10 = (f32[4,512]{1,0:T(4,128)S(1)}, f32[4,512]{1,0:T(4,128)}, u32[]{:S(2)}) copy-start(f32[4,512]{1,0:T(4,128)} %rsqrt.18) | copy-start | bytes 24580
  906.8 50.7 %copy-start.2 = (f32[8,256]{1,0:T(8,128)S(1)}, f32[8,256]{1,0:T(8,128)}, u32[]{:S(2)}) copy-start(f32[8,256]{1,0:T(8,128)} %copy-done.1) | copy-start | bytes 24580
  906.8 50.7 %copy-start.6 = (f32[8,256]{1,0:T(8,128)S(1)}, f32[8,256]{1,0:T(8,128)}, u32[]{:S(2)}) copy-start(f32[8,256]{1,0:T(8,128)} %copy-done.5) | copy-start | bytes 24580

commit v3 on v2

--- a/solution.py
+++ b/solution.py
@@ -14,59 +14,359 @@
 CHUNKS = 33
 SLOTS = 8
 TILE = 512
+PIECES = 4
+FORWARD_ROWS = 384
 MESH = pl.DeviceIdType.MESH
 
 
-def unit_at(i):
-    return 1 + i // 2 + (i // 2 + i % 2) // 2
-
-
-def has_unit(i, units):
-    return ((i % 2 == 1) | (i // 2 % 2 == 1)) & (unit_at(i) < units)
-
-
-def last_tick(units):
-    return max(i for i in range(1, 4 * units) if has_unit(i, units))
+def signal(barrier, **where):
+    pl.semaphore_signal(barrier, inc=1, device_id=where, device_id_type=MESH)
+
+
+def neighbours(tp):
+    core = tp % 2
+    partner = tp + 1 - 2 * core
+    beside = tp + 2 - 4 * (tp // 2)
+    return partner, beside, beside + 1 - 2 * core
+
+
+def forward_kernel(
+        n_dp, n_tp, table, hidden, gain, bias, mask,
+        x_all, xt_all, lse, count, hat_q, inv_q,
+        x_own, xt_own, send_q, got, x_mate, xt_mate, rows_buf, top, total, stats, counts, hat_buf,
+        rows_sem, y_sem, beside_sem, core_sem, relay_sem, stat_send, stat_recv, count_send, count_recv, out_sem):
+    own, width = hidden.shape
+    shard = table.shape[0]
+    size = rows_buf.shape[1]
+    blocks = shard // size
+    quarter = own // n_tp
+    piece = quarter // PIECES
+    dp = lax.axis_index('dp')
+    tp = lax.axis_index('tp')
+    mate = dp + 1 - 2 * (dp % Y)
+    partner, beside, across = neighbours(tp)
+    others = (partner, beside, across)
+    dp_others = [lax.rem(dp + j, n_dp) for j in range(1, n_dp)]
+
+    barrier = pltpu.get_barrier_semaphore()
+    for other in dp_others:
+        signal(barrier, dp=other)
+    for other in others:
+        signal(barrier, tp=other)
+        signal(barrier, dp=mate, tp=other)
+
+    def rows_copy(b):
+        return pltpu.make_async_copy(table.at[pl.ds(b * size, size)], rows_buf.at[b % 2], rows_sem.at[b % 2])
+
+    def remote(src, dst, sems, k, **where):
+        return pltpu.make_async_remote_copy(
+            src_ref=src, dst_ref=dst, send_sem=sems.at[0, k], recv_sem=sems.at[1, k],
+            device_id=where, device_id_type=MESH)
+
+    def got_piece(q, k):
+        return got.at[q, pl.ds(k * piece, piece)]
+
+    def y_copy(k):
+        return remote(send_q.at[pl.ds(k * piece, piece)], got_piece(tp, k), y_sem, k, dp=mate)
+
+    def beside_copy(k):
+        return remote(got_piece(tp, k), got_piece(tp, k), beside_sem, k, tp=beside)
+
+    def core_copy(k):
+        return remote(got_piece(tp, k), got_piece(tp, k), core_sem, k, tp=partner)
+
+    def relay_copy(k):
+        return remote(got_piece(beside, k), got_piece(beside, k), relay_sem, k, tp=partner)
+
+    def count_copy(j):
+        return pltpu.make_async_remote_copy(
+            src_ref=counts.at[dp], dst_ref=counts.at[dp], send_sem=count_send.at[j], recv_sem=count_recv.at[dp],
+            device_id={'dp': dp_others[j]}, device_id_type=MESH)
+
+    def count_arrival(j):
+        other = dp_others[j]
+        return pltpu.make_async_remote_copy(
+            src_ref=counts.at[other], dst_ref=counts.at[other], send_sem=count_send.at[j], recv_sem=count_recv.at[other],
+            device_id={'dp': other}, device_id_type=MESH)
+
+    def normalize(at):
+        h = hidden[at, :].astype(jnp.float32)
+        mean = jnp.mean(h, axis=-1, keepdims=True)
+        centred = h - mean
+        variance = jnp.mean(centred * centred, axis=-1, keepdims=True)
+        inv_std = lax.rsqrt(variance + LN_EPS)
+        x_hat = centred * inv_std
+        x = (x_hat * gain[...] + bias[...]).astype(jnp.bfloat16)
+        wide = x.astype(jnp.float32)
+        x_own[at, :] = x
+        xt_own[:, at] = wide.T.astype(jnp.bfloat16)
+        return x_hat, inv_std, wide
+
+    def block_of(q, k):
+        return pl.ds(pl.multiple_of(q * quarter + k * piece, piece), piece)
+
+    def first_piece(k, carry):
+        x_hat, inv_std, wide = normalize(block_of(tp, k))
+        at = pl.ds(pl.multiple_of(k * piece, piece), piece)
+        send_q[at, :] = wide
+        hat_buf[at, :] = x_hat
+        inv_q[at, :] = jnp.broadcast_to(inv_std, (piece, inv_q.shape[1]))
+
+        @pl.when(k == 0)
+        def _():
+            pl.semaphore_wait(barrier, n_dp - 1 + 2 * len(others))
+        y_copy(k).start()
+        return carry
+
+    rows_copy(0).start()
+    lax.fori_loop(0, PIECES, first_piece, 0)
+
+    def next_piece(j, carry):
+        normalize(block_of(lax.rem(tp + 1 + j // PIECES, n_tp), j % PIECES))
+        return carry
+
+    lax.fori_loop(0, (n_tp - 1) * PIECES, next_piece, 0)
+    own_outs = (
+        pltpu.make_async_copy(x_own, x_all.at[pl.ds(0, own)], out_sem.at[0]),
+        pltpu.make_async_copy(xt_own, xt_all.at[:, pl.ds(0, own)], out_sem.at[1]),
+        pltpu.make_async_copy(hat_buf, hat_q, out_sem.at[2]))
+    for copy in own_outs:
+        copy.start()
+
+    counts[dp] = jnp.full(counts.shape[1:], jnp.sum(mask[...]), jnp.float32)
+    for j in range(n_dp - 1):
+        count_copy(j).start()
+    top[...] = jnp.full_like(top, jnp.finfo(jnp.float32).min)
+    total[...] = jnp.zeros_like(total)
+
+    def convert(q, k):
+        wide = got[q, pl.ds(pl.multiple_of(k * piece, piece), piece)]
+        at = block_of(q, k)
+        x_mate[at, :] = wide.astype(jnp.bfloat16)
+        xt_mate[:, at] = wide.T.astype(jnp.bfloat16)
+
+    first_row = tp * shard
+
+    def block(b, carry):
+        rows_copy(b).wait()
+
+        @pl.when(b + 1 < blocks)
+        def _():
+            rows_copy(b + 1).start()
+
+        phase = b % 6
+
+        @pl.when((phase == 0) & (b > 0) & (b <= 6 * PIECES))
+        def _():
+            k = jnp.maximum(b // 6 - 1, 0)
+            y_copy(k).wait_recv()
+            beside_copy(k).start()
+            core_copy(k).start()
+            convert(tp, k)
+
+        @pl.when((phase == 2) & (b >= 14) & (b < 14 + 6 * PIECES))
+        def _():
+            k = jnp.maximum(b - 14, 0) // 6
+            beside_copy(k).wait_recv()
+            relay_copy(k).start()
+            convert(beside, k)
+
+        @pl.when((phase == 4) & (b >= 10) & (b < 10 + 6 * PIECES))
+        def _():
+            k = jnp.maximum(b - 10, 0) // 6
+            core_copy(k).wait_recv()
+            convert(partner, k)
+
+        @pl.when((phase == 4) & (b >= 16) & (b < 10 + 6 * PIECES))
+        def _():
+            k = jnp.maximum(b - 16, 0) // 6
+            relay_copy(k).wait_recv()
+            convert(across, k)
+
+        slot = b % 2
+        row_ids = first_row + b * size + lax.broadcasted_iota(jnp.int32, (size, 1), 0)
+
+        def tile(t, carry):
+            at = pl.ds(pl.multiple_of(t * TILE, TILE), TILE)
+            logits = jnp.dot(rows_buf[slot], xt_own[:, at], preferred_element_type=jnp.float32)
+            logits = jnp.where(row_ids < VOCAB, logits, -jnp.inf).reshape(size // 8, 8, TILE)
+            before = top[:, at]
+            now = jnp.maximum(before, jnp.max(logits, axis=0))
+            total[:, at] = total[:, at] * jnp.exp(before - now) + jnp.sum(jnp.exp(logits - now[None]), axis=0)
+            top[:, at] = now
+            return carry
+
+        lax.fori_loop(0, own // TILE, tile, 0)
+        return carry
+
+    assert blocks > 8 + 6 * PIECES
+    lax.fori_loop(0, blocks, block, 0)
+
+    best = jnp.max(top[...], axis=0, keepdims=True)
+    stats[0, tp, 0:1] = best
+    stats[0, tp, 1:2] = jnp.sum(total[...] * jnp.exp(top[...] - best), axis=0, keepdims=True)
+
+    def stat_copies():
+        copies = []
+        for i, other in enumerate(others):
+            copies.append((0, i, {'tp': other}))
+        copies.append((1, 3, {'dp': mate}))
+        for i, other in enumerate(others):
+            copies.append((1, 4 + i, {'dp': mate, 'tp': other}))
+        return [pltpu.make_async_remote_copy(
+            src_ref=stats.at[0, tp], dst_ref=stats.at[side, tp], send_sem=stat_send.at[i], recv_sem=stat_recv.at[side, tp],
+            device_id=where, device_id_type=MESH) for side, i, where in copies]
+
+    def stat_arrival(side, other):
+        return pltpu.make_async_remote_copy(
+            src_ref=stats.at[side, other], dst_ref=stats.at[side, other], send_sem=stat_send.at[0],
+            recv_sem=stat_recv.at[side, other], device_id={'tp': other}, device_id_type=MESH)
+
+    for copy in stat_copies():
+        copy.start()
+    last = PIECES - 1
+    relay_copy(last).wait_recv()
+    convert(across, last)
+    mate_outs = (
+        pltpu.make_async_copy(x_mate, x_all.at[pl.ds(own, own)], out_sem.at[3]),
+        pltpu.make_async_copy(xt_mate, xt_all.at[:, pl.ds(own, own)], out_sem.at[4]))
+    for copy in mate_outs:
+        copy.start()
+    for other in others:
+        stat_arrival(0, other).wait_recv()
+    for other in (tp,) + others:
+        stat_arrival(1, other).wait_recv()
+    for side in range(Y):
+        tops = [stats[side, j, 0:1] for j in range(n_tp)]
+        best = functools.reduce(jnp.maximum, tops)
+        mass = sum(stats[side, j, 1:2] * jnp.exp(tops[j] - best) for j in range(n_tp))
+        lse[:, side * own:(side + 1) * own] = best + jnp.log(mass)
+    for j in range(n_dp - 1):
+        count_arrival(j).wait_recv()
+    count[...] = sum(counts[j] for j in range(n_dp))
+
+    for k in range(PIECES):
+        for copy in (y_copy(k), beside_copy(k), core_copy(k), relay_copy(k)):
+            copy.wait_send()
+    for copy in stat_copies():
+        copy.wait_send()
+    for j in range(n_dp - 1):
+        count_copy(j).wait_send()
+    for copy in own_outs + mate_outs:
+        copy.wait()
+
+
+def forward(table, hidden, gain, bias, mask, n_dp, n_tp):
+    own, width = hidden.shape
+    shard = table.shape[0]
+    quarter = own // n_tp
+    assert shard % FORWARD_ROWS == 0
+    f32 = jnp.float32
+    b16 = jnp.bfloat16
+    dma = pltpu.SemaphoreType.DMA
+    vmem = pl.BlockSpec(memory_space=pltpu.VMEM)
+    hbm = pl.BlockSpec(memory_space=pl.ANY)
+    lanes = 128
+    return pl.pallas_call(
+        functools.partial(forward_kernel, n_dp, n_tp),
+        out_shape=(
+            jax.ShapeDtypeStruct((Y * own, width), b16),
+            jax.ShapeDtypeStruct((width, Y * own), b16),
+            jax.ShapeDtypeStruct((1, Y * own), f32),
+            jax.ShapeDtypeStruct((8, lanes), f32),
+            jax.ShapeDtypeStruct((quarter, width), f32),
+            jax.ShapeDtypeStruct((quarter, lanes), f32)),
+        in_specs=[hbm, vmem, vmem, vmem, vmem],
+        out_specs=(hbm, hbm, vmem, vmem, hbm, vmem),
+        scratch_shapes=[
+            pltpu.VMEM((own, width), b16), pltpu.VMEM((width, own), b16),
+            pltpu.VMEM((quarter, width), f32), pltpu.VMEM((n_tp, quarter, width), f32),
+            pltpu.VMEM((own, width), b16), pltpu.VMEM((width, own), b16),
+            pltpu.VMEM((2, FORWARD_ROWS, width), b16),
+            pltpu.VMEM((8, own), f32), pltpu.VMEM((8, own), f32),
+            pltpu.VMEM((Y, n_tp, 2, own), f32), pltpu.VMEM((n_dp, 8, lanes), f32),
+            pltpu.VMEM((quarter, width), f32),
+            dma((2,)), dma((2, PIECES)), dma((2, PIECES)), dma((2, PIECES)), dma((2, PIECES)),
+            dma((2 * n_tp - 1,)), dma((Y, n_tp)), dma((n_dp - 1,)), dma((n_dp,)), dma((5,)),
+        ],
+        compiler_params=pltpu.CompilerParams(
+            collective_id=1, has_side_effects=True, vmem_limit_bytes=56 * 1024 * 1024),
+        cost_estimate=pl.CostEstimate(
+            flops=2 * own * shard * width, bytes_accessed=2 * shard * width, transcendentals=own * shard),
+    )(table, hidden, gain, bias, mask)
+
+
+EVERY = 4
+
+
+def main_unit(i):
+    k, odd = i // 2, i % 2
+    return 1 + k + (k + EVERY - 2 + odd) // EVERY
+
+
+def has_main(i, units):
+    return ((i % 2 == 1) | (i // 2 % EVERY == 1)) & (main_unit(i) < units)
+
+
+def last_main(units):
+    return max(i for i in range(1, 4 * units) if has_main(i, units))
+
+
+def more_unit(i, units):
+    end = last_main(units)
+    return jnp.where(i <= end, i // 2 - 1, jnp.maximum(i - end, 0) + end // 2 - 1)
+
+
+def has_more(i, units):
+    end = last_main(units)
+    return (i > 0) & ((i > end) | (i % 2 == 0)) & (more_unit(i, units) < units)
+
+
+def last_more(units):
+    end = last_main(units)
+    return end + units - end // 2
 
 
 def backward_kernel(
-        chunks, table, x, x_t, lse, scale, label,
-        out, part, dx, target,
-        red, loc, q_t, rows_buf, more_buf, stage, dx_t, from_core, from_x, dx_q,
+        chunks, table, x, x_t, lse, weight, label, count, hat, inv, gain,
+        out, part, dh, sums,
+        red, loc, q_t, rows_buf, more_buf, stage, dx_t, from_core, from_x, dx_q, scale, target, levels, arrived,
         red_send, red_recv, credit, bc_send, bc_recv, y_send, y_recv, loc_sem, own_sem, part_sem, rows_sem, more_sem,
-        core_sem, x_sem, share_send, share_recv):
+        core_sem, x_sem, share_send, share_recv, level_sem):
     size = red.shape[2]
     half = part.shape[0]
     unit = 2 * size
     tokens = x.shape[0]
     own = tokens // Y
     width = x.shape[1]
-    quarter = dx.shape[1]
+    quarter = dh.shape[1]
+    n_tp = dh.shape[0]
     dp = lax.axis_index('dp')
     tp = lax.axis_index('tp')
     y = dp % Y
     z = dp // Y
     core = tp % 2
     mate = dp + 1 - 2 * y
-    partner = tp + 1 - 2 * core
-    beside = tp + 2 - 4 * (tp // 2)
-    across = beside + 1 - 2 * core
+    partner, beside, across = neighbours(tp)
+    z_mate = dp + Y - 2 * Y * (z % 2)
+    z_far = dp + 2 * Y - 4 * Y * (z // 2)
     place = (Z - 1 - z, z)
     onward = (dp - Y, dp + Y)
     back = (dp + Y, dp - Y)
 
     barrier = pltpu.get_barrier_semaphore()
-    pl.semaphore_signal(barrier, inc=1, device_id={'dp': mate}, device_id_type=MESH)
+    signal(barrier, dp=mate)
+    signal(barrier, dp=z_far)
     for other in (partner, beside, across):
-        pl.semaphore_signal(barrier, inc=1, device_id={'tp': other}, device_id_type=MESH)
+        signal(barrier, tp=other)
 
     @pl.when(z > 0)
     def _():
-        pl.semaphore_signal(barrier, inc=1, device_id={'dp': dp - Y}, device_id_type=MESH)
+        signal(barrier, dp=dp - Y)
 
     @pl.when(z < Z - 1)
     def _():
-        pl.semaphore_signal(barrier, inc=1, device_id={'dp': dp + Y}, device_id_type=MESH)
+        signal(barrier, dp=dp + Y)
 
     inner = jnp.where((z > 0) & (z < Z - 1), 1, 0)
 
@@ -129,16 +429,14 @@
         for h in range(2):
             part_copy(h, u).wait()
 
-    def compute(u):
+    def compute_main(u):
         for h in range(2):
             rows_copy(h, u).wait()
-        more_copy(u).wait()
 
         @pl.when(u + 1 < chunks)
         def _():
             for h in range(2):
                 rows_copy(h, u + 1).start()
-            more_copy(u + 1).start()
 
         slot = u % 2
         mine = y * half + u * size + steps_in_unit
@@ -166,6 +464,14 @@
         for h in range(2):
             part_copy(h, u).start()
 
+    def compute_more(u):
+        more_copy(u).wait()
+
+        @pl.when(u + 1 < chunks)
+        def _():
+            more_copy(u + 1).start()
+
+        slot = u % 2
         theirs = (1 - y) * half + u * unit + steps_in_unit
 
         def more_tile(t, carry):
@@ -256,11 +562,11 @@
 
     def share_copy(i, other):
         return pltpu.make_async_remote_copy(
-            src_ref=dx_q, dst_ref=dx.at[tp], send_sem=share_send.at[i], recv_sem=share_recv.at[i],
+            src_ref=dx_q, dst_ref=dh.at[tp], send_sem=share_send.at[i], recv_sem=share_recv.at[i],
             device_id={'tp': other}, device_id_type=MESH)
 
     def keep_copy():
-        return pltpu.make_async_copy(dx_q, dx.at[tp], share_send.at[3])
+        return pltpu.make_async_copy(dx_q, dh.at[tp], share_send.at[3])
 
     others = (partner, beside, across)
     block = 128
@@ -288,9 +594,45 @@
         for i in range(width // block):
             at = pl.ds(i * block, block)
             dx_q[:, at] = dx_t[tp, at].T
+
+        levels[0] = jnp.zeros(levels.shape[1:], jnp.float32)
+        own_loss = weight[:, :own] * lse[:, :own] * (1.0 / n_tp) - weight[:, :own] * target[:, :own]
+        loss_part = own_loss - weight[:, own:] * target[:, own:]
+        levels[0, 2:3] = sum(loss_part[:, i * width:(i + 1) * width] for i in range(own // width))
+        count_block = min(64, quarter)
+
+        def token_block(i, carry):
+            at = pl.ds(pl.multiple_of(i * count_block, count_block), count_block)
+            grad = dx_q[at, :]
+            x_hat = hat[at, :]
+            levels[0, 0:1] = levels[0, 0:1] + jnp.sum(grad * x_hat, axis=0, keepdims=True)
+            levels[0, 1:2] = levels[0, 1:2] + jnp.sum(grad, axis=0, keepdims=True)
+            grad_hat = grad * gain[...]
+            mean_grad = jnp.mean(grad_hat, axis=-1, keepdims=True)
+            mean_proj = jnp.mean(grad_hat * x_hat, axis=-1, keepdims=True)
+            dx_q[at, :] = inv[at, 0:1] * (grad_hat - mean_grad - x_hat * mean_proj)
+            return carry
+
+        lax.fori_loop(0, quarter // count_block, token_block, 0)
+        level_copy(0).start()
         for i, other in enumerate(others):
             share_copy(i, other).start()
         keep_copy().start()
+
+    level_peers = ({'tp': beside}, {'tp': partner}, {'dp': mate}, {'dp': z_mate}, {'dp': z_far})
+
+    def level_copy(i):
+        return pltpu.make_async_remote_copy(
+            src_ref=levels.at[i], dst_ref=arrived.at[i], send_sem=level_sem.at[0, i], recv_sem=level_sem.at[1, i],
+            device_id=level_peers[i], device_id_type=MESH)
+
+    def level_next(i):
+        level_copy(i).wait_recv()
+        if i + 1 < len(level_peers):
+            levels[i + 1] = levels[i] + arrived[i]
+            level_copy(i + 1).start()
+        else:
+            sums[...] = levels[i] + arrived[i]
 
     def dx_end():
         for i in range(2):
@@ -299,62 +641,61 @@
         for i, other in enumerate(others):
             share_copy(i, other).wait()
         keep_copy().wait()
+        for i in range(len(level_peers)):
+            level_copy(i).wait_send()
 
     for h in range(2):
         rows_copy(h, 0).start()
     more_copy(0).start()
     target[...] = jnp.zeros_like(target)
+    scale[...] = weight[...] / count[0:1, 0:1]
 
     def clear(t, carry):
         dx_t[t] = jnp.zeros(dx_t.shape[1:], jnp.float32)
         return carry
 
     lax.fori_loop(0, own // TILE, clear, 0)
-    pl.semaphore_wait(barrier, 5 + inner)
-
-    done = last_tick(chunks)
+    pl.semaphore_wait(barrier, 6 + inner)
+
+    done = max(last_more(chunks), last_main(chunks))
     ticks = 1 + 2 * (chunks + 2 * (Z - 1))
-    assert done + 9 < ticks
+    assert done + 18 < ticks
 
     def tick(i, carry):
-        k = i // 2
-        odd = i % 2 == 1
         earlier = jnp.maximum(i - 1, 1)
 
         @pl.when(i == 1)
         def _():
             settle(0)
 
-        @pl.when(odd)
-        def _():
-            reduce_phase(k)
+        @pl.when(i % 2 == 1)
+        def _():
+            reduce_phase(i // 2)
 
         @pl.when((i > 0) & (i % 2 == 0))
         def _():
-            spread_phase(k - 1)
-
-        @pl.when((i > 1) & has_unit(earlier, chunks))
-        def _():
-            settle(unit_at(earlier))
-
-        @pl.when((i == 0) | has_unit(i, chunks))
-        def _():
-            compute(jnp.where(i == 0, 0, unit_at(i)))
-
-        @pl.when(i == done + 1)
-        def _():
-            dx_start()
-
-        @pl.when(i == done + 2)
-        def _():
-            dx_middle()
-
-        @pl.when(i == done + 9)
-        def _():
-            dx_finish()
+            spread_phase(i // 2 - 1)
+
+        @pl.when((i > 1) & has_main(earlier, chunks))
+        def _():
+            settle(main_unit(earlier))
+
+        @pl.when((i == 0) | has_main(i, chunks))
+        def _():
+            compute_main(jnp.where(i == 0, 0, main_unit(i)))
+
+        @pl.when(has_more(i, chunks))
+        def _():
+            compute_more(more_unit(i, chunks))
+
+        events = ((1, dx_start), (2, dx_middle), (8, dx_finish), (9, lambda: level_next(0)), (10, lambda: level_next(1)),
+                  (14, lambda: level_next(2)), (17, lambda: level_next(3)))
+        for after, event in events:
+            pl.when(i == done + after)(event)
         return carry
 
     lax.fori_loop(0, ticks, tick, 0)
+    level_next(4)
 
     for h in range(2):
         p = place[h]
@@ -375,7 +716,7 @@
     dx_end()
 
 
-def backward(table, x, x_t, lse, scale, label, n_tp, chunks):
+def backward(table, x, x_t, lse, weight, label, count, hat, inv, gain, n_tp, chunks):
     shard, width = table.shape
     half = shard // Y
     size = half // (2 * chunks)
@@ -393,8 +734,8 @@
             jax.ShapeDtypeStruct((shard, width), f32),
             jax.ShapeDtypeStruct((half, width), f32),
             jax.ShapeDtypeStruct((n_tp, quarter, width), f32),
-            jax.ShapeDtypeStruct((1, tokens), f32)),
-        in_specs=[hbm, vmem, vmem, vmem, vmem, vmem],
+            jax.ShapeDtypeStruct((8, width), f32)),
+        in_specs=[hbm] + [vmem] * 9,
         out_specs=(hbm, hbm, hbm, vmem),
         scratch_shapes=[
             pltpu.VMEM((2, SLOTS, size, width), f32),
@@ -407,86 +748,43 @@
             pltpu.VMEM((2, width, quarter), f32),
             pltpu.VMEM((width, quarter), f32),
             pltpu.VMEM((quarter, width), f32),
+            pltpu.VMEM((1, tokens), f32), pltpu.VMEM((1, tokens), f32),
+            pltpu.VMEM((5, 8, width), f32), pltpu.VMEM((5, 8, width), f32),
             dma((2, SLOTS)), dma((2, SLOTS)), pltpu.SemaphoreType.REGULAR((2,)),
             dma((2,)), dma((2, chunks)),
             dma((2,)), dma((2,)),
             dma((2, 2)), dma((2,)), dma((2,)), dma((2, 2)), dma((2,)),
-            dma((2, 2)), dma((2,)), dma((4,)), dma((3,)),
+            dma((2, 2)), dma((2,)), dma((4,)), dma((3,)), dma((2, 5)),
         ],
         compiler_params=pltpu.CompilerParams(
             collective_id=0, has_side_effects=True, vmem_limit_bytes=62 * 1024 * 1024),
         cost_estimate=pl.CostEstimate(flops=flops, bytes_accessed=12 * half * width, transcendentals=half * tokens),
-    )(table, x, x_t, lse, scale, label)
-
-
-def norm_stats(hidden):
-    h32 = hidden.astype(jnp.float32)
-    mean = jnp.mean(h32, axis=-1, keepdims=True)
-    centred = h32 - mean
-    variance = jnp.mean(centred * centred, axis=-1, keepdims=True)
-    inv_std = lax.rsqrt(variance + LN_EPS)
-    return centred * inv_std, inv_std
-
-
-def norm_backward(grad_x, x_hat, inv_std, ln_gain):
-    grad_hat = grad_x * ln_gain.astype(jnp.float32)
-    mean_grad = jnp.mean(grad_hat, axis=-1, keepdims=True)
-    mean_proj = jnp.mean(grad_hat * x_hat, axis=-1, keepdims=True)
-    return (inv_std * (grad_hat - mean_grad - x_hat * mean_proj)).astype(jnp.bfloat16)
+    )(table, x, x_t, lse, weight, label, count, hat, inv, gain)
 
 
 def solution(mesh):
     n_dp = mesh.shape['dp']
     n_tp = mesh.shape['tp']
     to_mate = [(i, i ^ 1) for i in range(n_dp)]
-    to_core = [(i, i ^ 1) for i in range(n_tp)]
 
     def device_step(hidden, table, labels, loss_mask, ln_gain, ln_bias):
         batch, seq, width = hidden.shape
         tokens = batch * seq
         shard = table.shape[0]
         tp = lax.axis_index('tp')
-        core = tp % 2
-        gain = ln_gain.astype(jnp.float32)
-        bias = ln_bias.astype(jnp.float32)
-
-        x_hat, inv_std = norm_stats(hidden.reshape(tokens, width))
-        piece = lax.dynamic_slice(x_hat, (core * (tokens // 2), 0), (tokens // 2, width))
-        got = lax.ppermute(piece, 'dp', to_mate)
-        got2 = lax.ppermute(got, 'tp', to_core)
+        gain = ln_gain.astype(jnp.float32)[None]
+        bias = ln_bias.astype(jnp.float32)[None]
+
         ids = jnp.stack([labels.reshape(tokens), loss_mask.reshape(tokens)])
-        ids_mate = lax.ppermute(ids, 'dp', to_mate)
-
-        x = (x_hat * gain + bias).astype(jnp.bfloat16)
-        logits = lax.dot_general(x, table, (((1,), (1,)), ((), ())), preferred_element_type=jnp.float32)
-        row_ids = tp * shard + lax.broadcasted_iota(jnp.int32, (1, shard), 1)
-        logits = jnp.where(row_ids < VOCAB, logits, -jnp.inf)
-        top = jnp.maximum(jnp.max(logits, axis=-1), jnp.finfo(jnp.float32).min)
-        exp_sum = jnp.sum(jnp.exp(logits - top[:, None]), axis=-1)
-        stats = lax.all_gather(jnp.stack([top, exp_sum]), 'tp')
-        best = jnp.max(stats[:, 0], axis=0)
-        log_norm = best + jnp.log(jnp.sum(stats[:, 1] * jnp.exp(stats[:, 0] - best), axis=0))
-        norm_mate = lax.ppermute(log_norm, 'dp', to_mate)
-
-        mask = loss_mask.reshape(tokens).astype(jnp.float32)
-        count = lax.psum(jnp.sum(mask), 'dp')
-
-        first = jnp.where(core == 0, got, got2)
-        second = jnp.where(core == 0, got2, got)
-        x_mate = (jnp.concatenate([first, second]) * gain + bias).astype(jnp.bfloat16)
-        x_all = jnp.concatenate([x, x_mate])
-        lse = jnp.concatenate([log_norm, norm_mate])[None]
-        label = jnp.concatenate([ids[0], ids_mate[0]])[None] - tp * shard
-        weight = jnp.concatenate([mask, ids_mate[1].astype(jnp.float32)])[None]
-
-        grad_table, _, grad_x, target = backward(table, x_all, x_all.T, lse, weight / count, label, n_tp, CHUNKS)
-
-        grad_x = grad_x.reshape(tokens, width)
-        grad_hidden = norm_backward(grad_x, x_hat, inv_std, ln_gain).reshape(batch, seq, width)
-        sums = jnp.stack([jnp.sum(grad_x * x_hat, axis=0), jnp.sum(grad_x, axis=0)])
-        lost = jnp.sum(mask * log_norm) / n_tp - jnp.sum(weight * target)
-        sums, lost = lax.psum((sums / n_tp, lost), ('dp', 'tp'))
-        return lost / count, grad_hidden, grad_table, sums[0], sums[1]
+        ids_all = jnp.concatenate([ids, lax.ppermute(ids, 'dp', to_mate)], axis=1)
+        label = ids_all[0:1] - tp * shard
+        weight = ids_all[1:2].astype(jnp.float32)
+        mask = loss_mask.reshape(1, tokens).astype(jnp.float32)
+
+        x, x_t, lse, count, hat, inv = forward(table, hidden.reshape(tokens, width), gain, bias, mask, n_dp, n_tp)
+        grad_table, _, grad_hidden, sums = backward(table, x, x_t, lse, weight, label, count, hat, inv, gain, n_tp, CHUNKS)
+        return (jnp.sum(sums[2]) / count[0, 0], grad_hidden.reshape(batch, seq, width).astype(jnp.bfloat16), grad_table,
+                sums[0], sums[1])
 
     specs_in = (P('dp', None, None), P('tp', None), P('dp', None), P('dp', None), P(None), P(None))
     specs_out = (P(), P('dp', None, None), P('tp', None), P(None), P(None))

time: 1000 us -> 830 us (0.83)
  Pallas kernels: 687 us -> 772 us
  other arithmetic: 82.7 us -> 12 us
  blocking collectives: 67.9 us -> 0 us
  matrix products: 65.6 us -> 0 us
  waiting for transfers between devices: 26.7 us -> 0.01 us
  local copies, waits for them, and re-layouts: 63.1 us -> 37.7 us
    pallas_call x0 -> x1, Pallas kernels: none -> 118 us  [forward(): pl.pallas_call(functools.partial(forward_kernel, n_dp, n_tp), out_shape=(...]
    dot_general x1 -> x0, matrix products: 65.6 us -> none  [device_step(): lax.dot_general(x, table, (((1,), (1,)), ((), ())), preferred_element_typ...]
    psum x2 -> x0, blocking collectives: 62.7 us -> none  [the longest x1 40.2 us: device_step(): sums, lost = lax.psum((sums / n_tp, lost), ('dp', 'tp'))]
    reduce_sum x7 -> x0, other arithmetic: 47.9 us -> none  [the longest x1 32.3 us: device_step(): exp_sum = jnp.sum(jnp.exp(logits - top[:, None]), axis=-1)]
    pallas_call x1, Pallas kernels: 687 us -> 654 us  [backward(): pl.pallas_call(functools.partial(backward_kernel, chunks), out_shape=(jax...]
    ppermute x4 -> x1, waiting for transfers between devices: 26.7 us -> 0.01 us  [device_step(): ids_all = jnp.concatenate([ids, lax.ppermute(ids, 'dp', to_mate)], axis=1)]
    convert_element_type x6 -> x2, other arithmetic: 20.6 us -> 6.67 us  [the longest x1 6.06 us: device_step(): grad_hidden.reshape(batch, seq, width).astype(jnp.bfloat16)]
    concatenate x1 -> x0, local copies, waits for them, and re-layouts: 11.9 us -> none  [device_step(): x_all = jnp.concatenate([x, x_mate])]
  transfers between devices with their start and end apart: 4 -> 1, of which waited for: 1 -> 0; matrix products, arithmetic and copies ran while one was open for 13% -> 1% of each run, Pallas kernels for 0% -> 14%
where the time goes in v3:
time: 830 us; the launch traced here: 828 us
  Pallas kernels  772 us (93%)
  local copies, waits for them, and re-layouts  37.7 us (5%)
  other arithmetic  12 us (1%)
    pallas_call x1, Pallas kernels, backward(): pl.pallas_call(functools.partial(backward_kernel, chunks), out_shape=(jax...  654 us
    pallas_call x1, Pallas kernels, forward(): pl.pallas_call(functools.partial(forward_kernel, n_dp, n_tp), out_shape=(...  118 us
    unnamed x3, local copies, waits for them, and re-layouts  36.5 us
  transfers between devices with their start and end apart: 1, of which 0 were waited for; matrix products, arithmetic and copies ran while one was open for 1% of the time, Pallas kernels for 14%

profile of v3, /device:TPU:0, one launch (start us, length us, event | category | flops | bytes accessed | tf_op | source)
XLA Modules:
  0.0 828.2 jit_solution(5719781659480791078)
XLA Ops:
  0.6 0.7 copy.12
  1.3 0.7 copy.11
  2.1 3.1 collective-permute-start
  5.1 0.6 convert_element_type.14.mask
  5.7 1.3 broadcast_in_dim.14
  7.0 1.3 broadcast_in_dim.15
  8.3 118.2 %shard_map.101 = (bf16[4096,1024]{1,0:T(8,128)(2,1)}, bf16[1024,4096]{1,0:T(8,128)(2,1)}, f32[1,4096]{1,0:T(1,128)}, f32[8,128]{1,0:T(8,128)}, f32[512,1024]{1,0:T(8,128)}, /*index=5*/f32[512,128]{1,0:T(8,128)}) custom-call(bf16[12672,1024]{1,0:T(8,128)(2,1)} %table.3, bf16[2048,1024]{1,0:T(8,128)(2,1)} %bitcast.26, f32[1,1024]{1,0:T(1,128)} %bitcast.21, ...), custom_call_target="tpu_custom_call" | custom-call | flops 53150220288 | bytes 25952256 | tf_op jit(solution)/shard_map/pallas_call | solution.py:270
  126.5 1.2 slice.21
  127.7 0.0 collective-permute-done
  127.7 0.6 slice_subtract_fusion
  128.4 654.2 %shard_map.102 = (f32[12672,1024]{1,0:T(8,128)}, f32[6336,1024]{1,0:T(8,128)}, f32[4,512,1024]{2,1,0:T(8,128)}, f32[8,1024]{1,0:T(8,128)}) custom-call(bf16[12672,1024]{1,0:T(8,128)(2,1)} %table.3, bf16[4096,1024]{1,0:T(8,128)(2,1)} %get-tuple-element.14.x, bf16[1024,4096]{1,0:T(8,128)(2,1)} %get-tuple-element.15.x_t, f32[1,4096]{1,0:T(1,128)} %get-tuple-element.16.lse, ...), custom_call_target="tpu_custom_call" | custom-call | flops 186025771008 | bytes 77856768 | tf_op jit(solution)/shard_map/pallas_call | solution.py:731
  782.6 2.1 fusion
  784.7 6.1 convert_element_type.16
  792.0 35.1 %copy.14 = f32[12672,1024]{1,0:T(8,128)} copy(f32[12672,1024]{1,0:T(8,128)} %get-tuple-element.35) | data formatting | bytes 103809024
  (2 shorter events, 0.0 us)
Async XLA Ops:
  2.1 125.6 %collective-permute-start = (s32[2,2048]{1,0:T(2,128)S(1)}, s32[2,2048]{1,0:T(2,128)S(1)}, u32[]{:S(2)}, u32[]{:S(2)}) collective-permute-start(s32[2,2048]{1,0:T(2,128)S(1)} %pad_add_fusion.1), channel_id=1, source_target_pairs={{0,4},{4,0},{8,12},{12,8},{16,20},{20,16},{24,28},{28,24},{1,5},{5... | collective-permute-start | bytes 49160 | tf_op jit(solution)/shard_map/ppermute | solution.py:779

commit v4 on v0

v4 whole, which is shorter than its diff:
```python
import functools

import jax
import jax.numpy as jnp
from jax import lax
from jax.experimental import pallas as pl
from jax.experimental.pallas import tpu as pltpu
from jax.sharding import PartitionSpec as P

LN_EPS = 1e-5
VOCAB = 50257
Z = 4
Y = 2
UNITS = 33
PER_UNIT = 2
SLOTS = 12
TILE = 512
PIECES = 4
FORWARD_ROWS = 384
COLUMNS = 256
VMEM_BYTES = 67043328
MESH = pl.DeviceIdType.MESH


def signal(barrier, **where):
    pl.semaphore_signal(barrier, inc=1, device_id=where, device_id_type=MESH)


def remote(src, dst, send_sem, recv_sem, **where):
    return pltpu.make_async_remote_copy(
        src_ref=src, dst_ref=dst, send_sem=send_sem, recv_sem=recv_sem, device_id=where, device_id_type=MESH)


def neighbours(tp):
    core = tp % 2
    partner = tp + 1 - 2 * core
    beside = tp + 2 - 4 * (tp // 2)
    return partner, beside, beside + 1 - 2 * core


def tile_at(t):
    return slice(t * TILE, (t + 1) * TILE)


def aligned(start, size):
    return pl.ds(pl.multiple_of(start, size), size)


def head_kernel(
        n_dp, n_tp, table, hidden, gain, bias, labels, loss_mask,
        out, part, dh, sums,
        x, x_t, lse, scale, weight, label, target, hat, inv, send_q,
        got, block_buf, top, total, stats, counts, ids,
        red, loc, q_t, rows_buf, more_buf, stage, dx_t, from_core, from_x, levels, arrived,
        hidden_sem, block_sem, y_sem, beside_sem, core_sem, relay_sem, stat_send, stat_recv, count_send, count_recv,
        ids_sem,
        red_send, red_recv, credit, bc_send, bc_recv, mate_send, mate_recv, loc_sem, own_sem, part_sem, rows_sem, more_sem,
        swap_sem, cross_sem, share_send, share_recv, level_sem):
    own, width = hidden.shape
    tokens = Y * own
    shard = table.shape[0]
    half = shard // Y
    quarter = own // n_tp
    piece = quarter // PIECES
    batch, seq = labels.shape
    size = red.shape[2]
    chunks = half // (2 * size)
    strip = size * PER_UNIT
    units = chunks // PER_UNIT
    unit = 2 * strip
    block_rows = block_buf.shape[1]
    blocks = shard // block_rows
    last = PIECES - 1

    dp = lax.axis_index('dp')
    tp = lax.axis_index('tp')
    y = dp % Y
    z = dp // Y
    core = tp % 2
    mate = dp + 1 - 2 * y
    partner, beside, across = neighbours(tp)
    others = (partner, beside, across)
    dp_others = [lax.rem(dp + j, n_dp) for j in range(1, n_dp)]
    z_mate = dp + Y - 2 * Y * (z % 2)
    z_far = dp + 2 * Y - 4 * Y * (z // 2)
    place = (Z - 1 - z, z)
    onward = (dp - Y, dp + Y)
    back = (dp + Y, dp - Y)
    first_row = tp * shard

    barrier = pltpu.get_barrier_semaphore()
    for other in dp_others:
        signal(barrier, dp=other)
    for other in others:
        signal(barrier, tp=other)
        signal(barrier, dp=mate, tp=other)

    def hidden_copy(j):
        q = lax.rem(tp + j, n_tp)
        at = aligned(q * quarter, quarter)
        return pltpu.make_async_copy(hidden.at[at], x.at[at], hidden_sem.at[j])

    def block_copy(b):
        return pltpu.make_async_copy(
            table.at[pl.ds(b * block_rows, block_rows)], block_buf.at[b % 2], block_sem.at[b % 2])

    def got_piece(q, k):
        return got.at[q, pl.ds(k * piece, piece)]

    def y_copy(k):
        return remote(send_q.at[pl.ds(k * piece, piece)], got_piece(tp, k), y_sem.at[0, k], y_sem.at[1, k], dp=mate)

    def beside_copy(k):
        return remote(got_piece(tp, k), got_piece(tp, k), beside_sem.at[0, k], beside_sem.at[1, k], tp=beside)

    def core_copy(k):
        return remote(got_piece(tp, k), got_piece(tp, k), core_sem.at[0, k], core_sem.at[1, k], tp=partner)

    def relay_copy(k):
        return remote(got_piece(beside, k), got_piece(beside, k), relay_sem.at[0, k], relay_sem.at[1, k], tp=partner)

    def count_copy(j):
        return remote(counts.at[dp], counts.at[dp], count_send.at[j], count_recv.at[dp], dp=dp_others[j])

    def count_arrival(j):
        other = dp_others[j]
        return remote(counts.at[other], counts.at[other], count_send.at[j], count_recv.at[other], dp=other)

    def ids_copy(i):
        return remote((labels, loss_mask)[i], ids.at[i], ids_sem.at[0, i], ids_sem.at[1, i], dp=mate)

    def block_of(q, k):
        return aligned(q * quarter + k * piece, piece)

    def normalize(at):
        h = x[at, :].astype(jnp.float32)
        mean = jnp.mean(h, axis=-1, keepdims=True)
        centred = h - mean
        variance = jnp.mean(centred * centred, axis=-1, keepdims=True)
        inv_std = lax.rsqrt(variance + LN_EPS)
        x_hat = centred * inv_std
        normed = (x_hat * gain[...].astype(jnp.float32) + bias[...].astype(jnp.float32)).astype(jnp.bfloat16)
        wide = normed.astype(jnp.float32)
        x[at, :] = normed
        x_t[:, at] = wide.T.astype(jnp.bfloat16)
        return x_hat, inv_std, wide

    def first_piece(k, carry):
        x_hat, inv_std, wide = normalize(block_of(tp, k))
        at = aligned(k * piece, piece)
        send_q[at, :] = wide
        hat[at, :] = x_hat
        inv[at, :] = jnp.broadcast_to(inv_std, (piece, inv.shape[1]))

        @pl.when(k == 0)
        def _():
            pl.semaphore_wait(barrier, n_dp - 1 + 2 * len(others))
        y_copy(k).start()
        return carry

    def next_piece(j, carry):
        k = j % PIECES

        @pl.when(k == 0)
        def _():
            hidden_copy(1 + j // PIECES).wait()
        normalize(block_of(lax.rem(tp + 1 + j // PIECES, n_tp), k))
        return carry

    def convert(q, k):
        wide = got[q, aligned(k * piece, piece)]
        at = aligned(own + q * quarter + k * piece, piece)
        x[at, :] = wide.astype(jnp.bfloat16)
        x_t[:, at] = wide.T.astype(jnp.bfloat16)

    def block(b, carry):
        block_copy(b).wait()

        @pl.when(b + 1 < blocks)
        def _():
            block_copy(b + 1).start()

        phase = b % 6

        @pl.when((phase == 0) & (b > 0) & (b <= 6 * PIECES))
        def _():
            k = jnp.maximum(b // 6 - 1, 0)
            y_copy(k).wait_recv()
            beside_copy(k).start()
            core_copy(k).start()
            convert(tp, k)

        @pl.when((phase == 2) & (b >= 14) & (b < 14 + 6 * PIECES))
        def _():
            k = jnp.maximum(b - 14, 0) // 6
            beside_copy(k).wait_recv()
            relay_copy(k).start()
            convert(beside, k)

        @pl.when((phase == 4) & (b >= 10) & (b < 10 + 6 * PIECES))
        def _():
            k = jnp.maximum(b - 10, 0) // 6
            core_copy(k).wait_recv()
            convert(partner, k)

        @pl.when((phase == 4) & (b >= 16) & (b < 10 + 6 * PIECES))
        def _():
            k = jnp.maximum(b - 16, 0) // 6
            relay_copy(k).wait_recv()
            convert(across, k)

        slot = b % 2
        row_ids = first_row + b * block_rows + lax.broadcasted_iota(jnp.int32, (block_rows, 1), 0)
        for t in range(own // TILE):
            at = tile_at(t)
            logits = jnp.dot(block_buf[slot], x_t[:, at], preferred_element_type=jnp.float32)
            logits = jnp.where(row_ids < VOCAB, logits, -jnp.inf).reshape(block_rows // 8, 8, TILE)
            before = top[:, at]
            now = jnp.maximum(before, jnp.max(logits, axis=0))
            total[:, at] = total[:, at] * jnp.exp(before - now) + jnp.sum(jnp.exp(logits - now[None]), axis=0)
            top[:, at] = now
        return carry

    def stat_copies():
        where = [{'tp': other} for other in others] + [{'dp': mate}] + [{'dp': mate, 'tp': other} for other in others]
        return [remote(stats.at[0, tp], stats.at[int(i >= n_tp - 1), tp], stat_send.at[i], stat_recv.at[int(i >= n_tp - 1), tp],
                       **w) for i, w in enumerate(where)]

    def stat_arrival(side, other):
        return remote(stats.at[side, other], stats.at[side, other], stat_send.at[0], stat_recv.at[side, other], tp=partner)

    def part_rows(h, c):
        return part.at[pl.ds(h * (half // 2) + c * size, size)]

    def out_rows(side, h, c):
        return out.at[pl.ds(side * half + h * (half // 2) + c * size, size)]

    def fetch(h, c):
        return pltpu.make_async_copy(part_rows(h, c), loc.at[h, c % 2], loc_sem.at[h, c % 2])

    def reduce_copy(h, c, src):
        slot = c % SLOTS
        return remote(src, red.at[h, slot], red_send.at[h, slot], red_recv.at[h, slot], dp=onward[h])

    def spread_copy(h, c):
        return remote(out_rows(y, h, c), out_rows(y, h, c), bc_send.at[h], bc_recv.at[h, c], dp=back[h])

    def mate_copy(h, c):
        return remote(out_rows(y, h, c), out_rows(y, h, c), mate_send.at[h], mate_recv.at[h], dp=mate)

    def own_copy(h, c):
        return pltpu.make_async_copy(red.at[h, c % SLOTS], out_rows(y, h, c), own_sem.at[h])

    def rows_copy(h, u):
        return pltpu.make_async_copy(
            table.at[pl.ds(y * half + h * (half // 2) + u * strip, strip)],
            rows_buf.at[u % 2, pl.ds(h * strip, strip)], rows_sem.at[u % 2, h])

    def more_copy(u):
        return pltpu.make_async_copy(
            table.at[pl.ds((1 - y) * half + u * unit, unit)], more_buf.at[u % 2], more_sem.at[u % 2])

    def part_copy(h, u):
        return pltpu.make_async_copy(
            stage.at[pl.ds(h * strip, strip)], part.at[pl.ds(h * (half // 2) + u * strip, strip)], part_sem.at[h])

    unit_iota = lax.broadcasted_iota(jnp.int32, (unit, 1), 0)

    def grads(table_rows, row_ids, at):
        logits = jnp.dot(table_rows, x_t[:, at], preferred_element_type=jnp.float32)
        hit = row_ids == label[:, at]
        probs = jnp.where(row_ids + first_row < VOCAB, jnp.exp(logits - lse[:, at]), 0.0)
        q = ((probs - jnp.where(hit, 1.0, 0.0)) * scale[:, at]).astype(jnp.bfloat16)
        return q, jnp.where(hit, logits, 0.0)

    def add_dx(table_rows, q, t):
        dx_t[t] = dx_t[t] + lax.dot_general(
            table_rows, q, (((0,), (0,)), ((), ())), preferred_element_type=jnp.float32)

    def main_tile(u, t):
        slot = u % 2
        at = tile_at(t)
        mine = y * half + u * strip + unit_iota
        row_ids = jnp.where(unit_iota < strip, mine, mine + (half // 2 - strip))
        q, hits = grads(rows_buf[slot], row_ids, at)
        q_t[:, at] = q
        target[:, at] = target[:, at] + jnp.sum(hits, axis=0, keepdims=True)
        if t < own // TILE:
            add_dx(rows_buf[slot], q, t)

    def compute_own(u):
        for h in range(2):
            rows_copy(h, u).wait()

        @pl.when(u + 1 < units)
        def _():
            for h in range(2):
                rows_copy(h, u + 1).start()

        for t in range(own // TILE):
            main_tile(u, t)

    def compute_table(u):
        for t in range(own // TILE, tokens // TILE):
            main_tile(u, t)
        for n in range(width // COLUMNS):
            at = slice(n * COLUMNS, (n + 1) * COLUMNS)
            stage[:, at] = jnp.dot(q_t[...], x[:, at], preferred_element_type=jnp.float32)
        for h in range(2):
            part_copy(h, u).start()

    def compute_more(u):
        more_copy(u).wait()

        @pl.when(u + 1 < units)
        def _():
            more_copy(u + 1).start()

        slot = u % 2
        theirs = (1 - y) * half + u * unit + unit_iota
        for t in range(own // TILE):
            q, _ = grads(more_buf[slot], theirs, tile_at(t))
            add_dx(more_buf[slot], q, t)

    def settle(u):
        for h in range(2):
            part_copy(h, u).wait()

    def send_reduced(h, c, src):
        @pl.when(c >= SLOTS)
        def _():
            pl.semaphore_wait(credit.at[h], 1)
        reduce_copy(h, c, src).start()

    def free_slot(h, c):
        @pl.when(c + SLOTS < chunks)
        def _():
            pl.semaphore_signal(credit.at[h], inc=1, device_id={'dp': back[h]}, device_id_type=MESH)

    def reduce_phase(s):
        for h in range(2):
            p = place[h]
            c = s - p
            here = (c >= 0) & (c < chunks)

            @pl.when(here & (p == 0))
            def _():
                @pl.when(c >= 2)
                def _():
                    reduce_copy(h, c - 2, part_rows(h, c - 2)).wait_send()
                send_reduced(h, c, part_rows(h, c))

            @pl.when(here & (p > 0))
            def _():
                slot = c % SLOTS
                reduce_copy(h, c, red.at[h, slot]).wait_recv()
                fetch(h, c).wait()
                red[h, slot] = red[h, slot] + loc[h, c % 2]

                @pl.when(p < Z - 1)
                def _():
                    @pl.when(c >= 2)
                    def _():
                        reduce_copy(h, c - 2, red.at[h, (c - 2) % SLOTS]).wait_send()
                        free_slot(h, c - 2)
                    send_reduced(h, c, red.at[h, slot])

                @pl.when(p == Z - 1)
                def _():
                    own_copy(h, c).start()

            @pl.when((p > 0) & (c >= -1) & (c + 1 < chunks))
            def _():
                fetch(h, c + 1).start()

    def spread_phase(s):
        for h in range(2):
            p = place[h]
            c = s - 2 * (Z - 1) + p

            @pl.when((c >= 0) & (c < chunks))
            def _():
                @pl.when(p == Z - 1)
                def _():
                    own_copy(h, c).wait()
                    free_slot(h, c)

                @pl.when(p < Z - 1)
                def _():
                    spread_copy(h, c).wait_recv()

                @pl.when(p > 0)
                def _():
                    spread_copy(h, c).start()

                mate_copy(h, c).start()

    def swap_copy(i):
        return remote(dx_t.at[2 * i + 1 - core], from_core.at[i], swap_sem.at[0, i], swap_sem.at[1, i], tp=partner)

    def cross_copy():
        return remote(dx_t.at[beside], from_x, cross_sem.at[0], cross_sem.at[1], tp=beside)

    def share_copy(i):
        return remote(send_q, dh.at[tp], share_send.at[i], share_recv.at[i], tp=others[i])

    def keep_copy():
        return pltpu.make_async_copy(send_q, dh.at[tp], share_send.at[n_tp - 1])

    slab = 128

    def add_into(j, ref):
        def body(i, carry):
            at = aligned(i * slab, slab)
            dx_t[j, at] = dx_t[j, at] + ref[at]
            return carry
        lax.fori_loop(0, width // slab, body, 0)

    def dx_start():
        for i in range(2):
            swap_copy(i).start()

    def dx_middle():
        for i in range(2):
            swap_copy(i).wait_recv()
            add_into(2 * i + core, from_core.at[i])
        cross_copy().start()

    def dx_finish():
        cross_copy().wait_recv()
        add_into(tp, from_x)
        for i in range(width // slab):
            at = pl.ds(i * slab, slab)
            send_q[:, at] = dx_t[tp, at].T

        levels[0] = jnp.zeros(levels.shape[1:], jnp.float32)
        own_loss = weight[:, :own] * lse[:, :own] * (1.0 / n_tp) - weight[:, :own] * target[:, :own]
        loss_part = own_loss - weight[:, own:] * target[:, own:]
        levels[0, 2:3] = sum(loss_part[:, i * width:(i + 1) * width] for i in range(own // width))
        step = min(64, quarter)

        def token_block(i, carry):
            at = aligned(i * step, step)
            grad = send_q[at, :]
            x_hat = hat[at, :]
            levels[0, 0:1] = levels[0, 0:1] + jnp.sum(grad * x_hat, axis=0, keepdims=True)
            levels[0, 1:2] = levels[0, 1:2] + jnp.sum(grad, axis=0, keepdims=True)
            grad_hat = grad * gain[...].astype(jnp.float32)
            mean_grad = jnp.mean(grad_hat, axis=-1, keepdims=True)
            mean_proj = jnp.mean(grad_hat * x_hat, axis=-1, keepdims=True)
            send_q[at, :] = inv[at, 0:1] * (grad_hat - mean_grad - x_hat * mean_proj)
            return carry

        lax.fori_loop(0, quarter // step, token_block, 0)
        level_copy(0).start()
        for i in range(len(others)):
            share_copy(i).start()
        keep_copy().start()

    level_peers = ({'tp': beside}, {'tp': partner}, {'dp': mate}, {'dp': z_mate}, {'dp': z_far})

    def level_copy(i):
        return remote(levels.at[i], arrived.at[i], level_sem.at[0, i], level_sem.at[1, i], **level_peers[i])

    def level_next(i):
        level_copy(i).wait_recv()
        merged = levels[i] + arrived[i]
        if i + 1 < len(level_peers):
            levels[i + 1] = merged
            level_copy(i + 1).start()
        else:
            sums[...] = merged
            sums[2:3] = jnp.broadcast_to(jnp.sum(merged[2:3], axis=-1, keepdims=True) / tokens_counted(), (1, width))

    def tokens_counted():
        return sum(counts[j, 0:1, 0:1] for j in range(n_dp))

    for j in range(n_tp):
        hidden_copy(j).start()
    block_copy(0).start()
    for h in range(2):
        rows_copy(h, 0).start()
    more_copy(0).start()
    hidden_copy(0).wait()
    lax.fori_loop(0, PIECES, first_piece, 0)
    for i in range(2):
        ids_copy(i).start()
    counts[dp] = jnp.full(counts.shape[1:], jnp.sum(loss_mask[...].astype(jnp.float32)), jnp.float32)
    for j in range(n_dp - 1):
        count_copy(j).start()
    lax.fori_loop(0, (n_tp - 1) * PIECES, next_piece, 0)

    top[...] = jnp.full_like(top, jnp.finfo(jnp.float32).min)
    total[...] = jnp.zeros_like(total)
    target[...] = jnp.zeros_like(target)

    def clear(t, carry):
        dx_t[t] = jnp.zeros(dx_t.shape[1:], jnp.float32)
        return carry

    lax.fori_loop(0, own // TILE, clear, 0)
    assert blocks > 8 + 6 * PIECES
    lax.fori_loop(0, blocks, block, 0)

    best = jnp.max(top[...], axis=0, keepdims=True)
    stats[0, tp, 0:1] = best
    stats[0, tp, 1:2] = jnp.sum(total[...] * jnp.exp(top[...] - best), axis=0, keepdims=True)
    for copy in stat_copies():
        copy.start()

    relay_copy(last).wait_recv()
    convert(across, last)
    for i in range(2):
        ids_copy(i).wait()
    for j in range(n_dp - 1):
        count_arrival(j).wait_recv()
    for i in range(batch):
        for side, (rows_of, marks) in enumerate(((labels, loss_mask), (ids.at[0], ids.at[1]))):
            at = slice(side * own + i * seq, side * own + (i + 1) * seq)
            label[:, at] = rows_of[i:i + 1, :] - first_row
            weight[:, at] = marks[i:i + 1, :].astype(jnp.float32)
    scale[...] = weight[...] / tokens_counted()
    for k in range(PIECES):
        for copy in (y_copy(k), beside_copy(k), core_copy(k), relay_copy(k)):
            copy.wait_send()
    for j in range(n_dp - 1):
        count_copy(j).wait_send()
    for other in others:
        stat_arrival(0, other).wait_recv()
    for other in (tp,) + others:
        stat_arrival(1, other).wait_recv()
    for side in range(Y):
        tops = [stats[side, j, 0:1] for j in range(n_tp)]
        best = functools.reduce(jnp.maximum, tops)
        mass = sum(stats[side, j, 1:2] * jnp.exp(tops[j] - best) for j in range(n_tp))
        lse[:, side * own:(side + 1) * own] = best + jnp.log(mass)

    done = 3 * units - 1
    ticks = 2 + 2 * (chunks + 2 * (Z - 1))
    assert done + 36 < ticks

    def tick(i, carry):
        u = i // 3
        kind = i % 3

        @pl.when(i == 2)
        def _():
            settle(0)

        @pl.when((i >= 2) & (i % 2 == 0))
        def _():
            reduce_phase(jnp.maximum(i - 2, 0) // 2)

        @pl.when((i >= 2) & (i % 2 == 1))
        def _():
            spread_phase(jnp.maximum(i - 2, 0) // 2)

        @pl.when((i > 2) & (kind == 2) & (u < units))
        def _():
            settle(u)

        for j, compute in enumerate((compute_own, compute_table, compute_more)):
            pl.when((kind == j) & (u < units))(functools.partial(compute, u))

        events = ((1, dx_start), (4, dx_middle), (16, dx_finish), (18, lambda: level_next(0)), (20, lambda: level_next(1)),
                  (26, lambda: level_next(2)), (33, lambda: level_next(3)))
        for after, event in events:
            pl.when(i == done + after)(event)
        return carry

    lax.fori_loop(0, ticks, tick, 0)
    level_next(4)

    for h in range(2):
        p = place[h]
        mine = out.at[pl.ds(y * half + h * (half // 2), half // 2)]
        theirs = out.at[pl.ds((1 - y) * half + h * (half // 2), half // 2)]

        @pl.when(p < Z - 1)
        def _():
            for c in (chunks - 2, chunks - 1):
                reduce_copy(h, c, red.at[h, c % SLOTS]).wait_send()

        @pl.when(p > 0)
        def _():
            pltpu.make_async_copy(mine, mine, bc_send.at[h]).wait()

        pltpu.make_async_copy(mine, mine, mate_send.at[h]).wait()
        pltpu.make_async_copy(theirs, theirs, mate_recv.at[h]).wait()
    for copy in stat_copies():
        copy.wait_send()
    for i in range(2):
        swap_copy(i).wait_send()
    cross_copy().wait_send()
    for i in range(len(others)):
        share_copy(i).wait()
    keep_copy().wait()
    for i in range(len(level_peers)):
        level_copy(i).wait_send()


def head_step(table, hidden, gain, bias, labels, loss_mask, n_dp, n_tp):
    own, width = hidden.shape
    tokens = Y * own
    shard = table.shape[0]
    half = shard // Y
    size = half // (2 * UNITS * PER_UNIT)
    unit = 2 * size * PER_UNIT
    chunks = UNITS * PER_UNIT
    quarter = own // n_tp
    assert size * 2 * chunks == half and size % 8 == 0 and unit % 32 == 0 and quarter == TILE
    assert shard % FORWARD_ROWS == 0
    f32 = jnp.float32
    b16 = jnp.bfloat16
    i32 = jnp.int32
    lanes = 128
    dma = pltpu.SemaphoreType.DMA
    vmem = pl.BlockSpec(memory_space=pltpu.VMEM)
    hbm = pl.BlockSpec(memory_space=pl.ANY)
    flops = 2 * width * (own * shard + half * (2 * tokens + 3 * own))
    return pl.pallas_call(
        functools.partial(head_kernel, n_dp, n_tp),
        out_shape=(
            jax.ShapeDtypeStruct((shard, width), f32),
            jax.ShapeDtypeStruct((half, width), f32),
            jax.ShapeDtypeStruct((n_tp, quarter, width), f32),
            jax.ShapeDtypeStruct((8, width), f32)),
        in_specs=[hbm, hbm, vmem, vmem, vmem, vmem],
        out_specs=(hbm, hbm, hbm, vmem),
        scratch_shapes=[
            pltpu.VMEM((tokens, width), b16), pltpu.VMEM((width, tokens), b16),
            pltpu.VMEM((1, tokens), f32), pltpu.VMEM((1, tokens), f32), pltpu.VMEM((1, tokens), f32),
            pltpu.VMEM((1, tokens), i32), pltpu.VMEM((1, tokens), f32),
            pltpu.VMEM((quarter, width), f32), pltpu.VMEM((quarter, lanes), f32), pltpu.VMEM((quarter, width), f32),
            pltpu.VMEM((n_tp, quarter, width), f32), pltpu.VMEM((2, FORWARD_ROWS, width), b16),
            pltpu.VMEM((8, own), f32), pltpu.VMEM((8, own), f32),
            pltpu.VMEM((Y, n_tp, 2, own), f32), pltpu.VMEM((n_dp, 8, lanes), f32),
            pltpu.VMEM((2,) + labels.shape, i32),
            pltpu.VMEM((2, SLOTS, size, width), f32), pltpu.VMEM((2, 2, size, width), f32),
            pltpu.VMEM((unit, tokens), b16),
            pltpu.VMEM((2, unit, width), b16), pltpu.VMEM((2, unit, width), b16),
            pltpu.VMEM((unit, width), f32),
            pltpu.VMEM((n_tp, width, quarter), f32),
            pltpu.VMEM((2, width, quarter), f32), pltpu.VMEM((width, quarter), f32),
            pltpu.VMEM((5, 8, width), f32), pltpu.VMEM((5, 8, width), f32),
            dma((n_tp,)), dma((2,)), dma((2, PIECES)), dma((2, PIECES)), dma((2, PIECES)), dma((2, PIECES)),
            dma((2 * n_tp - 1,)), dma((Y, n_tp)), dma((n_dp - 1,)), dma((n_dp,)),
            dma((2, 2)),
            dma((2, SLOTS)), dma((2, SLOTS)), pltpu.SemaphoreType.REGULAR((2,)),
            dma((2,)), dma((2, chunks)), dma((2,)), dma((2,)),
            dma((2, 2)), dma((2,)), dma((2,)), dma((2, 2)), dma((2,)),
            dma((2, 2)), dma((2,)), dma((n_tp,)), dma((n_tp - 1,)), dma((2, 5)),
        ],
        compiler_params=pltpu.CompilerParams(
            collective_id=0, has_side_effects=True, vmem_limit_bytes=VMEM_BYTES),
        cost_estimate=pl.CostEstimate(flops=flops, bytes_accessed=12 * half * width, transcendentals=half * tokens),
    )(table, hidden, gain, bias, labels, loss_mask)


def solution(mesh):
    n_dp = mesh.shape['dp']
    n_tp = mesh.shape['tp']

    def device_step(hidden, table, labels, loss_mask, ln_gain, ln_bias):
        batch, seq, width = hidden.shape
        grad_table, _, grad_hidden, sums = head_step(
            table, hidden.reshape(batch * seq, width), ln_gain[None], ln_bias[None], labels, loss_mask, n_dp, n_tp)
        return sums[2, 0], grad_hidden.reshape(batch, seq, width).astype(jnp.bfloat16), grad_table, sums[0], sums[1]

    specs_in = (P('dp', None, None), P('tp', None), P('dp', None), P('dp', None), P(None), P(None))
    specs_out = (P(), P('dp', None, None), P('tp', None), P(None), P(None))
    return jax.shard_map(device_step, mesh=mesh, in_specs=specs_in, out_specs=specs_out, check_vma=False)
```

time: 1980 us -> 746 us (0.38)
  waiting for transfers between devices: 1540 us -> 0 us
  Pallas kernels: 0 us -> 697 us
  matrix products: 246 us -> 0 us
  other arithmetic: 74.2 us -> 6.08 us
  blocking collectives: 65.6 us -> 0 us
    psum x2 -> x0, waiting for transfers between devices: 1540 us -> none  [the longest x1 1480 us: device_step(): lax.psum(jnp.einsum('btv,btd->vd', grad_logits, x_norm, preferred_element...]
    pallas_call x0 -> x1, Pallas kernels: none -> 697 us  [head_step(): pl.pallas_call(functools.partial(head_kernel, n_dp, n_tp), out_shape=(jax...]
    dot_general x3 -> x0, matrix products: 246 us -> none  [the longest x1 93.1 us: device_step(): jnp.einsum('btv,vd->btd', grad_logits, table, preferred_element_type=jnp....]
    psum x3 -> x0, blocking collectives: 57.1 us -> none  [the longest x1 24.4 us: device_step(): loss = lax.psum(jnp.sum(weight * (log_norm - target)), 'dp') / count]
    reduce_sum x5 -> x0, other arithmetic: 48.1 us -> none  [the longest x1 38.7 us: device_step(): stats = lax.psum(jnp.stack([jnp.sum(shifted, axis=-1), target_part]), 'tp')]
  transfers between devices with their start and end apart: 2 -> 0, of which waited for: 2 -> 0; matrix products, arithmetic and copies ran while one was open for 6% -> 0% of each run, Pallas kernels for 0% -> 0%
where the time goes in v4:
time: 746 us; the launch traced here: 744 us
  Pallas kernels  697 us (93%)
  local copies, waits for them, and re-layouts  40.2 us (5%)
    pallas_call x1, Pallas kernels, head_step(): pl.pallas_call(functools.partial(head_kernel, n_dp, n_tp), out_shape=(jax...  697 us
    unnamed x1, local copies, waits for them, and re-layouts  35.1 us

profile of v4, /device:TPU:0, one launch (start us, length us, event | category | flops | bytes accessed | tf_op | source)
XLA Modules:
  0.0 744.3 jit_solution(1053761280303737489)
XLA Ops:
  0.6 1.3 broadcast_in_dim.6.gain
  1.9 1.3 broadcast_in_dim.7.bias
  3.2 697.4 %shard_map.101 = (f32[12672,1024]{1,0:T(8,128)}, f32[6336,1024]{1,0:T(8,128)}, f32[4,512,1024]{2,1,0:T(8,128)}, f32[8,1024]{1,0:T(8,128)}) custom-call(bf16[12672,1024]{1,0:T(8,128)(2,1)} %table.1, bf16[2048,1024]{1,0:T(8,128)(2,1)} %bitcast.8, bf16[1,1024]{1,0:T(2,128)(2,1)} %broadcast_in_dim.6.gain, bf16[1,1024]{1,0:T(2,128)(2,1)} %broadcast_in_dim.7.bias, ...), custom_call_target="tpu_custom_call" | custom-call | flops 239175991296 | bytes 77856768 | tf_op jit(solution)/shard_map/pallas_call | solution.py:621
  700.6 1.2 slice.9
  701.8 6.1 convert_element_type.6
  707.8 1.4 fusion
  709.3 35.1 %copy.12 = f32[12672,1024]{1,0:T(8,128)} copy(f32[12672,1024]{1,0:T(8,128)} %get-tuple-element.20) | data formatting | bytes 103809024

commit v5 on v4

--- a/solution.py
+++ b/solution.py
@@ -12,8 +12,8 @@
 Z = 4
 Y = 2
 UNITS = 33
-PER_UNIT = 2
-SLOTS = 12
+PER_UNIT = 3
+SLOTS = 16
 TILE = 512
 PIECES = 4
 FORWARD_ROWS = 384
@@ -50,7 +50,7 @@
         n_dp, n_tp, table, hidden, gain, bias, labels, loss_mask,
         out, part, dh, sums,
         x, x_t, lse, scale, weight, label, target, hat, inv, send_q,
-        got, block_buf, top, total, stats, counts, ids,
+        got, block_buf, held, top, total, stats, counts, ids,
         red, loc, q_t, rows_buf, more_buf, stage, dx_t, from_core, from_x, levels, arrived,
         hidden_sem, block_sem, y_sem, beside_sem, core_sem, relay_sem, stat_send, stat_recv, count_send, count_recv,
         ids_sem,
@@ -71,6 +71,7 @@
     block_rows = block_buf.shape[1]
     blocks = shard // block_rows
     last = PIECES - 1
+    own_tiles, all_tiles, columns = own // TILE, tokens // TILE, width // COLUMNS
 
     dp = lax.axis_index('dp')
     tp = lax.axis_index('tp')
@@ -129,6 +130,9 @@
     def ids_copy(i):
         return remote((labels, loss_mask)[i], ids.at[i], ids_sem.at[0, i], ids_sem.at[1, i], dp=mate)
 
+    def row_of(ref):
+        return ref[...].astype(jnp.float32)[None, :]
+
     def block_of(q, k):
         return aligned(q * quarter + k * piece, piece)
 
@@ -139,7 +143,7 @@
         variance = jnp.mean(centred * centred, axis=-1, keepdims=True)
         inv_std = lax.rsqrt(variance + LN_EPS)
         x_hat = centred * inv_std
-        normed = (x_hat * gain[...].astype(jnp.float32) + bias[...].astype(jnp.float32)).astype(jnp.bfloat16)
+        normed = (x_hat * row_of(gain) + row_of(bias)).astype(jnp.bfloat16)
         wide = normed.astype(jnp.float32)
         x[at, :] = normed
         x_t[:, at] = wide.T.astype(jnp.bfloat16)
@@ -173,6 +177,13 @@
         x[at, :] = wide.astype(jnp.bfloat16)
         x_t[:, at] = wide.T.astype(jnp.bfloat16)
 
+    def fold(logits, at):
+        logits = logits.reshape(block_rows // 8, 8, TILE)
+        before = top[:, at]
+        now = jnp.maximum(before, jnp.max(logits, axis=0))
+        total[:, at] = total[:, at] * jnp.exp(before - now) + jnp.sum(jnp.exp(logits - now[None]), axis=0)
+        top[:, at] = now
+
     def block(b, carry):
         block_copy(b).wait()
 
@@ -211,14 +222,15 @@
 
         slot = b % 2
         row_ids = first_row + b * block_rows + lax.broadcasted_iota(jnp.int32, (block_rows, 1), 0)
-        for t in range(own // TILE):
+        fold(held[...], tile_at(own_tiles - 1))
+        for t in range(own_tiles):
             at = tile_at(t)
             logits = jnp.dot(block_buf[slot], x_t[:, at], preferred_element_type=jnp.float32)
-            logits = jnp.where(row_ids < VOCAB, logits, -jnp.inf).reshape(block_rows // 8, 8, TILE)
-            before = top[:, at]
-            now = jnp.maximum(before, jnp.max(logits, axis=0))
-            total[:, at] = total[:, at] * jnp.exp(before - now) + jnp.sum(jnp.exp(logits - now[None]), axis=0)
-            top[:, at] = now
+            logits = jnp.where(row_ids < VOCAB, logits, -jnp.inf)
+            if t + 1 < own_tiles:
+                fold(logits, at)
+            else:
+                held[...] = logits
         return carry
 
     def stat_copies():
@@ -288,7 +300,18 @@
         if t < own // TILE:
             add_dx(rows_buf[slot], q, t)
 
-    def compute_own(u):
+    def table_tile(n):
+        at = slice(n * COLUMNS, (n + 1) * COLUMNS)
+        stage[:, at] = jnp.dot(q_t[...], x[:, at], preferred_element_type=jnp.float32)
+
+    def more_tile(u, t):
+        theirs = (1 - y) * half + u * unit + unit_iota
+        q, _ = grads(more_buf[u % 2], theirs, tile_at(t))
+        add_dx(more_buf[u % 2], q, t)
+
+    few = (all_tiles - own_tiles) // 4
+
+    def compute_0(u):
         for h in range(2):
             rows_copy(h, u).wait()
 
@@ -297,30 +320,35 @@
             for h in range(2):
                 rows_copy(h, u + 1).start()
 
-        for t in range(own // TILE):
+        for t in list(range(own_tiles // 2)) + list(range(own_tiles, own_tiles + few)):
             main_tile(u, t)
 
-    def compute_table(u):
-        for t in range(own // TILE, tokens // TILE):
+    def compute_1(u):
+        for t in list(range(own_tiles // 2, own_tiles)) + list(range(own_tiles + few, own_tiles + 2 * few)):
             main_tile(u, t)
-        for n in range(width // COLUMNS):
-            at = slice(n * COLUMNS, (n + 1) * COLUMNS)
-            stage[:, at] = jnp.dot(q_t[...], x[:, at], preferred_element_type=jnp.float32)
+
+    def compute_2(u):
+        for t in range(own_tiles + 2 * few, all_tiles):
+            main_tile(u, t)
+        for n in range(columns - 1):
+            table_tile(n)
+
+    def compute_3(u):
+        more_copy(u).wait()
+
+        @pl.when(u + 1 < units)
+        def _():
+            more_copy(u + 1).start()
+
+        table_tile(columns - 1)
         for h in range(2):
             part_copy(h, u).start()
-
-    def compute_more(u):
-        more_copy(u).wait()
-
-        @pl.when(u + 1 < units)
-        def _():
-            more_copy(u + 1).start()
-
-        slot = u % 2
-        theirs = (1 - y) * half + u * unit + unit_iota
-        for t in range(own // TILE):
-            q, _ = grads(more_buf[slot], theirs, tile_at(t))
-            add_dx(more_buf[slot], q, t)
+        for t in range(own_tiles // 2):
+            more_tile(u, t)
+
+    def compute_4(u):
+        for t in range(own_tiles // 2, own_tiles):
+            more_tile(u, t)
 
     def settle(u):
         for h in range(2):
@@ -402,10 +430,30 @@
         return remote(dx_t.at[beside], from_x, cross_sem.at[0], cross_sem.at[1], tp=beside)
 
     def share_copy(i):
-        return remote(send_q, dh.at[tp], share_send.at[i], share_recv.at[i], tp=others[i])
-
-    def keep_copy():
-        return pltpu.make_async_copy(send_q, dh.at[tp], share_send.at[n_tp - 1])
+        return remote(send_q, got.at[tp], share_send.at[i], share_recv.at[i], tp=others[i])
+
+    def pass_copy():
+        return remote(got.at[beside], got.at[beside], share_send.at[2], share_recv.at[2], tp=partner)
+
+    def round_dh(q, ref):
+        at = aligned(q * quarter, quarter)
+        x[at, :] = ref.astype(jnp.bfloat16)
+
+    def dh_relay():
+        share_copy(1).wait_recv()
+        pass_copy().start()
+        round_dh(beside, got[beside])
+        share_copy(0).wait_recv()
+        round_dh(partner, got[partner])
+        round_dh(tp, send_q[...])
+
+    def dh_copy():
+        return pltpu.make_async_copy(x.at[pl.ds(0, own)], dh, hidden_sem.at[0])
+
+    def dh_finish():
+        pass_copy().wait_recv()
+        round_dh(across, got[across])
+        dh_copy().start()
 
     slab = 128
 
@@ -445,7 +493,7 @@
             x_hat = hat[at, :]
             levels[0, 0:1] = levels[0, 0:1] + jnp.sum(grad * x_hat, axis=0, keepdims=True)
             levels[0, 1:2] = levels[0, 1:2] + jnp.sum(grad, axis=0, keepdims=True)
-            grad_hat = grad * gain[...].astype(jnp.float32)
+            grad_hat = grad * row_of(gain)
             mean_grad = jnp.mean(grad_hat, axis=-1, keepdims=True)
             mean_proj = jnp.mean(grad_hat * x_hat, axis=-1, keepdims=True)
             send_q[at, :] = inv[at, 0:1] * (grad_hat - mean_grad - x_hat * mean_proj)
@@ -453,9 +501,8 @@
 
         lax.fori_loop(0, quarter // step, token_block, 0)
         level_copy(0).start()
-        for i in range(len(others)):
+        for i in range(2):
             share_copy(i).start()
-        keep_copy().start()
 
     level_peers = ({'tp': beside}, {'tp': partner}, {'dp': mate}, {'dp': z_mate}, {'dp': z_far})
 
@@ -492,6 +539,7 @@
 
     top[...] = jnp.full_like(top, jnp.finfo(jnp.float32).min)
     total[...] = jnp.zeros_like(total)
+    held[...] = jnp.full_like(held, -jnp.inf)
     target[...] = jnp.zeros_like(target)
 
     def clear(t, carry):
@@ -501,6 +549,7 @@
     lax.fori_loop(0, own // TILE, clear, 0)
     assert blocks > 8 + 6 * PIECES
     lax.fori_loop(0, blocks, block, 0)
+    fold(held[...], tile_at(own_tiles - 1))
 
     best = jnp.max(top[...], axis=0, keepdims=True)
     stats[0, tp, 0:1] = best
@@ -535,41 +584,46 @@
         mass = sum(stats[side, j, 1:2] * jnp.exp(tops[j] - best) for j in range(n_tp))
         lse[:, side * own:(side + 1) * own] = best + jnp.log(mass)
 
-    done = 3 * units - 1
-    ticks = 2 + 2 * (chunks + 2 * (Z - 1))
-    assert done + 36 < ticks
+    computes = (compute_0, compute_1, compute_2, compute_3, compute_4)
+    beats = len(computes)
+    start = beats - 1
+    done = beats * units - 1
+    ticks = start + 2 * (chunks + 2 * (Z - 1))
+    assert done + 38 < ticks
 
     def tick(i, carry):
-        u = i // 3
-        kind = i % 3
-
-        @pl.when(i == 2)
+        u = i // beats
+        kind = i % beats
+        since = jnp.maximum(i - start, 0)
+
+        @pl.when(i == start)
         def _():
             settle(0)
 
-        @pl.when((i >= 2) & (i % 2 == 0))
-        def _():
-            reduce_phase(jnp.maximum(i - 2, 0) // 2)
-
-        @pl.when((i >= 2) & (i % 2 == 1))
-        def _():
-            spread_phase(jnp.maximum(i - 2, 0) // 2)
-
-        @pl.when((i > 2) & (kind == 2) & (u < units))
+        @pl.when((i >= start) & (since % 2 == 0))
+        def _():
+            reduce_phase(since // 2)
+
+        @pl.when((i >= start) & (since % 2 == 1))
+        def _():
+            spread_phase(since // 2)
+
+        @pl.when((i > start) & (kind == beats - 1) & (u < units))
         def _():
             settle(u)
 
-        for j, compute in enumerate((compute_own, compute_table, compute_more)):
+        for j, compute in enumerate(computes):
             pl.when((kind == j) & (u < units))(functools.partial(compute, u))
 
-        events = ((1, dx_start), (4, dx_middle), (16, dx_finish), (18, lambda: level_next(0)), (20, lambda: level_next(1)),
-                  (26, lambda: level_next(2)), (33, lambda: level_next(3)))
+        events = ((1, dx_start), (5, dx_middle), (22, dx_finish), (24, lambda: level_next(0)), (26, lambda: level_next(1)),
+                  (33, lambda: level_next(2)), (37, lambda: level_next(3)), (38, dh_relay))
         for after, event in events:
             pl.when(i == done + after)(event)
         return carry
 
     lax.fori_loop(0, ticks, tick, 0)
     level_next(4)
+    dh_finish()
 
     for h in range(2):
         p = place[h]
@@ -592,9 +646,10 @@
     for i in range(2):
         swap_copy(i).wait_send()
     cross_copy().wait_send()
-    for i in range(len(others)):
-        share_copy(i).wait()
-    keep_copy().wait()
+    for i in range(2):
+        share_copy(i).wait_send()
+    pass_copy().wait_send()
+    dh_copy().wait()
     for i in range(len(level_peers)):
         level_copy(i).wait_send()
 
@@ -623,7 +678,7 @@
         out_shape=(
             jax.ShapeDtypeStruct((shard, width), f32),
             jax.ShapeDtypeStruct((half, width), f32),
-            jax.ShapeDtypeStruct((n_tp, quarter, width), f32),
+            jax.ShapeDtypeStruct((own, width), b16),
             jax.ShapeDtypeStruct((8, width), f32)),
         in_specs=[hbm, hbm, vmem, vmem, vmem, vmem],
         out_specs=(hbm, hbm, hbm, vmem),
@@ -633,6 +688,7 @@
             pltpu.VMEM((1, tokens), i32), pltpu.VMEM((1, tokens), f32),
             pltpu.VMEM((quarter, width), f32), pltpu.VMEM((quarter, lanes), f32), pltpu.VMEM((quarter, width), f32),
             pltpu.VMEM((n_tp, quarter, width), f32), pltpu.VMEM((2, FORWARD_ROWS, width), b16),
+            pltpu.VMEM((FORWARD_ROWS, TILE), f32),
             pltpu.VMEM((8, own), f32), pltpu.VMEM((8, own), f32),
             pltpu.VMEM((Y, n_tp, 2, own), f32), pltpu.VMEM((n_dp, 8, lanes), f32),
             pltpu.VMEM((2,) + labels.shape, i32),
@@ -649,7 +705,7 @@
             dma((2, SLOTS)), dma((2, SLOTS)), pltpu.SemaphoreType.REGULAR((2,)),
             dma((2,)), dma((2, chunks)), dma((2,)), dma((2,)),
             dma((2, 2)), dma((2,)), dma((2,)), dma((2, 2)), dma((2,)),
-            dma((2, 2)), dma((2,)), dma((n_tp,)), dma((n_tp - 1,)), dma((2, 5)),
+            dma((2, 2)), dma((2,)), dma((3,)), dma((3,)), dma((2, 5)),
         ],
         compiler_params=pltpu.CompilerParams(
             collective_id=0, has_side_effects=True, vmem_limit_bytes=VMEM_BYTES),
@@ -664,8 +720,8 @@
     def device_step(hidden, table, labels, loss_mask, ln_gain, ln_bias):
         batch, seq, width = hidden.shape
         grad_table, _, grad_hidden, sums = head_step(
-            table, hidden.reshape(batch * seq, width), ln_gain[None], ln_bias[None], labels, loss_mask, n_dp, n_tp)
-        return sums[2, 0], grad_hidden.reshape(batch, seq, width).astype(jnp.bfloat16), grad_table, sums[0], sums[1]
+            table, hidden.reshape(batch * seq, width), ln_gain, ln_bias, labels, loss_mask, n_dp, n_tp)
+        return sums[2, 0], grad_hidden.reshape(batch, seq, width), grad_table, sums[0], sums[1]
 
     specs_in = (P('dp', None, None), P('tp', None), P('dp', None), P('dp', None), P(None), P(None))
     specs_out = (P(), P('dp', None, None), P('tp', None), P(None), P(None))

time: 746 us -> 734 us (0.984)
    unnamed x1 -> x2, local copies, waits for them, and re-layouts: 35.1 us -> 39.7 us
where the time goes in v5:
time: 734 us
  Pallas kernels  691 us (94%)
  local copies, waits for them, and re-layouts  42.3 us (6%)
    pallas_call x1, Pallas kernels, head_step(): pl.pallas_call(functools.partial(head_kernel, n_dp, n_tp), out_shape=(jax...  691 us
    unnamed x2, local copies, waits for them, and re-layouts  39.7 us

profile of v5, /device:TPU:0, one launch (start us, length us, event | category | flops | bytes accessed | tf_op | source)
XLA Modules:
  0.0 734.2 jit_solution(16217616430260565737)
XLA Ops:
  0.6 691.2 %shard_map.101 = (f32[12672,1024]{1,0:T(8,128)}, f32[6336,1024]{1,0:T(8,128)}, bf16[2048,1024]{1,0:T(8,128)(2,1)}, f32[8,1024]{1,0:T(8,128)}) custom-call(bf16[12672,1024]{1,0:T(8,128)(2,1)} %table.1, bf16[2048,1024]{1,0:T(8,128)(2,1)} %bitcast.8, bf16[1024]{0:T(1024)(128)(2,1)} %gain.1, bf16[1024]{0:T(1024)(128)(2,1)} %bias.1, s32[8,256]{1,0:T(8,128)} %labels.1, ...), custom_call_target="tpu_custom_call" | custom-call | flops 239175991296 | bytes 77856768 | tf_op jit(solution)/shard_map/pallas_call | solution.py:676
  691.8 1.2 slice.9
  693.0 1.4 fusion
  694.4 4.6 copy.13
  699.1 35.1 %copy.14 = f32[12672,1024]{1,0:T(8,128)} copy(f32[12672,1024]{1,0:T(8,128)} %get-tuple-element.20) | data formatting | bytes 103809024

commit v6 on v5

--- a/solution.py
+++ b/solution.py
@@ -16,7 +16,9 @@
 SLOTS = 16
 TILE = 512
 PIECES = 4
-FORWARD_ROWS = 384
+FORWARD_ROWS = 704
+PLACE_ROWS = 264
+PLACE_SLOTS = 12
 COLUMNS = 256
 VMEM_BYTES = 67043328
 MESH = pl.DeviceIdType.MESH
@@ -155,11 +157,6 @@
         send_q[at, :] = wide
         hat[at, :] = x_hat
         inv[at, :] = jnp.broadcast_to(inv_std, (piece, inv.shape[1]))
-
-        @pl.when(k == 0)
-        def _():
-            pl.semaphore_wait(barrier, n_dp - 1 + 2 * len(others))
-        y_copy(k).start()
         return carry
 
     def next_piece(j, carry):
@@ -191,34 +188,40 @@
         def _():
             block_copy(b + 1).start()
 
-        phase = b % 6
-
-        @pl.when((phase == 0) & (b > 0) & (b <= 6 * PIECES))
-        def _():
-            k = jnp.maximum(b // 6 - 1, 0)
-            y_copy(k).wait_recv()
-            beside_copy(k).start()
-            core_copy(k).start()
-            convert(tp, k)
-
-        @pl.when((phase == 2) & (b >= 14) & (b < 14 + 6 * PIECES))
-        def _():
-            k = jnp.maximum(b - 14, 0) // 6
-            beside_copy(k).wait_recv()
-            relay_copy(k).start()
-            convert(beside, k)
-
-        @pl.when((phase == 4) & (b >= 10) & (b < 10 + 6 * PIECES))
-        def _():
-            k = jnp.maximum(b - 10, 0) // 6
-            core_copy(k).wait_recv()
-            convert(partner, k)
-
-        @pl.when((phase == 4) & (b >= 16) & (b < 10 + 6 * PIECES))
-        def _():
-            k = jnp.maximum(b - 16, 0) // 6
-            relay_copy(k).wait_recv()
-            convert(across, k)
+        def every_third(first, count):
+            d = b - first
+            return (d >= 0) & (d < 3 * count) & (jnp.maximum(d, 0) % 3 == 0), jnp.maximum(d, 0) // 3
+
+        due, k_y = every_third(4, PIECES)
+
+        @pl.when(due)
+        def _():
+            y_copy(k_y).wait_recv()
+            beside_copy(k_y).start()
+            core_copy(k_y).start()
+            convert(tp, k_y)
+
+        due, k_core = every_third(5, PIECES)
+
+        @pl.when(due)
+        def _():
+            core_copy(k_core).wait_recv()
+            convert(partner, k_core)
+
+        due, k_x = every_third(8, PIECES)
+
+        @pl.when(due)
+        def _():
+            beside_copy(k_x).wait_recv()
+            relay_copy(k_x).start()
+            convert(beside, k_x)
+
+        due, k_relay = every_third(9, PIECES - 1)
+
+        @pl.when(due)
+        def _():
+            relay_copy(k_relay).wait_recv()
+            convert(across, k_relay)
 
         slot = b % 2
         row_ids = first_row + b * block_rows + lax.broadcasted_iota(jnp.int32, (block_rows, 1), 0)
@@ -330,8 +333,10 @@
     def compute_2(u):
         for t in range(own_tiles + 2 * few, all_tiles):
             main_tile(u, t)
-        for n in range(columns - 1):
+        for n in range(columns):
             table_tile(n)
+        for h in range(2):
+            part_copy(h, u).start()
 
     def compute_3(u):
         more_copy(u).wait()
@@ -340,9 +345,6 @@
         def _():
             more_copy(u + 1).start()
 
-        table_tile(columns - 1)
-        for h in range(2):
-            part_copy(h, u).start()
         for t in range(own_tiles // 2):
             more_tile(u, t)
 
@@ -530,12 +532,15 @@
     more_copy(0).start()
     hidden_copy(0).wait()
     lax.fori_loop(0, PIECES, first_piece, 0)
+    lax.fori_loop(0, (n_tp - 1) * PIECES, next_piece, 0)
+    counts[dp] = jnp.full(counts.shape[1:], jnp.sum(loss_mask[...].astype(jnp.float32)), jnp.float32)
+    pl.semaphore_wait(barrier, n_dp - 1 + 2 * len(others))
+    for k in range(PIECES):
+        y_copy(k).start()
     for i in range(2):
         ids_copy(i).start()
-    counts[dp] = jnp.full(counts.shape[1:], jnp.sum(loss_mask[...].astype(jnp.float32)), jnp.float32)
     for j in range(n_dp - 1):
         count_copy(j).start()
-    lax.fori_loop(0, (n_tp - 1) * PIECES, next_piece, 0)
 
     top[...] = jnp.full_like(top, jnp.finfo(jnp.float32).min)
     total[...] = jnp.zeros_like(total)
@@ -547,7 +552,7 @@
         return carry
 
     lax.fori_loop(0, own // TILE, clear, 0)
-    assert blocks > 8 + 6 * PIECES
+    assert blocks >= 6 + 3 * PIECES
     lax.fori_loop(0, blocks, block, 0)
     fold(held[...], tile_at(own_tiles - 1))
 
@@ -586,7 +591,7 @@
 
     computes = (compute_0, compute_1, compute_2, compute_3, compute_4)
     beats = len(computes)
-    start = beats - 1
+    start = beats - 2
     done = beats * units - 1
     ticks = start + 2 * (chunks + 2 * (Z - 1))
     assert done + 38 < ticks
@@ -608,7 +613,7 @@
         def _():
             spread_phase(since // 2)
 
-        @pl.when((i > start) & (kind == beats - 1) & (u < units))
+        @pl.when((i > start) & (kind == start) & (u < units))
         def _():
             settle(u)
 
@@ -713,6 +718,62 @@
     )(table, hidden, gain, bias, labels, loss_mask)
 
 
+def place_kernel(table_in, dh_in, sums, table_out, dh_out, loss, gain_out, bias_out, buf, dh_buf, in_sem, out_sem, dh_sem):
+    size = buf.shape[1]
+    count = table_in.shape[0] // size
+    lag = PLACE_SLOTS // 2
+
+    def read(i):
+        return pltpu.make_async_copy(table_in.at[pl.ds(i * size, size)], buf.at[i % PLACE_SLOTS], in_sem.at[i % PLACE_SLOTS])
+
+    def write(i):
+        return pltpu.make_async_copy(buf.at[i % PLACE_SLOTS], table_out.at[pl.ds(i * size, size)], out_sem.at[i % PLACE_SLOTS])
+
+    dh_read = pltpu.make_async_copy(dh_in, dh_buf, dh_sem.at[0])
+    dh_write = pltpu.make_async_copy(dh_buf, dh_out, dh_sem.at[1])
+    for i in range(count + lag):
+        if i < count:
+            if i >= PLACE_SLOTS:
+                write(i - PLACE_SLOTS).wait()
+            read(i).start()
+        if i == 0:
+            dh_read.start()
+            loss[...] = sums[2:3, 0:1]
+            gain_out[...] = sums[0:1, :]
+            bias_out[...] = sums[1:2, :]
+        if i == lag:
+            dh_read.wait()
+            dh_write.start()
+        if i >= lag:
+            read(i - lag).wait()
+            write(i - lag).start()
+    for i in range(count - PLACE_SLOTS, count):
+        write(i).wait()
+    dh_write.wait()
+
+
+def place(table, dh, sums):
+    f32 = jnp.float32
+    dma = pltpu.SemaphoreType.DMA
+    vmem = pl.BlockSpec(memory_space=pltpu.VMEM)
+    hbm = pl.BlockSpec(memory_space=pltpu.HBM)
+    width = table.shape[1]
+    assert table.shape[0] % PLACE_ROWS == 0
+    return pl.pallas_call(
+        place_kernel,
+        out_shape=(
+            jax.ShapeDtypeStruct(table.shape, f32), jax.ShapeDtypeStruct(dh.shape, dh.dtype),
+            jax.ShapeDtypeStruct((1, 1), f32), jax.ShapeDtypeStruct((1, width), f32), jax.ShapeDtypeStruct((1, width), f32)),
+        in_specs=[hbm, hbm, vmem],
+        out_specs=(hbm, hbm, vmem, vmem, vmem),
+        scratch_shapes=[
+            pltpu.VMEM((PLACE_SLOTS, PLACE_ROWS, width), f32), pltpu.VMEM(dh.shape, dh.dtype),
+            dma((PLACE_SLOTS,)), dma((PLACE_SLOTS,)), dma((2,))],
+        compiler_params=pltpu.CompilerParams(vmem_limit_bytes=VMEM_BYTES),
+        cost_estimate=pl.CostEstimate(flops=0, bytes_accessed=8 * table.size + 4 * dh.size, transcendentals=0),
+    )(table, dh, sums)
+
+
 def solution(mesh):
     n_dp = mesh.shape['dp']
     n_tp = mesh.shape['tp']
@@ -721,7 +782,9 @@
         batch, seq, width = hidden.shape
         grad_table, _, grad_hidden, sums = head_step(
             table, hidden.reshape(batch * seq, width), ln_gain, ln_bias, labels, loss_mask, n_dp, n_tp)
-        return sums[2, 0], grad_hidden.reshape(batch, seq, width), grad_table, sums[0], sums[1]
+        grad_table, grad_hidden, loss, grad_gain, grad_bias = place(grad_table, grad_hidden, sums)
+        return (loss.reshape(()), grad_hidden.reshape(batch, seq, width), grad_table,
+                grad_gain.reshape(width), grad_bias.reshape(width))
 
     specs_in = (P('dp', None, None), P('tp', None), P('dp', None), P('dp', None), P(None), P(None))
     specs_out = (P(), P('dp', None, None), P('tp', None), P(None), P(None))

time: 734 us -> 726 us (0.989)
  local copies, waits for them, and re-layouts: 42.3 us -> 0 us
  Pallas kernels: 691 us -> 725 us
    unnamed x2 -> x0, local copies, waits for them, and re-layouts: 39.7 us -> none
    pallas_call x0 -> x1, Pallas kernels: none -> 39.4 us  [place(): pl.pallas_call(place_kernel, out_shape=(jax.ShapeDtypeStruct(table.shape,...]
where the time goes in v6:
time: 726 us
  Pallas kernels  725 us (100%)
    pallas_call x1, Pallas kernels, head_step(): pl.pallas_call(functools.partial(head_kernel, n_dp, n_tp), out_shape=(jax...  686 us
    pallas_call x1, Pallas kernels, place(): pl.pallas_call(place_kernel, out_shape=(jax.ShapeDtypeStruct(table.shape,...  39.4 us

profile of v6, /device:TPU:0, one launch (start us, length us, event | category | flops | bytes accessed | tf_op | source)
XLA Modules:
  0.0 726.0 jit_solution(10073288811490768989)
XLA Ops:
  0.6 685.8 %shard_map.101 = (f32[12672,1024]{1,0:T(8,128)}, f32[6336,1024]{1,0:T(8,128)}, bf16[2048,1024]{1,0:T(8,128)(2,1)}, f32[8,1024]{1,0:T(8,128)}) custom-call(bf16[12672,1024]{1,0:T(8,128)(2,1)} %table.1, bf16[2048,1024]{1,0:T(8,128)(2,1)} %bitcast.5, bf16[1024]{0:T(1024)(128)(2,1)} %gain.1, bf16[1024]{0:T(1024)(128)(2,1)} %bias.1, s32[8,256]{1,0:T(8,128)} %labels.1, ...), custom_call_target="tpu_custom_call" | custom-call | flops 239175991296 | bytes 77856768 | tf_op jit(solution)/shard_map/pallas_call | solution.py:681
  686.5 39.4 %shard_map.102 = (f32[12672,1024]{1,0:T(8,128)}, bf16[2048,1024]{1,0:T(8,128)(2,1)}, f32[1,1]{1,0:T(1,128)}, f32[1,1024]{1,0:T(1,128)}, f32[1,1024]{1,0:T(1,128)}) custom-call(f32[12672,1024]{1,0:T(8,128)} %get-tuple-element.13.table_in, bf16[2048,1024]{1,0:T(8,128)(2,1)} %get-tuple-element.14.dh_in, f32[8,1024]{1,0:T(8,128)} %get-tuple-element.15.sums), custom_call_target="tpu_custom_call" | custom-call | bytes 112197632 | tf_op jit(solution)/shard_map/pallas_call | solution.py:762

commit v7 on v6

--- a/solution.py
+++ b/solution.py
@@ -16,9 +16,10 @@
 SLOTS = 16
 TILE = 512
 PIECES = 4
+PARCELS = 8
 FORWARD_ROWS = 704
-PLACE_ROWS = 264
-PLACE_SLOTS = 12
+PLACE_ROWS = 528
+PLACE_SLOTS = 16
 COLUMNS = 256
 VMEM_BYTES = 67043328
 MESH = pl.DeviceIdType.MESH
@@ -72,7 +73,8 @@
     unit = 2 * strip
     block_rows = block_buf.shape[1]
     blocks = shard // block_rows
-    last = PIECES - 1
+    last = PARCELS - 1
+    parcel = quarter // PARCELS
     own_tiles, all_tiles, columns = own // TILE, tokens // TILE, width // COLUMNS
 
     dp = lax.axis_index('dp')
@@ -108,10 +110,10 @@
             table.at[pl.ds(b * block_rows, block_rows)], block_buf.at[b % 2], block_sem.at[b % 2])
 
     def got_piece(q, k):
-        return got.at[q, pl.ds(k * piece, piece)]
+        return got.at[q, pl.ds(k * parcel, parcel)]
 
     def y_copy(k):
-        return remote(send_q.at[pl.ds(k * piece, piece)], got_piece(tp, k), y_sem.at[0, k], y_sem.at[1, k], dp=mate)
+        return remote(send_q.at[pl.ds(k * parcel, parcel)], got_piece(tp, k), y_sem.at[0, k], y_sem.at[1, k], dp=mate)
 
     def beside_copy(k):
         return remote(got_piece(tp, k), got_piece(tp, k), beside_sem.at[0, k], beside_sem.at[1, k], tp=beside)
@@ -188,40 +190,46 @@
         def _():
             block_copy(b + 1).start()
 
-        def every_third(first, count):
-            d = b - first
-            return (d >= 0) & (d < 3 * count) & (jnp.maximum(d, 0) % 3 == 0), jnp.maximum(d, 0) // 3
-
-        due, k_y = every_third(4, PIECES)
+        def paced(first, count):
+            d = jnp.maximum(b - first, 0)
+            beat = d % 5
+            k = 3 * (d // 5) + (beat + 1) // 2
+            return (b >= first) & ((beat < 2) | (beat == 3)) & (k < count), jnp.minimum(k, PARCELS - 1)
+
+        due, k_y = paced(3, PARCELS)
 
         @pl.when(due)
         def _():
-            y_copy(k_y).wait_recv()
+            with jax.named_scope('wait_y'):
+                y_copy(k_y).wait_recv()
             beside_copy(k_y).start()
             core_copy(k_y).start()
-            convert(tp, k_y)
-
-        due, k_core = every_third(5, PIECES)
+            pl.when(k_y % 2 == 1)(lambda: convert(tp, k_y // 2))
+
+        due, k_core = paced(4, PARCELS)
 
         @pl.when(due)
         def _():
-            core_copy(k_core).wait_recv()
-            convert(partner, k_core)
-
-        due, k_x = every_third(8, PIECES)
+            with jax.named_scope('wait_core'):
+                core_copy(k_core).wait_recv()
+            pl.when(k_core % 2 == 1)(lambda: convert(partner, k_core // 2))
+
+        due, k_x = paced(6, PARCELS)
 
         @pl.when(due)
         def _():
-            beside_copy(k_x).wait_recv()
+            with jax.named_scope('wait_x'):
+                beside_copy(k_x).wait_recv()
             relay_copy(k_x).start()
-            convert(beside, k_x)
-
-        due, k_relay = every_third(9, PIECES - 1)
+            pl.when(k_x % 2 == 1)(lambda: convert(beside, k_x // 2))
+
+        due, k_relay = paced(7, PARCELS - 1)
 
         @pl.when(due)
         def _():
-            relay_copy(k_relay).wait_recv()
-            convert(across, k_relay)
+            with jax.named_scope('wait_relay'):
+                relay_copy(k_relay).wait_recv()
+            pl.when(k_relay % 2 == 1)(lambda: convert(across, k_relay // 2))
 
         slot = b % 2
         row_ids = first_row + b * block_rows + lax.broadcasted_iota(jnp.int32, (block_rows, 1), 0)
@@ -531,11 +539,14 @@
         rows_copy(h, 0).start()
     more_copy(0).start()
     hidden_copy(0).wait()
-    lax.fori_loop(0, PIECES, first_piece, 0)
-    lax.fori_loop(0, (n_tp - 1) * PIECES, next_piece, 0)
+    with jax.named_scope('lnfirst'):
+        lax.fori_loop(0, PIECES, first_piece, 0)
+    with jax.named_scope('lnrest'):
+        lax.fori_loop(0, (n_tp - 1) * PIECES, next_piece, 0)
     counts[dp] = jnp.full(counts.shape[1:], jnp.sum(loss_mask[...].astype(jnp.float32)), jnp.float32)
-    pl.semaphore_wait(barrier, n_dp - 1 + 2 * len(others))
-    for k in range(PIECES):
+    with jax.named_scope('entry'):
+        pl.semaphore_wait(barrier, n_dp - 1 + 2 * len(others))
+    for k in range(PARCELS):
         y_copy(k).start()
     for i in range(2):
         ids_copy(i).start()
@@ -552,8 +563,9 @@
         return carry
 
     lax.fori_loop(0, own // TILE, clear, 0)
-    assert blocks >= 6 + 3 * PIECES
-    lax.fori_loop(0, blocks, block, 0)
+    assert blocks > 6 + 5 * (PARCELS - 1) // 3 and PARCELS == 2 * PIECES
+    with jax.named_scope('blocks'):
+        lax.fori_loop(0, blocks, block, 0)
     fold(held[...], tile_at(own_tiles - 1))
 
     best = jnp.max(top[...], axis=0, keepdims=True)
@@ -562,8 +574,9 @@
     for copy in stat_copies():
         copy.start()
 
-    relay_copy(last).wait_recv()
-    convert(across, last)
+    with jax.named_scope('lastrelay'):
+        relay_copy(last).wait_recv()
+    convert(across, PIECES - 1)
     for i in range(2):
         ids_copy(i).wait()
     for j in range(n_dp - 1):
@@ -574,15 +587,16 @@
             label[:, at] = rows_of[i:i + 1, :] - first_row
             weight[:, at] = marks[i:i + 1, :].astype(jnp.float32)
     scale[...] = weight[...] / tokens_counted()
-    for k in range(PIECES):
+    for k in range(PARCELS):
         for copy in (y_copy(k), beside_copy(k), core_copy(k), relay_copy(k)):
             copy.wait_send()
     for j in range(n_dp - 1):
         count_copy(j).wait_send()
-    for other in others:
-        stat_arrival(0, other).wait_recv()
-    for other in (tp,) + others:
-        stat_arrival(1, other).wait_recv()
+    with jax.named_scope('statwait'):
+        for other in others:
+            stat_arrival(0, other).wait_recv()
+        for other in (tp,) + others:
+            stat_arrival(1, other).wait_recv()
     for side in range(Y):
         tops = [stats[side, j, 0:1] for j in range(n_tp)]
         best = functools.reduce(jnp.maximum, tops)
@@ -607,18 +621,23 @@
 
         @pl.when((i >= start) & (since % 2 == 0))
         def _():
-            reduce_phase(since // 2)
+            with jax.named_scope('red'):
+                reduce_phase(since // 2)
 
         @pl.when((i >= start) & (since % 2 == 1))
         def _():
-            spread_phase(since // 2)
+            with jax.named_scope('spread'):
+                spread_phase(since // 2)
 
         @pl.when((i > start) & (kind == start) & (u < units))
         def _():
             settle(u)
 
         for j, compute in enumerate(computes):
-            pl.when((kind == j) & (u < units))(functools.partial(compute, u))
+            def scoped(compute=compute, j=j):
+                with jax.named_scope(f'calc{j}'):
+                    compute(u)
+            pl.when((kind == j) & (u < units))(scoped)
 
         events = ((1, dx_start), (5, dx_middle), (22, dx_finish), (24, lambda: level_next(0)), (26, lambda: level_next(1)),
                   (33, lambda: level_next(2)), (37, lambda: level_next(3)), (38, dh_relay))
@@ -627,8 +646,10 @@
         return carry
 
     lax.fori_loop(0, ticks, tick, 0)
-    level_next(4)
-    dh_finish()
+    with jax.named_scope('finallevel'):
+        level_next(4)
+    with jax.named_scope('dhfinish'):
+        dh_finish()
 
     for h in range(2):
         p = place[h]
@@ -644,8 +665,9 @@
         def _():
             pltpu.make_async_copy(mine, mine, bc_send.at[h]).wait()
 
-        pltpu.make_async_copy(mine, mine, mate_send.at[h]).wait()
-        pltpu.make_async_copy(theirs, theirs, mate_recv.at[h]).wait()
+        with jax.named_scope('matewait'):
+            pltpu.make_async_copy(mine, mine, mate_send.at[h]).wait()
+            pltpu.make_async_copy(theirs, theirs, mate_recv.at[h]).wait()
     for copy in stat_copies():
         copy.wait_send()
     for i in range(2):
@@ -704,7 +726,7 @@
             pltpu.VMEM((n_tp, width, quarter), f32),
             pltpu.VMEM((2, width, quarter), f32), pltpu.VMEM((width, quarter), f32),
             pltpu.VMEM((5, 8, width), f32), pltpu.VMEM((5, 8, width), f32),
-            dma((n_tp,)), dma((2,)), dma((2, PIECES)), dma((2, PIECES)), dma((2, PIECES)), dma((2, PIECES)),
+            dma((n_tp,)), dma((2,)), dma((2, PARCELS)), dma((2, PARCELS)), dma((2, PARCELS)), dma((2, PARCELS)),
             dma((2 * n_tp - 1,)), dma((Y, n_tp)), dma((n_dp - 1,)), dma((n_dp,)),
             dma((2, 2)),
             dma((2, SLOTS)), dma((2, SLOTS)), pltpu.SemaphoreType.REGULAR((2,)),

time: 726 us -> 726 us (level)
  no operation moved by 1% of the time
where the time goes in v7:
time: 726 us
  Pallas kernels  725 us (100%)
    pallas_call x1, Pallas kernels, head_step(): pl.pallas_call(functools.partial(head_kernel, n_dp, n_tp), out_shape=(jax...  687 us
    pallas_call x1, Pallas kernels, place(): pl.pallas_call(place_kernel, out_shape=(jax.ShapeDtypeStruct(table.shape,...  38.1 us

profile of v7, /device:TPU:0, one launch (start us, length us, event | category | flops | bytes accessed | tf_op | source)
XLA Modules:
  0.0 725.9 jit_solution(17237165087981138559)
XLA Ops:
  0.6 687.0 %shard_map.101 = (f32[12672,1024]{1,0:T(8,128)}, f32[6336,1024]{1,0:T(8,128)}, bf16[2048,1024]{1,0:T(8,128)(2,1)}, f32[8,1024]{1,0:T(8,128)}) custom-call(bf16[12672,1024]{1,0:T(8,128)(2,1)} %table.1, bf16[2048,1024]{1,0:T(8,128)(2,1)} %bitcast.5, bf16[1024]{0:T(1024)(128)(2,1)} %gain.1, bf16[1024]{0:T(1024)(128)(2,1)} %bias.1, s32[8,256]{1,0:T(8,128)} %labels.1, ...), custom_call_target="tpu_custom_call" | custom-call | flops 239175991296 | bytes 77856768 | tf_op jit(solution)/shard_map/pallas_call | solution.py:703
  687.7 38.1 %shard_map.102 = (f32[12672,1024]{1,0:T(8,128)}, bf16[2048,1024]{1,0:T(8,128)(2,1)}, f32[1,1]{1,0:T(1,128)}, f32[1,1024]{1,0:T(1,128)}, f32[1,1024]{1,0:T(1,128)}) custom-call(f32[12672,1024]{1,0:T(8,128)} %get-tuple-element.13.table_in, bf16[2048,1024]{1,0:T(8,128)(2,1)} %get-tuple-element.14.dh_in, f32[8,1024]{1,0:T(8,128)} %get-tuple-element.15.sums), custom_call_target="tpu_custom_call" | custom-call | bytes 112197632 | tf_op jit(solution)/shard_map/pallas_call | solution.py:784

commit v8 on v6

--- a/solution.py
+++ b/solution.py
@@ -12,13 +12,15 @@
 Z = 4
 Y = 2
 UNITS = 33
-PER_UNIT = 3
+PER_UNIT = 6
 SLOTS = 16
+RING = 4
+END_LAG = 6
 TILE = 512
 PIECES = 4
 FORWARD_ROWS = 704
-PLACE_ROWS = 264
-PLACE_SLOTS = 12
+PLACE_ROWS = 528
+PLACE_SLOTS = 16
 COLUMNS = 256
 VMEM_BYTES = 67043328
 MESH = pl.DeviceIdType.MESH
@@ -53,10 +55,11 @@
         out, part, dh, sums,
         x, x_t, lse, scale, weight, label, target, hat, inv, send_q,
         got, block_buf, held, top, total, stats, counts, ids,
-        red, loc, q_t, rows_buf, more_buf, stage, dx_t, from_core, from_x, levels, arrived,
+        red, met, loc, q_t, rows_buf, more_buf, stage, dx_t, from_core, from_x, levels, arrived,
         hidden_sem, block_sem, y_sem, beside_sem, core_sem, relay_sem, stat_send, stat_recv, count_send, count_recv,
         ids_sem,
-        red_send, red_recv, credit, bc_send, bc_recv, mate_send, mate_recv, loc_sem, own_sem, part_sem, rows_sem, more_sem,
+        up_send, up_recv, meet_send, meet_recv, down_send, down_recv, mate_send, mate_recv, credit,
+        loc_sem, own_sem, part_sem, rows_sem, more_sem,
         swap_sem, cross_sem, share_send, share_recv, level_sem):
     own, width = hidden.shape
     tokens = Y * own
@@ -65,11 +68,10 @@
     quarter = own // n_tp
     piece = quarter // PIECES
     batch, seq = labels.shape
-    size = red.shape[2]
-    chunks = half // (2 * size)
-    strip = size * PER_UNIT
+    size = red.shape[1]
+    chunks = half // size
+    unit = size * PER_UNIT
     units = chunks // PER_UNIT
-    unit = 2 * strip
     block_rows = block_buf.shape[1]
     blocks = shard // block_rows
     last = PIECES - 1
@@ -86,9 +88,8 @@
     dp_others = [lax.rem(dp + j, n_dp) for j in range(1, n_dp)]
     z_mate = dp + Y - 2 * Y * (z % 2)
     z_far = dp + 2 * Y - 4 * Y * (z // 2)
-    place = (Z - 1 - z, z)
-    onward = (dp - Y, dp + Y)
-    back = (dp + Y, dp - Y)
+    inner = (z == 1) | (z == 2)
+    z_cross = dp + Y * (Z - 1 - 2 * z)
     first_row = tp * shard
 
     barrier = pltpu.get_barrier_semaphore()
@@ -244,40 +245,39 @@
     def stat_arrival(side, other):
         return remote(stats.at[side, other], stats.at[side, other], stat_send.at[0], stat_recv.at[side, other], tp=partner)
 
-    def part_rows(h, c):
-        return part.at[pl.ds(h * (half // 2) + c * size, size)]
-
-    def out_rows(side, h, c):
-        return out.at[pl.ds(side * half + h * (half // 2) + c * size, size)]
-
-    def fetch(h, c):
-        return pltpu.make_async_copy(part_rows(h, c), loc.at[h, c % 2], loc_sem.at[h, c % 2])
-
-    def reduce_copy(h, c, src):
-        slot = c % SLOTS
-        return remote(src, red.at[h, slot], red_send.at[h, slot], red_recv.at[h, slot], dp=onward[h])
-
-    def spread_copy(h, c):
-        return remote(out_rows(y, h, c), out_rows(y, h, c), bc_send.at[h], bc_recv.at[h, c], dp=back[h])
-
-    def mate_copy(h, c):
-        return remote(out_rows(y, h, c), out_rows(y, h, c), mate_send.at[h], mate_recv.at[h], dp=mate)
-
-    def own_copy(h, c):
-        return pltpu.make_async_copy(red.at[h, c % SLOTS], out_rows(y, h, c), own_sem.at[h])
-
-    def rows_copy(h, u):
-        return pltpu.make_async_copy(
-            table.at[pl.ds(y * half + h * (half // 2) + u * strip, strip)],
-            rows_buf.at[u % 2, pl.ds(h * strip, strip)], rows_sem.at[u % 2, h])
+    def part_rows(c):
+        return part.at[pl.ds(c * size, size)]
+
+    def out_rows(side, c):
+        return out.at[pl.ds(side * half + c * size, size)]
+
+    def fetch(c):
+        return pltpu.make_async_copy(part_rows(c), loc.at[c % 2], loc_sem.at[c % 2])
+
+    def up_copy(c):
+        return remote(part_rows(c), red.at[c % SLOTS], up_send.at[c % RING], up_recv.at[c % SLOTS], dp=z_mate)
+
+    def meet_copy(c):
+        return remote(red.at[c % SLOTS], met.at[c % SLOTS], meet_send.at[c % RING], meet_recv.at[c % SLOTS], dp=z_cross)
+
+    def down_copy(c):
+        return remote(met.at[c % SLOTS], out_rows(y, c), down_send.at[c % RING], down_recv.at[c % SLOTS], dp=z_mate)
+
+    def mate_copy(c, src):
+        return remote(src, out_rows(y, c), mate_send.at[c % RING], mate_recv.at[c // (chunks // 2)], dp=mate)
+
+    def own_copy(c):
+        return pltpu.make_async_copy(met.at[c % SLOTS], out_rows(y, c), own_sem.at[c % RING])
+
+    def rows_copy(u):
+        return pltpu.make_async_copy(table.at[pl.ds(y * half + u * unit, unit)], rows_buf.at[u % 2], rows_sem.at[u % 2])
 
     def more_copy(u):
         return pltpu.make_async_copy(
             table.at[pl.ds((1 - y) * half + u * unit, unit)], more_buf.at[u % 2], more_sem.at[u % 2])
 
-    def part_copy(h, u):
-        return pltpu.make_async_copy(
-            stage.at[pl.ds(h * strip, strip)], part.at[pl.ds(h * (half // 2) + u * strip, strip)], part_sem.at[h])
+    def part_copy(u):
+        return pltpu.make_async_copy(stage, part.at[pl.ds(u * unit, unit)], part_sem.at[0])
 
     unit_iota = lax.broadcasted_iota(jnp.int32, (unit, 1), 0)
 
@@ -295,8 +295,7 @@
     def main_tile(u, t):
         slot = u % 2
         at = tile_at(t)
-        mine = y * half + u * strip + unit_iota
-        row_ids = jnp.where(unit_iota < strip, mine, mine + (half // 2 - strip))
+        row_ids = y * half + u * unit + unit_iota
         q, hits = grads(rows_buf[slot], row_ids, at)
         q_t[:, at] = q
         target[:, at] = target[:, at] + jnp.sum(hits, axis=0, keepdims=True)
@@ -315,13 +314,11 @@
     few = (all_tiles - own_tiles) // 4
 
     def compute_0(u):
-        for h in range(2):
-            rows_copy(h, u).wait()
+        rows_copy(u).wait()
 
         @pl.when(u + 1 < units)
         def _():
-            for h in range(2):
-                rows_copy(h, u + 1).start()
+            rows_copy(u + 1).start()
 
         for t in list(range(own_tiles // 2)) + list(range(own_tiles, own_tiles + few)):
             main_tile(u, t)
@@ -335,8 +332,7 @@
             main_tile(u, t)
         for n in range(columns):
             table_tile(n)
-        for h in range(2):
-            part_copy(h, u).start()
+        part_copy(u).start()
 
     def compute_3(u):
         more_copy(u).wait()
@@ -353,77 +349,78 @@
             more_tile(u, t)
 
     def settle(u):
-        for h in range(2):
-            part_copy(h, u).wait()
-
-    def send_reduced(h, c, src):
+        part_copy(u).wait()
+
+    def within(c):
+        return (c >= 0) & (c < chunks)
+
+    def take_credit(i, c):
         @pl.when(c >= SLOTS)
         def _():
-            pl.semaphore_wait(credit.at[h], 1)
-        reduce_copy(h, c, src).start()
-
-    def free_slot(h, c):
+            pl.semaphore_wait(credit.at[i], 1)
+
+    def give_credit(i, c, other):
         @pl.when(c + SLOTS < chunks)
         def _():
-            pl.semaphore_signal(credit.at[h], inc=1, device_id={'dp': back[h]}, device_id_type=MESH)
-
-    def reduce_phase(s):
-        for h in range(2):
-            p = place[h]
-            c = s - p
-            here = (c >= 0) & (c < chunks)
-
-            @pl.when(here & (p == 0))
+            pl.semaphore_signal(credit.at[i], inc=1, device_id={'dp': other}, device_id_type=MESH)
+
+    def end_step(t):
+        @pl.when(t < chunks)
+        def _():
+            @pl.when(t >= 2)
             def _():
-                @pl.when(c >= 2)
-                def _():
-                    reduce_copy(h, c - 2, part_rows(h, c - 2)).wait_send()
-                send_reduced(h, c, part_rows(h, c))
-
-            @pl.when(here & (p > 0))
+                up_copy(t - 2).wait_send()
+            take_credit(0, t)
+            up_copy(t).start()
+
+        c = t - END_LAG
+
+        @pl.when(within(c))
+        def _():
+            down_copy(c).wait_recv()
+
+            @pl.when(c >= RING)
             def _():
-                slot = c % SLOTS
-                reduce_copy(h, c, red.at[h, slot]).wait_recv()
-                fetch(h, c).wait()
-                red[h, slot] = red[h, slot] + loc[h, c % 2]
-
-                @pl.when(p < Z - 1)
-                def _():
-                    @pl.when(c >= 2)
-                    def _():
-                        reduce_copy(h, c - 2, red.at[h, (c - 2) % SLOTS]).wait_send()
-                        free_slot(h, c - 2)
-                    send_reduced(h, c, red.at[h, slot])
-
-                @pl.when(p == Z - 1)
-                def _():
-                    own_copy(h, c).start()
-
-            @pl.when((p > 0) & (c >= -1) & (c + 1 < chunks))
-            def _():
-                fetch(h, c + 1).start()
-
-    def spread_phase(s):
-        for h in range(2):
-            p = place[h]
-            c = s - 2 * (Z - 1) + p
-
-            @pl.when((c >= 0) & (c < chunks))
-            def _():
-                @pl.when(p == Z - 1)
-                def _():
-                    own_copy(h, c).wait()
-                    free_slot(h, c)
-
-                @pl.when(p < Z - 1)
-                def _():
-                    spread_copy(h, c).wait_recv()
-
-                @pl.when(p > 0)
-                def _():
-                    spread_copy(h, c).start()
-
-                mate_copy(h, c).start()
+                mate_copy(c - RING, out_rows(y, c - RING)).wait_send()
+            mate_copy(c, out_rows(y, c)).start()
+
+    def inner_step(t):
+        c = t - 2
+
+        @pl.when(within(c))
+        def _():
+            slot = c % SLOTS
+            up_copy(c).wait_recv()
+            fetch(c).wait()
+            red[slot] = red[slot] + loc[c % 2]
+            take_credit(1, c)
+            meet_copy(c).start()
+
+        @pl.when(within(c + 1))
+        def _():
+            fetch(c + 1).start()
+
+        c_met = t - 4
+
+        @pl.when(within(c_met))
+        def _():
+            slot = c_met % SLOTS
+            meet_copy(c_met).wait_recv()
+            met[slot] = red[slot] + met[slot]
+            down_copy(c_met).start()
+            mate_copy(c_met, met.at[slot]).start()
+            own_copy(c_met).start()
+            meet_copy(c_met).wait_send()
+            give_credit(0, c_met, z_mate)
+
+        c_gone = t - 6
+
+        @pl.when(within(c_gone))
+        def _():
+            own_copy(c_gone).wait()
+            down_copy(c_gone).wait_send()
+            mate_copy(c_gone, met.at[c_gone % SLOTS]).wait_send()
+            give_credit(1, c_gone, z_cross)
 
     def swap_copy(i):
         return remote(dx_t.at[2 * i + 1 - core], from_core.at[i], swap_sem.at[0, i], swap_sem.at[1, i], tp=partner)
@@ -527,12 +524,12 @@
     for j in range(n_tp):
         hidden_copy(j).start()
     block_copy(0).start()
-    for h in range(2):
-        rows_copy(h, 0).start()
+    rows_copy(0).start()
     more_copy(0).start()
     hidden_copy(0).wait()
     lax.fori_loop(0, PIECES, first_piece, 0)
-    lax.fori_loop(0, (n_tp - 1) * PIECES, next_piece, 0)
+    with jax.named_scope('lnrest'):
+        lax.fori_loop(0, (n_tp - 1) * PIECES, next_piece, 0)
     counts[dp] = jnp.full(counts.shape[1:], jnp.sum(loss_mask[...].astype(jnp.float32)), jnp.float32)
     pl.semaphore_wait(barrier, n_dp - 1 + 2 * len(others))
     for k in range(PIECES):
@@ -553,7 +550,8 @@
 
     lax.fori_loop(0, own // TILE, clear, 0)
     assert blocks >= 6 + 3 * PIECES
-    lax.fori_loop(0, blocks, block, 0)
+    with jax.named_scope('blocks'):
+        lax.fori_loop(0, blocks, block, 0)
     fold(held[...], tile_at(own_tiles - 1))
 
     best = jnp.max(top[...], axis=0, keepdims=True)
@@ -562,7 +560,8 @@
     for copy in stat_copies():
         copy.start()
 
-    relay_copy(last).wait_recv()
+    with jax.named_scope('lastrelay'):
+        relay_copy(last).wait_recv()
     convert(across, last)
     for i in range(2):
         ids_copy(i).wait()
@@ -579,10 +578,11 @@
             copy.wait_send()
     for j in range(n_dp - 1):
         count_copy(j).wait_send()
-    for other in others:
-        stat_arrival(0, other).wait_recv()
-    for other in (tp,) + others:
-        stat_arrival(1, other).wait_recv()
+    with jax.named_scope('statwait'):
+        for other in others:
+            stat_arrival(0, other).wait_recv()
+        for other in (tp,) + others:
+            stat_arrival(1, other).wait_recv()
     for side in range(Y):
         tops = [stats[side, j, 0:1] for j in range(n_tp)]
         best = functools.reduce(jnp.maximum, tops)
@@ -593,59 +593,63 @@
     beats = len(computes)
     start = beats - 2
     done = beats * units - 1
-    ticks = start + 2 * (chunks + 2 * (Z - 1))
+    ticks = start + chunks + END_LAG
     assert done + 38 < ticks
 
     def tick(i, carry):
         u = i // beats
         kind = i % beats
-        since = jnp.maximum(i - start, 0)
 
         @pl.when(i == start)
         def _():
             settle(0)
 
-        @pl.when((i >= start) & (since % 2 == 0))
-        def _():
-            reduce_phase(since // 2)
-
-        @pl.when((i >= start) & (since % 2 == 1))
-        def _():
-            spread_phase(since // 2)
+        @pl.when((i >= start) & jnp.logical_not(inner))
+        def _():
+            with jax.named_scope('red'):
+                end_step(jnp.maximum(i - start, 0))
+
+        @pl.when((i >= start) & inner)
+        def _():
+            with jax.named_scope('red'):
+                inner_step(jnp.maximum(i - start, 0))
 
         @pl.when((i > start) & (kind == start) & (u < units))
         def _():
             settle(u)
 
         for j, compute in enumerate(computes):
-            pl.when((kind == j) & (u < units))(functools.partial(compute, u))
+            def scoped(compute=compute, j=j):
+                with jax.named_scope(f'calc{j}'):
+                    compute(u)
+            pl.when((kind == j) & (u < units))(scoped)
 
         events = ((1, dx_start), (5, dx_middle), (22, dx_finish), (24, lambda: level_next(0)), (26, lambda: level_next(1)),
-                  (33, lambda: level_next(2)), (37, lambda: level_next(3)), (38, dh_relay))
+                  (31, lambda: level_next(2)), (36, lambda: level_next(3)), (38, dh_relay))
         for after, event in events:
-            pl.when(i == done + after)(event)
+            def noted(event=event, after=after):
+                with jax.named_scope(f'event{after}'):
+                    event()
+            pl.when(i == done + after)(noted)
         return carry
 
     lax.fori_loop(0, ticks, tick, 0)
-    level_next(4)
-    dh_finish()
-
-    for h in range(2):
-        p = place[h]
-        mine = out.at[pl.ds(y * half + h * (half // 2), half // 2)]
-        theirs = out.at[pl.ds((1 - y) * half + h * (half // 2), half // 2)]
-
-        @pl.when(p < Z - 1)
-        def _():
-            for c in (chunks - 2, chunks - 1):
-                reduce_copy(h, c, red.at[h, c % SLOTS]).wait_send()
-
-        @pl.when(p > 0)
-        def _():
-            pltpu.make_async_copy(mine, mine, bc_send.at[h]).wait()
-
-        pltpu.make_async_copy(mine, mine, mate_send.at[h]).wait()
-        pltpu.make_async_copy(theirs, theirs, mate_recv.at[h]).wait()
+    with jax.named_scope('finallevel'):
+        level_next(4)
+    with jax.named_scope('dhfinish'):
+        dh_finish()
+
+    @pl.when(jnp.logical_not(inner))
+    def _():
+        for c in range(chunks - 2, chunks):
+            up_copy(c).wait_send()
+        for c in range(chunks - RING, chunks):
+            mate_copy(c, out_rows(y, c)).wait_send()
+
+    for i in range(2):
+        theirs = out.at[pl.ds((1 - y) * half + i * (half // 2), half // 2)]
+        with jax.named_scope('matewait'):
+            pltpu.make_async_copy(theirs, theirs, mate_recv.at[i]).wait()
     for copy in stat_copies():
         copy.wait_send()
     for i in range(2):
@@ -664,11 +668,10 @@
     tokens = Y * own
     shard = table.shape[0]
     half = shard // Y
-    size = half // (2 * UNITS * PER_UNIT)
-    unit = 2 * size * PER_UNIT
-    chunks = UNITS * PER_UNIT
+    size = half // (UNITS * PER_UNIT)
+    unit = size * PER_UNIT
     quarter = own // n_tp
-    assert size * 2 * chunks == half and size % 8 == 0 and unit % 32 == 0 and quarter == TILE
+    assert unit * UNITS == half and size % 8 == 0 and unit % 32 == 0 and quarter == TILE
     assert shard % FORWARD_ROWS == 0
     f32 = jnp.float32
     b16 = jnp.bfloat16
@@ -697,7 +700,7 @@
             pltpu.VMEM((8, own), f32), pltpu.VMEM((8, own), f32),
             pltpu.VMEM((Y, n_tp, 2, own), f32), pltpu.VMEM((n_dp, 8, lanes), f32),
             pltpu.VMEM((2,) + labels.shape, i32),
-            pltpu.VMEM((2, SLOTS, size, width), f32), pltpu.VMEM((2, 2, size, width), f32),
+            pltpu.VMEM((SLOTS, size, width), f32), pltpu.VMEM((SLOTS, size, width), f32), pltpu.VMEM((2, size, width), f32),
             pltpu.VMEM((unit, tokens), b16),
             pltpu.VMEM((2, unit, width), b16), pltpu.VMEM((2, unit, width), b16),
             pltpu.VMEM((unit, width), f32),
@@ -707,9 +710,9 @@
             dma((n_tp,)), dma((2,)), dma((2, PIECES)), dma((2, PIECES)), dma((2, PIECES)), dma((2, PIECES)),
             dma((2 * n_tp - 1,)), dma((Y, n_tp)), dma((n_dp - 1,)), dma((n_dp,)),
             dma((2, 2)),
-            dma((2, SLOTS)), dma((2, SLOTS)), pltpu.SemaphoreType.REGULAR((2,)),
-            dma((2,)), dma((2, chunks)), dma((2,)), dma((2,)),
-            dma((2, 2)), dma((2,)), dma((2,)), dma((2, 2)), dma((2,)),
+            dma((RING,)), dma((SLOTS,)), dma((RING,)), dma((SLOTS,)), dma((RING,)), dma((SLOTS,)), dma((RING,)), dma((2,)),
+            pltpu.SemaphoreType.REGULAR((2,)),
+            dma((2,)), dma((RING,)), dma((1,)), dma((2,)), dma((2,)),
             dma((2, 2)), dma((2,)), dma((3,)), dma((3,)), dma((2, 5)),
         ],
         compiler_params=pltpu.CompilerParams(

time: 726 us -> 714 us (0.983)
  Pallas kernels: 725 us -> 713 us
    pallas_call x1, Pallas kernels: 686 us -> 674 us  [head_step(): pl.pallas_call(functools.partial(head_kernel, n_dp, n_tp), out_shape=(jax...]
where the time goes in v8:
time: 714 us; the launch traced here: 713 us
  Pallas kernels  713 us (100%)
    pallas_call x1, Pallas kernels, head_step(): pl.pallas_call(functools.partial(head_kernel, n_dp, n_tp), out_shape=(jax...  674 us
    pallas_call x1, Pallas kernels, place(): pl.pallas_call(place_kernel, out_shape=(jax.ShapeDtypeStruct(table.shape,...  38.1 us

profile of v8, /device:TPU:0, one launch (start us, length us, event | category | flops | bytes accessed | tf_op | source)
XLA Modules:
  0.0 713.3 jit_solution(14442811775484088044)
XLA Ops:
  0.6 674.4 %shard_map.101 = (f32[12672,1024]{1,0:T(8,128)}, f32[6336,1024]{1,0:T(8,128)}, bf16[2048,1024]{1,0:T(8,128)(2,1)}, f32[8,1024]{1,0:T(8,128)}) custom-call(bf16[12672,1024]{1,0:T(8,128)(2,1)} %table.1, bf16[2048,1024]{1,0:T(8,128)(2,1)} %bitcast.5, bf16[1024]{0:T(1024)(128)(2,1)} %gain.1, bf16[1024]{0:T(1024)(128)(2,1)} %bias.1, s32[8,256]{1,0:T(8,128)} %labels.1, ...), custom_call_target="tpu_custom_call" | custom-call | flops 239175991296 | bytes 77856768 | tf_op jit(solution)/shard_map/pallas_call | solution.py:684
  675.1 38.1 %shard_map.102 = (f32[12672,1024]{1,0:T(8,128)}, bf16[2048,1024]{1,0:T(8,128)(2,1)}, f32[1,1]{1,0:T(1,128)}, f32[1,1024]{1,0:T(1,128)}, f32[1,1024]{1,0:T(1,128)}) custom-call(f32[12672,1024]{1,0:T(8,128)} %get-tuple-element.13.table_in, bf16[2048,1024]{1,0:T(8,128)(2,1)} %get-tuple-element.14.dh_in, f32[8,1024]{1,0:T(8,128)} %get-tuple-element.15.sums), custom_call_target="tpu_custom_call" | custom-call | bytes 112197632 | tf_op jit(solution)/shard_map/pallas_call | solution.py:765

commit v9 on v8

--- a/solution.py
+++ b/solution.py
@@ -18,9 +18,9 @@
 END_LAG = 6
 TILE = 512
 PIECES = 4
-FORWARD_ROWS = 704
-PLACE_ROWS = 528
-PLACE_SLOTS = 16
+FORWARD_ROWS = 1056
+PLACE_ROWS = 1056
+PLACE_SLOTS = 12
 COLUMNS = 256
 VMEM_BYTES = 67043328
 MESH = pl.DeviceIdType.MESH
@@ -147,33 +147,29 @@
         inv_std = lax.rsqrt(variance + LN_EPS)
         x_hat = centred * inv_std
         normed = (x_hat * row_of(gain) + row_of(bias)).astype(jnp.bfloat16)
-        wide = normed.astype(jnp.float32)
         x[at, :] = normed
-        x_t[:, at] = wide.T.astype(jnp.bfloat16)
-        return x_hat, inv_std, wide
-
-    def first_piece(k, carry):
-        x_hat, inv_std, wide = normalize(block_of(tp, k))
-        at = aligned(k * piece, piece)
-        send_q[at, :] = wide
+        x_t[:, at] = normed.T
+        return x_hat, inv_std, normed
+
+    def first_piece(k):
+        x_hat, inv_std, normed = normalize(block_of(tp, k))
+        at = slice(k * piece, (k + 1) * piece)
+        send_q[at, :] = normed.astype(jnp.float32)
         hat[at, :] = x_hat
         inv[at, :] = jnp.broadcast_to(inv_std, (piece, inv.shape[1]))
-        return carry
-
-    def next_piece(j, carry):
-        k = j % PIECES
-
-        @pl.when(k == 0)
-        def _():
-            hidden_copy(1 + j // PIECES).wait()
-        normalize(block_of(lax.rem(tp + 1 + j // PIECES, n_tp), k))
+
+    def next_quarter(j, carry):
+        hidden_copy(j).wait()
+        for k in range(PIECES):
+            normalize(block_of(lax.rem(tp + j, n_tp), k))
         return carry
 
     def convert(q, k):
         wide = got[q, aligned(k * piece, piece)]
         at = aligned(own + q * quarter + k * piece, piece)
-        x[at, :] = wide.astype(jnp.bfloat16)
-        x_t[:, at] = wide.T.astype(jnp.bfloat16)
+        narrow = wide.astype(jnp.bfloat16)
+        x[at, :] = narrow
+        x_t[:, at] = narrow.T
 
     def fold(logits, at):
         logits = logits.reshape(block_rows // 8, 8, TILE)
@@ -189,35 +185,37 @@
         def _():
             block_copy(b + 1).start()
 
-        def every_third(first, count):
-            d = b - first
-            return (d >= 0) & (d < 3 * count) & (jnp.maximum(d, 0) % 3 == 0), jnp.maximum(d, 0) // 3
-
-        due, k_y = every_third(4, PIECES)
+        def spaced(first, count):
+            d = jnp.maximum(b - first, 0)
+            return (b >= first) & ((d < 2) | (d == 3) | (d == 5)) & (d < 2 * count - 1), jnp.minimum((d + 1) // 2, last)
+
+        due, k_y = spaced(3, PIECES)
 
         @pl.when(due)
         def _():
-            y_copy(k_y).wait_recv()
+            with jax.named_scope('wait_y'):
+                y_copy(k_y).wait_recv()
             beside_copy(k_y).start()
             core_copy(k_y).start()
             convert(tp, k_y)
 
-        due, k_core = every_third(5, PIECES)
+        due, k_core = spaced(4, PIECES)
 
         @pl.when(due)
         def _():
             core_copy(k_core).wait_recv()
             convert(partner, k_core)
 
-        due, k_x = every_third(8, PIECES)
+        due, k_x = spaced(6, PIECES)
 
         @pl.when(due)
         def _():
-            beside_copy(k_x).wait_recv()
+            with jax.named_scope('wait_x'):
+                beside_copy(k_x).wait_recv()
             relay_copy(k_x).start()
             convert(beside, k_x)
 
-        due, k_relay = every_third(9, PIECES - 1)
+        due, k_relay = spaced(7, PIECES - 1)
 
         @pl.when(due)
         def _():
@@ -281,8 +279,10 @@
 
     unit_iota = lax.broadcasted_iota(jnp.int32, (unit, 1), 0)
 
-    def grads(table_rows, row_ids, at):
-        logits = jnp.dot(table_rows, x_t[:, at], preferred_element_type=jnp.float32)
+    def logits_of(table_rows, at):
+        return jnp.dot(table_rows, x_t[:, at], preferred_element_type=jnp.float32)
+
+    def grads(logits, row_ids, at):
         hit = row_ids == label[:, at]
         probs = jnp.where(row_ids + first_row < VOCAB, jnp.exp(logits - lse[:, at]), 0.0)
         q = ((probs - jnp.where(hit, 1.0, 0.0)) * scale[:, at]).astype(jnp.bfloat16)
@@ -292,11 +292,13 @@
         dx_t[t] = dx_t[t] + lax.dot_general(
             table_rows, q, (((0,), (0,)), ((), ())), preferred_element_type=jnp.float32)
 
-    def main_tile(u, t):
+    def main_tile(u, t, logits=None):
         slot = u % 2
         at = tile_at(t)
         row_ids = y * half + u * unit + unit_iota
-        q, hits = grads(rows_buf[slot], row_ids, at)
+        if logits is None:
+            logits = logits_of(rows_buf[slot], at)
+        q, hits = grads(logits, row_ids, at)
         q_t[:, at] = q
         target[:, at] = target[:, at] + jnp.sum(hits, axis=0, keepdims=True)
         if t < own // TILE:
@@ -308,7 +310,7 @@
 
     def more_tile(u, t):
         theirs = (1 - y) * half + u * unit + unit_iota
-        q, _ = grads(more_buf[u % 2], theirs, tile_at(t))
+        q, _ = grads(logits_of(more_buf[u % 2], tile_at(t)), theirs, tile_at(t))
         add_dx(more_buf[u % 2], q, t)
 
     few = (all_tiles - own_tiles) // 4
@@ -333,6 +335,22 @@
         for n in range(columns):
             table_tile(n)
         part_copy(u).start()
+
+    def early(t):
+        return got.at[t // 2, pl.ds(0, unit), pl.ds(t % 2 * TILE, TILE)]
+
+    def first_logits():
+        rows_copy(0).wait()
+        rows_copy(1).start()
+        for t in range(all_tiles):
+            early(t)[...] = logits_of(rows_buf[0], tile_at(t))
+
+    def first_unit():
+        for t in range(all_tiles):
+            main_tile(0, t, early(t)[...])
+        for n in range(columns):
+            table_tile(n)
+        part_copy(0).start()
 
     def compute_3(u):
         more_copy(u).wait()
@@ -527,9 +545,10 @@
     rows_copy(0).start()
     more_copy(0).start()
     hidden_copy(0).wait()
-    lax.fori_loop(0, PIECES, first_piece, 0)
+    for k in range(PIECES):
+        first_piece(k)
     with jax.named_scope('lnrest'):
-        lax.fori_loop(0, (n_tp - 1) * PIECES, next_piece, 0)
+        lax.fori_loop(1, n_tp, next_quarter, 0)
     counts[dp] = jnp.full(counts.shape[1:], jnp.sum(loss_mask[...].astype(jnp.float32)), jnp.float32)
     pl.semaphore_wait(barrier, n_dp - 1 + 2 * len(others))
     for k in range(PIECES):
@@ -549,7 +568,7 @@
         return carry
 
     lax.fori_loop(0, own // TILE, clear, 0)
-    assert blocks >= 6 + 3 * PIECES
+    assert blocks > 11 and PIECES == 4
     with jax.named_scope('blocks'):
         lax.fori_loop(0, blocks, block, 0)
     fold(held[...], tile_at(own_tiles - 1))
@@ -578,6 +597,8 @@
             copy.wait_send()
     for j in range(n_dp - 1):
         count_copy(j).wait_send()
+    with jax.named_scope('early'):
+        first_logits()
     with jax.named_scope('statwait'):
         for other in others:
             stat_arrival(0, other).wait_recv()
@@ -589,6 +610,9 @@
         mass = sum(stats[side, j, 1:2] * jnp.exp(tops[j] - best) for j in range(n_tp))
         lse[:, side * own:(side + 1) * own] = best + jnp.log(mass)
 
+    with jax.named_scope('first'):
+        first_unit()
+
     computes = (compute_0, compute_1, compute_2, compute_3, compute_4)
     beats = len(computes)
     start = beats - 2
@@ -604,12 +628,12 @@
         def _():
             settle(0)
 
-        @pl.when((i >= start) & jnp.logical_not(inner))
+        @pl.when(jnp.logical_not(inner))
         def _():
             with jax.named_scope('red'):
                 end_step(jnp.maximum(i - start, 0))
 
-        @pl.when((i >= start) & inner)
+        @pl.when(inner)
         def _():
             with jax.named_scope('red'):
                 inner_step(jnp.maximum(i - start, 0))
@@ -627,17 +651,12 @@
         events = ((1, dx_start), (5, dx_middle), (22, dx_finish), (24, lambda: level_next(0)), (26, lambda: level_next(1)),
                   (31, lambda: level_next(2)), (36, lambda: level_next(3)), (38, dh_relay))
         for after, event in events:
-            def noted(event=event, after=after):
-                with jax.named_scope(f'event{after}'):
-                    event()
-            pl.when(i == done + after)(noted)
+            pl.when(i == done + after)(event)
         return carry
 
-    lax.fori_loop(0, ticks, tick, 0)
-    with jax.named_scope('finallevel'):
-        level_next(4)
-    with jax.named_scope('dhfinish'):
-        dh_finish()
+    lax.fori_loop(start, ticks, tick, 0)
+    level_next(4)
+    dh_finish()
 
     @pl.when(jnp.logical_not(inner))
     def _():
@@ -671,7 +690,7 @@
     size = half // (UNITS * PER_UNIT)
     unit = size * PER_UNIT
     quarter = own // n_tp
-    assert unit * UNITS == half and size % 8 == 0 and unit % 32 == 0 and quarter == TILE
+    assert unit <= quarter and 2 * TILE <= width and unit * UNITS == half and size % 8 == 0 and unit % 32 == 0 and quarter == TILE
     assert shard % FORWARD_ROWS == 0
     f32 = jnp.float32
     b16 = jnp.bfloat16

time: 714 us -> 708 us (level)
  no operation moved by 1% of the time
where the time goes in v9:
time: 708 us; the launch traced here: 707 us
  Pallas kernels  707 us (100%)
    pallas_call x1, Pallas kernels, head_step(): pl.pallas_call(functools.partial(head_kernel, n_dp, n_tp), out_shape=(jax...  671 us
    pallas_call x1, Pallas kernels, place(): pl.pallas_call(place_kernel, out_shape=(jax.ShapeDtypeStruct(table.shape,...  36 us

profile of v9, /device:TPU:0, one launch (start us, length us, event | category | flops | bytes accessed | tf_op | source)
XLA Modules:
  0.0 707.4 jit_solution(16247001029265765718)
XLA Ops:
  0.6 670.6 %shard_map.101 = (f32[12672,1024]{1,0:T(8,128)}, f32[6336,1024]{1,0:T(8,128)}, bf16[2048,1024]{1,0:T(8,128)(2,1)}, f32[8,1024]{1,0:T(8,128)}) custom-call(bf16[12672,1024]{1,0:T(8,128)(2,1)} %table.1, bf16[2048,1024]{1,0:T(8,128)(2,1)} %bitcast.5, bf16[1024]{0:T(1024)(128)(2,1)} %gain.1, bf16[1024]{0:T(1024)(128)(2,1)} %bias.1, s32[8,256]{1,0:T(8,128)} %labels.1, ...), custom_call_target="tpu_custom_call" | custom-call | flops 239175991296 | bytes 77856768 | tf_op jit(solution)/shard_map/pallas_call | solution.py:703
  671.3 36.0 %shard_map.102 = (f32[12672,1024]{1,0:T(8,128)}, bf16[2048,1024]{1,0:T(8,128)(2,1)}, f32[1,1]{1,0:T(1,128)}, f32[1,1024]{1,0:T(1,128)}, f32[1,1024]{1,0:T(1,128)}) custom-call(f32[12672,1024]{1,0:T(8,128)} %get-tuple-element.13.table_in, bf16[2048,1024]{1,0:T(8,128)(2,1)} %get-tuple-element.14.dh_in, f32[8,1024]{1,0:T(8,128)} %get-tuple-element.15.sums), custom_call_target="tpu_custom_call" | custom-call | bytes 112197632 | tf_op jit(solution)/shard_map/pallas_call | solution.py:784

commit v10 on v9

--- a/solution.py
+++ b/solution.py
@@ -13,7 +13,7 @@
 Y = 2
 UNITS = 33
 PER_UNIT = 6
-SLOTS = 16
+SLOTS = 8
 RING = 4
 END_LAG = 6
 TILE = 512
@@ -193,8 +193,7 @@
 
         @pl.when(due)
         def _():
-            with jax.named_scope('wait_y'):
-                y_copy(k_y).wait_recv()
+            y_copy(k_y).wait_recv()
             beside_copy(k_y).start()
             core_copy(k_y).start()
             convert(tp, k_y)
@@ -210,8 +209,7 @@
 
         @pl.when(due)
         def _():
-            with jax.named_scope('wait_x'):
-                beside_copy(k_x).wait_recv()
+            beside_copy(k_x).wait_recv()
             relay_copy(k_x).start()
             convert(beside, k_x)
 
@@ -288,20 +286,25 @@
         q = ((probs - jnp.where(hit, 1.0, 0.0)) * scale[:, at]).astype(jnp.bfloat16)
         return q, jnp.where(hit, logits, 0.0)
 
+    def dx_of(table_rows, q):
+        return lax.dot_general(table_rows, q, (((0,), (0,)), ((), ())), preferred_element_type=jnp.float32)
+
     def add_dx(table_rows, q, t):
-        dx_t[t] = dx_t[t] + lax.dot_general(
-            table_rows, q, (((0,), (0,)), ((), ())), preferred_element_type=jnp.float32)
+        dx_t[t] = dx_t[t] + dx_of(table_rows, q)
 
     def main_tile(u, t, logits=None):
         slot = u % 2
         at = tile_at(t)
         row_ids = y * half + u * unit + unit_iota
-        if logits is None:
+        is_first = logits is not None
+        if not is_first:
             logits = logits_of(rows_buf[slot], at)
         q, hits = grads(logits, row_ids, at)
         q_t[:, at] = q
         target[:, at] = target[:, at] + jnp.sum(hits, axis=0, keepdims=True)
-        if t < own // TILE:
+        if t < own_tiles and is_first:
+            dx_t[t] = dx_of(rows_buf[slot], q)
+        elif t < own_tiles:
             add_dx(rows_buf[slot], q, t)
 
     def table_tile(n):
@@ -456,18 +459,22 @@
         at = aligned(q * quarter, quarter)
         x[at, :] = ref.astype(jnp.bfloat16)
 
+    def dh_own():
+        round_dh(tp, send_q[...])
+
+    def dh_partner():
+        share_copy(0).wait_recv()
+        round_dh(partner, got[partner])
+
     def dh_relay():
         share_copy(1).wait_recv()
         pass_copy().start()
-        round_dh(beside, got[beside])
-        share_copy(0).wait_recv()
-        round_dh(partner, got[partner])
-        round_dh(tp, send_q[...])
 
     def dh_copy():
         return pltpu.make_async_copy(x.at[pl.ds(0, own)], dh, hidden_sem.at[0])
 
     def dh_finish():
+        round_dh(beside, got[beside])
         pass_copy().wait_recv()
         round_dh(across, got[across])
         dh_copy().start()
@@ -547,8 +554,7 @@
     hidden_copy(0).wait()
     for k in range(PIECES):
         first_piece(k)
-    with jax.named_scope('lnrest'):
-        lax.fori_loop(1, n_tp, next_quarter, 0)
+    lax.fori_loop(1, n_tp, next_quarter, 0)
     counts[dp] = jnp.full(counts.shape[1:], jnp.sum(loss_mask[...].astype(jnp.float32)), jnp.float32)
     pl.semaphore_wait(barrier, n_dp - 1 + 2 * len(others))
     for k in range(PIECES):
@@ -563,14 +569,8 @@
     held[...] = jnp.full_like(held, -jnp.inf)
     target[...] = jnp.zeros_like(target)
 
-    def clear(t, carry):
-        dx_t[t] = jnp.zeros(dx_t.shape[1:], jnp.float32)
-        return carry
-
-    lax.fori_loop(0, own // TILE, clear, 0)
     assert blocks > 11 and PIECES == 4
-    with jax.named_scope('blocks'):
-        lax.fori_loop(0, blocks, block, 0)
+    lax.fori_loop(0, blocks, block, 0)
     fold(held[...], tile_at(own_tiles - 1))
 
     best = jnp.max(top[...], axis=0, keepdims=True)
@@ -579,8 +579,7 @@
     for copy in stat_copies():
         copy.start()
 
-    with jax.named_scope('lastrelay'):
-        relay_copy(last).wait_recv()
+    relay_copy(last).wait_recv()
     convert(across, last)
     for i in range(2):
         ids_copy(i).wait()
@@ -597,28 +596,25 @@
             copy.wait_send()
     for j in range(n_dp - 1):
         count_copy(j).wait_send()
-    with jax.named_scope('early'):
-        first_logits()
-    with jax.named_scope('statwait'):
-        for other in others:
-            stat_arrival(0, other).wait_recv()
-        for other in (tp,) + others:
-            stat_arrival(1, other).wait_recv()
+    first_logits()
+    for other in others:
+        stat_arrival(0, other).wait_recv()
+    for other in (tp,) + others:
+        stat_arrival(1, other).wait_recv()
     for side in range(Y):
         tops = [stats[side, j, 0:1] for j in range(n_tp)]
         best = functools.reduce(jnp.maximum, tops)
         mass = sum(stats[side, j, 1:2] * jnp.exp(tops[j] - best) for j in range(n_tp))
         lse[:, side * own:(side + 1) * own] = best + jnp.log(mass)
 
-    with jax.named_scope('first'):
-        first_unit()
+    first_unit()
 
     computes = (compute_0, compute_1, compute_2, compute_3, compute_4)
     beats = len(computes)
     start = beats - 2
     done = beats * units - 1
     ticks = start + chunks + END_LAG
-    assert done + 38 < ticks
+    assert done + 39 < ticks
 
     def tick(i, carry):
         u = i // beats
@@ -630,26 +626,21 @@
 
         @pl.when(jnp.logical_not(inner))
         def _():
-            with jax.named_scope('red'):
-                end_step(jnp.maximum(i - start, 0))
+            end_step(jnp.maximum(i - start, 0))
 
         @pl.when(inner)
         def _():
-            with jax.named_scope('red'):
-                inner_step(jnp.maximum(i - start, 0))
+            inner_step(jnp.maximum(i - start, 0))
 
         @pl.when((i > start) & (kind == start) & (u < units))
         def _():
             settle(u)
 
         for j, compute in enumerate(computes):
-            def scoped(compute=compute, j=j):
-                with jax.named_scope(f'calc{j}'):
-                    compute(u)
-            pl.when((kind == j) & (u < units))(scoped)
+            pl.when((kind == j) & (u < units))(functools.partial(compute, u))
 
         events = ((1, dx_start), (5, dx_middle), (22, dx_finish), (24, lambda: level_next(0)), (26, lambda: level_next(1)),
-                  (31, lambda: level_next(2)), (36, lambda: level_next(3)), (38, dh_relay))
+                  (28, dh_own), (30, dh_partner), (32, lambda: level_next(2)), (36, lambda: level_next(3)), (39, dh_relay))
         for after, event in events:
             pl.when(i == done + after)(event)
         return carry
@@ -667,8 +658,7 @@
 
     for i in range(2):
         theirs = out.at[pl.ds((1 - y) * half + i * (half // 2), half // 2)]
-        with jax.named_scope('matewait'):
-            pltpu.make_async_copy(theirs, theirs, mate_recv.at[i]).wait()
+        pltpu.make_async_copy(theirs, theirs, mate_recv.at[i]).wait()
     for copy in stat_copies():
         copy.wait_send()
     for i in range(2):

time: 708 us -> 707 us (level)
  no operation moved by 1% of the time
where the time goes in v10:
time: 707 us
  Pallas kernels  706 us (100%)
    pallas_call x1, Pallas kernels, head_step(): pl.pallas_call(functools.partial(head_kernel, n_dp, n_tp), out_shape=(jax...  670 us
    pallas_call x1, Pallas kernels, place(): pl.pallas_call(place_kernel, out_shape=(jax.ShapeDtypeStruct(table.shape,...  36 us

profile of v10, /device:TPU:0, one launch (start us, length us, event | category | flops | bytes accessed | tf_op | source)
XLA Modules:
  0.0 707.2 jit_solution(15784520984348913786)
XLA Ops:
  0.6 670.4 %shard_map.101 = (f32[12672,1024]{1,0:T(8,128)}, f32[6336,1024]{1,0:T(8,128)}, bf16[2048,1024]{1,0:T(8,128)(2,1)}, f32[8,1024]{1,0:T(8,128)}) custom-call(bf16[12672,1024]{1,0:T(8,128)(2,1)} %table.1, bf16[2048,1024]{1,0:T(8,128)(2,1)} %bitcast.5, bf16[1024]{0:T(1024)(128)(2,1)} %gain.1, bf16[1024]{0:T(1024)(128)(2,1)} %bias.1, s32[8,256]{1,0:T(8,128)} %labels.1, ...), custom_call_target="tpu_custom_call" | custom-call | flops 239175991296 | bytes 77856768 | tf_op jit(solution)/shard_map/pallas_call | solution.py:693
  671.0 36.0 %shard_map.102 = (f32[12672,1024]{1,0:T(8,128)}, bf16[2048,1024]{1,0:T(8,128)(2,1)}, f32[1,1]{1,0:T(1,128)}, f32[1,1024]{1,0:T(1,128)}, f32[1,1024]{1,0:T(1,128)}) custom-call(f32[12672,1024]{1,0:T(8,128)} %get-tuple-element.13.table_in, bf16[2048,1024]{1,0:T(8,128)(2,1)} %get-tuple-element.14.dh_in, f32[8,1024]{1,0:T(8,128)} %get-tuple-element.15.sums), custom_call_target="tpu_custom_call" | custom-call | bytes 112197632 | tf_op jit(solution)/shard_map/pallas_call | solution.py:774

commit v11 on v10

--- a/solution.py
+++ b/solution.py
@@ -253,6 +253,9 @@
     def up_copy(c):
         return remote(part_rows(c), red.at[c % SLOTS], up_send.at[c % RING], up_recv.at[c % SLOTS], dp=z_mate)
 
+    def first_up_copy():
+        return remote(stage.at[pl.ds(0, size)], red.at[0], up_send.at[0], up_recv.at[0], dp=z_mate)
+
     def meet_copy(c):
         return remote(red.at[c % SLOTS], met.at[c % SLOTS], meet_send.at[c % RING], meet_recv.at[c % SLOTS], dp=z_cross)
 
@@ -302,9 +305,7 @@
         q, hits = grads(logits, row_ids, at)
         q_t[:, at] = q
         target[:, at] = target[:, at] + jnp.sum(hits, axis=0, keepdims=True)
-        if t < own_tiles and is_first:
-            dx_t[t] = dx_of(rows_buf[slot], q)
-        elif t < own_tiles:
+        if t < own_tiles and not is_first:
             add_dx(rows_buf[slot], q, t)
 
     def table_tile(n):
@@ -355,6 +356,10 @@
             table_tile(n)
         part_copy(0).start()
 
+    def first_dx():
+        for t in range(own_tiles):
+            dx_t[t] = dx_of(rows_buf[0], q_t[:, tile_at(t)])
+
     def compute_3(u):
         more_copy(u).wait()
 
@@ -392,7 +397,14 @@
             def _():
                 up_copy(t - 2).wait_send()
             take_credit(0, t)
-            up_copy(t).start()
+
+            @pl.when(t == 0)
+            def _():
+                first_up_copy().start()
+
+            @pl.when(t > 0)
+            def _():
+                up_copy(t).start()
 
         c = t - END_LAG
 
@@ -620,17 +632,21 @@
         u = i // beats
         kind = i % beats
 
+        @pl.when(i == start + 1)
+        def _():
+            settle(0)
+
+        @pl.when(jnp.logical_not(inner))
+        def _():
+            end_step(jnp.maximum(i - start, 0))
+
+        @pl.when(inner)
+        def _():
+            inner_step(jnp.maximum(i - start, 0))
+
         @pl.when(i == start)
         def _():
-            settle(0)
-
-        @pl.when(jnp.logical_not(inner))
-        def _():
-            end_step(jnp.maximum(i - start, 0))
-
-        @pl.when(inner)
-        def _():
-            inner_step(jnp.maximum(i - start, 0))
+            first_dx()
 
         @pl.when((i > start) & (kind == start) & (u < units))
         def _():

time: 707 us -> 706 us (level)
  no operation moved by 1% of the time
where the time goes in v11:
time: 706 us
  Pallas kernels  705 us (100%)
    pallas_call x1, Pallas kernels, head_step(): pl.pallas_call(functools.partial(head_kernel, n_dp, n_tp), out_shape=(jax...  669 us
    pallas_call x1, Pallas kernels, place(): pl.pallas_call(place_kernel, out_shape=(jax.ShapeDtypeStruct(table.shape,...  36 us

profile of v11, /device:TPU:0, one launch (start us, length us, event | category | flops | bytes accessed | tf_op | source)
XLA Modules:
  0.0 705.8 jit_solution(13148760957422749792)
XLA Ops:
  0.6 669.0 %shard_map.101 = (f32[12672,1024]{1,0:T(8,128)}, f32[6336,1024]{1,0:T(8,128)}, bf16[2048,1024]{1,0:T(8,128)(2,1)}, f32[8,1024]{1,0:T(8,128)}) custom-call(bf16[12672,1024]{1,0:T(8,128)(2,1)} %table.1, bf16[2048,1024]{1,0:T(8,128)(2,1)} %bitcast.5, bf16[1024]{0:T(1024)(128)(2,1)} %gain.1, bf16[1024]{0:T(1024)(128)(2,1)} %bias.1, s32[8,256]{1,0:T(8,128)} %labels.1, ...), custom_call_target="tpu_custom_call" | custom-call | flops 239175991296 | bytes 77856768 | tf_op jit(solution)/shard_map/pallas_call | solution.py:709
  669.6 36.0 %shard_map.102 = (f32[12672,1024]{1,0:T(8,128)}, bf16[2048,1024]{1,0:T(8,128)(2,1)}, f32[1,1]{1,0:T(1,128)}, f32[1,1024]{1,0:T(1,128)}, f32[1,1024]{1,0:T(1,128)}) custom-call(f32[12672,1024]{1,0:T(8,128)} %get-tuple-element.13.table_in, bf16[2048,1024]{1,0:T(8,128)(2,1)} %get-tuple-element.14.dh_in, f32[8,1024]{1,0:T(8,128)} %get-tuple-element.15.sums), custom_call_target="tpu_custom_call" | custom-call | bytes 112197632 | tf_op jit(solution)/shard_map/pallas_call | solution.py:790

commit v12 on v11

--- a/solution.py
+++ b/solution.py
@@ -51,12 +51,13 @@
 
 
 def head_kernel(
-        n_dp, n_tp, table, hidden, gain, bias, labels, loss_mask,
-        out, part, dh, sums,
+        n_dp, n_tp, table, hidden, gain_in, bias_in, labels_in, mask_in,
+        out, part, dh, sums_out,
+        gain, bias, labels, loss_mask, sums,
         x, x_t, lse, scale, weight, label, target, hat, inv, send_q,
         got, block_buf, held, top, total, stats, counts, ids,
         red, met, loc, q_t, rows_buf, more_buf, stage, dx_t, from_core, from_x, levels, arrived,
-        hidden_sem, block_sem, y_sem, beside_sem, core_sem, relay_sem, stat_send, stat_recv, count_send, count_recv,
+        small_sem, piece_sem, hidden_sem, block_sem, y_sem, beside_sem, core_sem, relay_sem, stat_send, stat_recv, count_send, count_recv,
         ids_sem,
         up_send, up_recv, meet_send, meet_recv, down_send, down_recv, mate_send, mate_recv, credit,
         loc_sem, own_sem, part_sem, rows_sem, more_sem,
@@ -99,6 +100,13 @@
         signal(barrier, tp=other)
         signal(barrier, dp=mate, tp=other)
 
+    small_copies = [pltpu.make_async_copy(src, dst, small_sem.at[i]) for i, (src, dst) in enumerate((
+        (gain_in, gain), (bias_in, bias), (labels_in, labels), (mask_in, loss_mask), (sums, sums_out)))]
+
+    def piece_copy(k):
+        at = block_of(tp, k)
+        return pltpu.make_async_copy(hidden.at[at], x.at[at], piece_sem.at[k])
+
     def hidden_copy(j):
         q = lax.rem(tp + j, n_tp)
         at = aligned(q * quarter, quarter)
@@ -558,13 +566,19 @@
     def tokens_counted():
         return sum(counts[j, 0:1, 0:1] for j in range(n_dp))
 
-    for j in range(n_tp):
+    for k in range(PIECES):
+        piece_copy(k).start()
+    for copy in small_copies[:4]:
+        copy.start()
+    for j in range(1, n_tp):
         hidden_copy(j).start()
     block_copy(0).start()
     rows_copy(0).start()
     more_copy(0).start()
-    hidden_copy(0).wait()
+    for copy in small_copies[:4]:
+        copy.wait()
     for k in range(PIECES):
+        piece_copy(k).wait()
         first_piece(k)
     lax.fori_loop(1, n_tp, next_quarter, 0)
     counts[dp] = jnp.full(counts.shape[1:], jnp.sum(loss_mask[...].astype(jnp.float32)), jnp.float32)
@@ -664,6 +678,7 @@
     lax.fori_loop(start, ticks, tick, 0)
     level_next(4)
     dh_finish()
+    small_copies[4].start()
 
     @pl.when(jnp.logical_not(inner))
     def _():
@@ -684,6 +699,7 @@
         share_copy(i).wait_send()
     pass_copy().wait_send()
     dh_copy().wait()
+    small_copies[4].wait()
     for i in range(len(level_peers)):
         level_copy(i).wait_send()
 
@@ -703,7 +719,6 @@
     i32 = jnp.int32
     lanes = 128
     dma = pltpu.SemaphoreType.DMA
-    vmem = pl.BlockSpec(memory_space=pltpu.VMEM)
     hbm = pl.BlockSpec(memory_space=pl.ANY)
     flops = 2 * width * (own * shard + half * (2 * tokens + 3 * own))
     return pl.pallas_call(
@@ -713,9 +728,11 @@
             jax.ShapeDtypeStruct((half, width), f32),
             jax.ShapeDtypeStruct((own, width), b16),
             jax.ShapeDtypeStruct((8, width), f32)),
-        in_specs=[hbm, hbm, vmem, vmem, vmem, vmem],
-        out_specs=(hbm, hbm, hbm, vmem),
+        in_specs=[hbm] * 6,
+        out_specs=(hbm,) * 4,
         scratch_shapes=[
+            pltpu.VMEM((width,), b16), pltpu.VMEM((width,), b16), pltpu.VMEM(labels.shape, i32), pltpu.VMEM(labels.shape, i32),
+            pltpu.VMEM((8, width), f32),
             pltpu.VMEM((tokens, width), b16), pltpu.VMEM((width, tokens), b16),
             pltpu.VMEM((1, tokens), f32), pltpu.VMEM((1, tokens), f32), pltpu.VMEM((1, tokens), f32),
             pltpu.VMEM((1, tokens), i32), pltpu.VMEM((1, tokens), f32),
@@ -732,7 +749,7 @@
             pltpu.VMEM((n_tp, width, quarter), f32),
             pltpu.VMEM((2, width, quarter), f32), pltpu.VMEM((width, quarter), f32),
             pltpu.VMEM((5, 8, width), f32), pltpu.VMEM((5, 8, width), f32),
-            dma((n_tp,)), dma((2,)), dma((2, PIECES)), dma((2, PIECES)), dma((2, PIECES)), dma((2, PIECES)),
+            dma((5,)), dma((PIECES,)), dma((n_tp,)), dma((2,)), dma((2, PIECES)), dma((2, PIECES)), dma((2, PIECES)), dma((2, PIECES)),
             dma((2 * n_tp - 1,)), dma((Y, n_tp)), dma((n_dp - 1,)), dma((n_dp,)),
             dma((2, 2)),
             dma((RING,)), dma((SLOTS,)), dma((RING,)), dma((SLOTS,)), dma((RING,)), dma((SLOTS,)), dma((RING,)), dma((2,)),

time: 706 us -> 706 us (level)
  no operation moved by 1% of the time
where the time goes in v12:
time: 706 us; the launch traced here: 705 us
  Pallas kernels  705 us (100%)
    pallas_call x1, Pallas kernels, head_step(): pl.pallas_call(functools.partial(head_kernel, n_dp, n_tp), out_shape=(jax...  669 us
    pallas_call x1, Pallas kernels, place(): pl.pallas_call(place_kernel, out_shape=(jax.ShapeDtypeStruct(table.shape,...  36 us

profile of v12, /device:TPU:0, one launch (start us, length us, event | category | flops | bytes accessed | tf_op | source)
XLA Modules:
  0.0 705.5 jit_solution(1280202019696656243)
XLA Ops:
  0.6 668.6 %shard_map.101 = (f32[12672,1024]{1,0:T(8,128)}, f32[6336,1024]{1,0:T(8,128)}, bf16[2048,1024]{1,0:T(8,128)(2,1)}, f32[8,1024]{1,0:T(8,128)}) custom-call(bf16[12672,1024]{1,0:T(8,128)(2,1)} %table.1, bf16[2048,1024]{1,0:T(8,128)(2,1)} %bitcast.5, bf16[1024]{0:T(1024)(128)(2,1)} %gain_in.1, bf16[1024]{0:T(1024)(128)(2,1)} %bias_in.1, s32[8,256]{1,0:T(8,128)} %labels_in.1, ...), custom_call_target="tpu_custom_call" | custom-call | flops 239175991296 | bytes 77856768 | tf_op jit(solution)/shard_map/pallas_call | solution.py:724
  669.3 36.0 %shard_map.102 = (f32[12672,1024]{1,0:T(8,128)}, bf16[2048,1024]{1,0:T(8,128)(2,1)}, f32[1,1]{1,0:T(1,128)}, f32[1,1024]{1,0:T(1,128)}, f32[1,1024]{1,0:T(1,128)}) custom-call(f32[12672,1024]{1,0:T(8,128)} %get-tuple-element.13.table_in, bf16[2048,1024]{1,0:T(8,128)(2,1)} %get-tuple-element.14.dh_in, f32[8,1024]{1,0:T(8,128)} %get-tuple-element.15.sums), custom_call_target="tpu_custom_call" | custom-call | bytes 112197632 | tf_op jit(solution)/shard_map/pallas_call | solution.py:807
